TPU v7x, 32 devices: a whole 2x2x4 slice. The times are simulated.
32 devices in a mesh: seq: 8 (over z, x), batch: 4 (over y, core).
Axes of the slice: x: 2, y: 2, z: 4, core: 2. Of those that a mesh axis runs over, the one named last changes fastest.
Arguments:
- inputs: bfloat16 [4, 2048, 1024], P('batch', 'seq'), may hold values from -6 to 6
- cotangent: float32 [4, 2048, 1024], P('batch', 'seq'), may hold values from -6 to 6
- mixer_gain: bfloat16 [1024], P(('seq', 'batch')), may hold values from 0.5 to 1.5
- feed_gain: bfloat16 [1024], P(('seq', 'batch')), may hold values from 0.5 to 1.5
- w_query: bfloat16 [1024, 512], P(('seq', 'batch')), may hold values from -0.1875 to 0.1875
- w_key: bfloat16 [1024, 512], P(('seq', 'batch')), may hold values from -0.1875 to 0.1875
- w_value: bfloat16 [1024, 1024], P(('seq', 'batch')), may hold values from -0.1875 to 0.1875
- w_outgate: bfloat16 [1024, 1024], P(('seq', 'batch')), may hold values from -0.1875 to 0.1875
- w_decay_down: bfloat16 [1024, 16], P(('seq', 'batch')), may hold values from -0.1875 to 0.1875
- w_decay_up: bfloat16 [16, 512], P(None, ('seq', 'batch')), may hold values from -1.5 to 1.5
- decay_bias: bfloat16 [512], P(('seq', 'batch')), may hold values from -1 to 9
- head_gain: bfloat16 [256], P(('seq', 'batch')), may hold values from 0.5 to 1.5
- w_output: bfloat16 [1024, 1024], P(('seq', 'batch')), may hold values from -0.1875 to 0.1875
- w_gate: bfloat16 [1024, 2816], P(('seq', 'batch')), may hold values from -0.1875 to 0.1875
- w_up: bfloat16 [1024, 2816], P(('seq', 'batch')), may hold values from -0.1875 to 0.1875
- w_down: bfloat16 [2816, 1024], P(('seq', 'batch')), may hold values from -0.109375 to 0.109375
Outputs:
- block_output: float32 [4, 2048, 1024], P('batch', 'seq')
- input_grad: float32 [4, 2048, 1024], P('batch', 'seq')
- grad_mixer_gain: float32 [1024], P(('seq', 'batch'))
- grad_feed_gain: float32 [1024], P(('seq', 'batch'))
- grad_query: float32 [1024, 512], P(('seq', 'batch'))
- grad_key: float32 [1024, 512], P(('seq', 'batch'))
- grad_value: float32 [1024, 1024], P(('seq', 'batch'))
- grad_outgate: float32 [1024, 1024], P(('seq', 'batch'))
- grad_decay_down: float32 [1024, 16], P(('seq', 'batch'))
- grad_decay_up: float32 [16, 512], P(None, ('seq', 'batch'))
- grad_decay_bias: float32 [512], P(('seq', 'batch'))
- grad_head_gain: float32 [256], P(('seq', 'batch'))
- grad_output: float32 [1024, 1024], P(('seq', 'batch'))
- grad_gate: float32 [1024, 2816], P(('seq', 'batch'))
- grad_up: float32 [1024, 2816], P(('seq', 'batch'))
- grad_down: float32 [2816, 1024], P(('seq', 'batch'))
All inputs are finite; a program needn't handle non-finite values.
Results may differ from a plain program's by a relative error of at most 0.035.
Values may be sent and summed in bfloat16 or wider, within the bound.
A program may use at most 192 MiB of HBM per device.

v0:
```python
import jax
import jax.numpy as jnp
from jax import lax
from jax.sharding import PartitionSpec as P

HEADS = 4
KEY_DIM = 128
VALUE_DIM = 256
GROUP = 64


epsilon = 1e-06
highest = lax.Precision.HIGHEST


def entering(value, axis, combine, identity, reverse):
    length, mine = (lax.axis_size(axis), lax.axis_index(axis))
    everything = jax.tree.map(lambda part: lax.all_gather(part, axis), value)
    start = jax.tree.map(
        lambda part, zero: jnp.broadcast_to(jnp.asarray(zero, part.dtype), part.shape),
        value,
        identity,
    )

    def turn(k, before):
        at = length - 1 - k if reverse else k
        reached = at > mine if reverse else at < mine
        new = combine(before, jax.tree.map(lambda part: part[at], everything))
        return jax.tree.map(lambda a, b: jnp.where(reached, a, b), new, before)

    return lax.fori_loop(0, length, turn, start)


def causal_mask():
    return jnp.tril(jnp.ones((GROUP, GROUP), jnp.float32))


def group_tables(query_scaled, key_full, log_decay):
    cumulative = jnp.cumsum(log_decay, axis=1)
    middle = cumulative[:, GROUP // 2 - 1 : GROUP // 2]
    ending = cumulative[:, GROUP - 1 :]
    gated_query = query_scaled * jnp.exp(cumulative - middle)
    inverse_key = key_full * jnp.exp(middle - cumulative)
    tail_key = key_full * jnp.exp(ending - cumulative)
    state_query = query_scaled * jnp.exp(cumulative)
    return (cumulative, middle, ending, gated_query, inverse_key, tail_key, state_query)


def group_forward(state, pieces):
    query_scaled, key_full, value_full, log_decay = pieces
    cumulative, middle, ending, gated_query, inverse_key, tail_key, state_query = group_tables(
        query_scaled, key_full, log_decay
    )
    scores = (
        jnp.einsum("sthc,suhc->shtu", gated_query, inverse_key, precision=highest) * causal_mask()
    )
    outputs = jnp.einsum("sthc,shcv->sthv", state_query, state, precision=highest)
    outputs = outputs + jnp.einsum("shtu,suhv->sthv", scores, value_full, precision=highest)
    new_state = jnp.exp(ending[:, 0])[..., None] * state
    new_state = new_state + jnp.einsum("suhc,suhv->shcv", tail_key, value_full, precision=highest)
    return (new_state, (outputs, state))


def group_backward(grad_state, pieces):
    query_scaled, key_full, value_full, log_decay, grad_out, state = pieces
    cumulative, middle, ending, gated_query, inverse_key, tail_key, state_query = group_tables(
        query_scaled, key_full, log_decay
    )
    lower = causal_mask()
    scores = jnp.einsum("sthc,suhc->shtu", gated_query, inverse_key, precision=highest) * lower
    grad_scores = jnp.einsum("sthv,suhv->shtu", grad_out, value_full, precision=highest) * lower
    grad_query = jnp.exp(cumulative) * jnp.einsum(
        "sthv,shcv->sthc", grad_out, state, precision=highest
    )
    grad_query = grad_query + jnp.exp(cumulative - middle) * jnp.einsum(
        "shtu,suhc->sthc", grad_scores, inverse_key, precision=highest
    )
    grad_key = jnp.exp(middle - cumulative) * jnp.einsum(
        "shtu,sthc->suhc", grad_scores, gated_query, precision=highest
    )
    grad_key = grad_key + jnp.exp(ending - cumulative) * jnp.einsum(
        "suhv,shcv->suhc", value_full, grad_state, precision=highest
    )
    grad_value = jnp.einsum("shtu,sthv->suhv", scores, grad_out, precision=highest)
    grad_value = grad_value + jnp.einsum("suhc,shcv->suhv", tail_key, grad_state, precision=highest)
    decay_end = jnp.exp(ending[:, 0])[..., None]
    end_state = decay_end * state + jnp.einsum(
        "suhc,suhv->shcv", tail_key, value_full, precision=highest
    )
    grad_cumul = query_scaled * grad_query - key_full * grad_key
    grad_log = jnp.einsum("ut,suhc->sthc", lower, grad_cumul, precision=highest)
    grad_log = grad_log + jnp.sum(end_state * grad_state, axis=-1)[:, None]
    previous = decay_end * grad_state + jnp.einsum(
        "sthc,sthv->shcv", state_query, grad_out, precision=highest
    )
    return (previous, (grad_query, grad_key, grad_value, grad_log))


def split_groups(array):
    lead, length = (array.shape[0], array.shape[1])
    shaped = array.reshape(lead, length // GROUP, GROUP, array.shape[2], array.shape[3])
    return jnp.moveaxis(shaped, 1, 0)


def join_groups(array):
    moved = jnp.moveaxis(array, 0, 1)
    return moved.reshape(
        moved.shape[0], moved.shape[1] * moved.shape[2], moved.shape[3], moved.shape[4]
    )


def chain_combine(earlier, later):
    return (earlier[0] * later[0], later[0][..., None] * earlier[1] + later[1])


def grad_combine(earlier, later):
    return (earlier[0] * later[0], later[1] + later[0][..., None] * earlier[1])


def matmul(left, right):
    return jnp.dot(left, right, preferred_element_type=jnp.float32)


def contract_rows(left, right):
    return lax.dot_general(
        left, right, (((0,), (0,)), ((), ())), preferred_element_type=jnp.float32
    )


def times_transpose(left, right):
    return lax.dot_general(
        left, right, (((1,), (1,)), ((), ())), preferred_element_type=jnp.float32
    )


def local(
    inputs,
    cotangent,
    mixer_gain,
    feed_gain,
    w_query,
    w_key,
    w_value,
    w_outgate,
    w_decay_down,
    w_decay_up,
    decay_bias,
    head_gain,
    w_output,
    w_gate,
    w_up,
    w_down,
):
    whole = (
        lax.all_gather(mixer_gain, ("seq", "batch"), axis=0, tiled=True),
        lax.all_gather(feed_gain, ("seq", "batch"), axis=0, tiled=True),
        lax.all_gather(w_query, ("seq", "batch"), axis=0, tiled=True),
        lax.all_gather(w_key, ("seq", "batch"), axis=0, tiled=True),
        lax.all_gather(w_value, ("seq", "batch"), axis=0, tiled=True),
        lax.all_gather(w_outgate, ("seq", "batch"), axis=0, tiled=True),
        lax.all_gather(w_decay_down, ("seq", "batch"), axis=0, tiled=True),
        lax.all_gather(w_decay_up, ("seq", "batch"), axis=1, tiled=True),
        lax.all_gather(decay_bias, ("seq", "batch"), axis=0, tiled=True),
        lax.all_gather(head_gain, ("seq", "batch"), axis=0, tiled=True),
        lax.all_gather(w_output, ("seq", "batch"), axis=0, tiled=True),
        lax.all_gather(w_gate, ("seq", "batch"), axis=0, tiled=True),
        lax.all_gather(w_up, ("seq", "batch"), axis=0, tiled=True),
        lax.all_gather(w_down, ("seq", "batch"), axis=0, tiled=True),
    )
    (
        gain_one,
        gain_two,
        proj_query,
        proj_key,
        proj_value,
        proj_gate,
        decay_down,
        decay_up,
        bias_full,
        norm_head,
        proj_output,
        feed_gate,
        feed_up,
        feed_down,
    ) = whole
    seqs_here, tokens_here, width = inputs.shape
    rows = seqs_here * tokens_here
    key_scale = KEY_DIM ** (-0.5)
    shape_key = (seqs_here, tokens_here, HEADS, KEY_DIM)
    shape_value = (seqs_here, tokens_here, HEADS, VALUE_DIM)
    hidden_in = inputs.reshape(rows, width).astype(jnp.float32)
    mixer_scale = lax.rsqrt(jnp.mean(hidden_in * hidden_in, axis=-1, keepdims=True) + epsilon)
    normed = (hidden_in * mixer_scale * gain_one.astype(jnp.float32)).astype(jnp.bfloat16)
    query_b = matmul(normed, proj_query).astype(jnp.bfloat16)
    key_b = matmul(normed, proj_key).astype(jnp.bfloat16)
    value_b = matmul(normed, proj_value).astype(jnp.bfloat16)
    gate_pre = matmul(normed, proj_gate)
    rank_act = matmul(normed, decay_down).astype(jnp.bfloat16)
    decay_pre = matmul(rank_act, decay_up) + bias_full.astype(jnp.float32)
    log_decay = jax.nn.log_sigmoid(decay_pre) / 16.0
    query_scaled = query_b.astype(jnp.float32).reshape(shape_key) * key_scale
    key_full = key_b.astype(jnp.float32).reshape(shape_key)
    value_full = value_b.astype(jnp.float32).reshape(shape_value)
    decay_rows = log_decay.reshape(shape_key)
    cumulative_dev = jnp.cumsum(decay_rows, axis=1)
    total = cumulative_dev[:, -1]
    decay_total = jnp.exp(total)
    local_state = jnp.einsum(
        "sthc,sthv->shcv",
        key_full * jnp.exp(total[:, None] - cumulative_dev),
        value_full,
        precision=highest,
    )
    start_state = entering(
        (decay_total, local_state),
        "seq",
        chain_combine,
        (jnp.ones_like(decay_total), jnp.zeros_like(local_state)),
        False,
    )[1]
    group_pieces = (
        split_groups(query_scaled),
        split_groups(key_full),
        split_groups(value_full),
        split_groups(decay_rows),
    )
    final_state, (group_out, group_starts) = lax.scan(group_forward, start_state, group_pieces)
    mixed = join_groups(group_out)
    head_scale = lax.rsqrt(jnp.mean(mixed * mixed, axis=-1, keepdims=True) + epsilon)
    head_normed = mixed * head_scale * norm_head.astype(jnp.float32)
    gate_heads = gate_pre.reshape(shape_value)
    gate_sig = jax.nn.sigmoid(gate_heads)
    swish = gate_heads * gate_sig
    gated = (head_normed * swish).astype(jnp.bfloat16).reshape(rows, HEADS * VALUE_DIM)
    middle = hidden_in + matmul(gated, proj_output)
    feed_scale = lax.rsqrt(jnp.mean(middle * middle, axis=-1, keepdims=True) + epsilon)
    normed_two = (middle * feed_scale * gain_two.astype(jnp.float32)).astype(jnp.bfloat16)
    up_gate = matmul(normed_two, feed_gate)
    up_lin = matmul(normed_two, feed_up)
    up_sig = jax.nn.sigmoid(up_gate)
    activated = (up_gate * up_sig * up_lin).astype(jnp.bfloat16)
    result = middle + matmul(activated, feed_down)
    grad_rows = cotangent.reshape(rows, width)
    grad_b = grad_rows.astype(jnp.bfloat16)
    grad_down = contract_rows(activated, grad_b)
    act_grad = times_transpose(grad_b, feed_down)
    gate_grad = (act_grad * up_lin * up_sig * (1.0 + up_gate * (1.0 - up_sig))).astype(jnp.bfloat16)
    lin_grad = (act_grad * up_gate * up_sig).astype(jnp.bfloat16)
    grad_gate = contract_rows(normed_two, gate_grad)
    grad_up = contract_rows(normed_two, lin_grad)
    normed_two_grad = times_transpose(gate_grad, feed_gate) + times_transpose(lin_grad, feed_up)
    grad_feed_gain = jnp.sum(normed_two_grad * middle * feed_scale, axis=0)
    scaled_two = normed_two_grad * gain_two.astype(jnp.float32)
    middle_grad = (
        grad_rows
        + feed_scale * scaled_two
        - middle * feed_scale**3 * jnp.mean(scaled_two * middle, axis=-1, keepdims=True)
    )
    middle_b = middle_grad.astype(jnp.bfloat16)
    grad_output = contract_rows(gated, middle_b)
    gated_grad = times_transpose(middle_b, proj_output).reshape(shape_value)
    head_normed_grad = gated_grad * swish
    grad_head_gain = jnp.sum(head_normed_grad * mixed * head_scale, axis=(0, 1, 2))
    scaled_head = head_normed_grad * norm_head.astype(jnp.float32)
    mixed_grad = head_scale * scaled_head - mixed * head_scale**3 * jnp.mean(
        scaled_head * mixed, axis=-1, keepdims=True
    )
    outgate_grad = (
        (gated_grad * head_normed * gate_sig * (1.0 + gate_heads * (1.0 - gate_sig)))
        .reshape(rows, HEADS * VALUE_DIM)
        .astype(jnp.bfloat16)
    )
    local_grad = jnp.einsum(
        "sthc,sthv->shcv", query_scaled * jnp.exp(cumulative_dev), mixed_grad, precision=highest
    )
    end_grad = entering(
        (decay_total, local_grad),
        "seq",
        grad_combine,
        (jnp.ones_like(decay_total), jnp.zeros_like(local_grad)),
        True,
    )[1]
    back_pieces = group_pieces + (split_groups(mixed_grad), group_starts)
    begin_grad, (query_groups, key_groups, value_groups, log_groups) = lax.scan(
        group_backward, end_grad, back_pieces, reverse=True
    )
    query_grad = (
        (join_groups(query_groups) * key_scale).reshape(rows, HEADS * KEY_DIM).astype(jnp.bfloat16)
    )
    key_grad = join_groups(key_groups).reshape(rows, HEADS * KEY_DIM).astype(jnp.bfloat16)
    value_grad = join_groups(value_groups).reshape(rows, HEADS * VALUE_DIM).astype(jnp.bfloat16)
    log_grad = join_groups(log_groups).reshape(rows, HEADS * KEY_DIM)
    decay_grad = log_grad * jax.nn.sigmoid(-decay_pre) / 16.0
    grad_decay_bias = jnp.sum(decay_grad, axis=0)
    decay_grad_b = decay_grad.astype(jnp.bfloat16)
    grad_decay_up = contract_rows(rank_act, decay_grad_b)
    rank_grad = times_transpose(decay_grad_b, decay_up).astype(jnp.bfloat16)
    grad_decay_down = contract_rows(normed, rank_grad)
    grad_query = contract_rows(normed, query_grad)
    grad_key = contract_rows(normed, key_grad)
    grad_value = contract_rows(normed, value_grad)
    grad_outgate = contract_rows(normed, outgate_grad)
    normed_grad = (
        times_transpose(query_grad, proj_query)
        + times_transpose(key_grad, proj_key)
        + times_transpose(value_grad, proj_value)
    )
    normed_grad = (
        normed_grad
        + times_transpose(outgate_grad, proj_gate)
        + times_transpose(rank_grad, decay_down)
    )
    grad_mixer_gain = jnp.sum(normed_grad * hidden_in * mixer_scale, axis=0)
    scaled_one = normed_grad * gain_one.astype(jnp.float32)
    input_grad = (
        middle_grad
        + mixer_scale * scaled_one
        - hidden_in * mixer_scale**3 * jnp.mean(scaled_one * hidden_in, axis=-1, keepdims=True)
    )
    summed = (
        lax.psum_scatter(grad_mixer_gain, ("seq", "batch"), scatter_dimension=0, tiled=True),
        lax.psum_scatter(grad_feed_gain, ("seq", "batch"), scatter_dimension=0, tiled=True),
        lax.psum_scatter(grad_query, ("seq", "batch"), scatter_dimension=0, tiled=True),
        lax.psum_scatter(grad_key, ("seq", "batch"), scatter_dimension=0, tiled=True),
        lax.psum_scatter(grad_value, ("seq", "batch"), scatter_dimension=0, tiled=True),
        lax.psum_scatter(grad_outgate, ("seq", "batch"), scatter_dimension=0, tiled=True),
        lax.psum_scatter(grad_decay_down, ("seq", "batch"), scatter_dimension=0, tiled=True),
        lax.psum_scatter(grad_decay_up, ("seq", "batch"), scatter_dimension=1, tiled=True),
        lax.psum_scatter(grad_decay_bias, ("seq", "batch"), scatter_dimension=0, tiled=True),
        lax.psum_scatter(grad_head_gain, ("seq", "batch"), scatter_dimension=0, tiled=True),
        lax.psum_scatter(grad_output, ("seq", "batch"), scatter_dimension=0, tiled=True),
        lax.psum_scatter(grad_gate, ("seq", "batch"), scatter_dimension=0, tiled=True),
        lax.psum_scatter(grad_up, ("seq", "batch"), scatter_dimension=0, tiled=True),
        lax.psum_scatter(grad_down, ("seq", "batch"), scatter_dimension=0, tiled=True),
    )
    return (result.reshape(inputs.shape), input_grad.reshape(inputs.shape)) + tuple(summed)


def solution(mesh):
    placed = (
        P("batch", "seq", None),
        P("batch", "seq", None),
        P(("seq", "batch")),
        P(("seq", "batch")),
        P(("seq", "batch"), None),
        P(("seq", "batch"), None),
        P(("seq", "batch"), None),
        P(("seq", "batch"), None),
        P(("seq", "batch"), None),
        P(None, ("seq", "batch")),
        P(("seq", "batch")),
        P(("seq", "batch")),
        P(("seq", "batch"), None),
        P(("seq", "batch"), None),
        P(("seq", "batch"), None),
        P(("seq", "batch"), None),
    )
    return jax.shard_map(
        local,
        mesh=mesh,
        in_specs=placed,
        out_specs=(
            P("batch", "seq", None),
            P("batch", "seq", None),
            P(("seq", "batch")),
            P(("seq", "batch")),
            P(("seq", "batch"), None),
            P(("seq", "batch"), None),
            P(("seq", "batch"), None),
            P(("seq", "batch"), None),
            P(("seq", "batch"), None),
            P(None, ("seq", "batch")),
            P(("seq", "batch")),
            P(("seq", "batch")),
            P(("seq", "batch"), None),
            P(("seq", "batch"), None),
            P(("seq", "batch"), None),
            P(("seq", "batch"), None),
        ),
        check_vma=False,
    )
```

profile of v0, /device:TPU:0, one launch (start us, length us, event | category | flops | bytes accessed | tf_op | source)
XLA Modules:
  0.0 2214.9 jit_solution(13865441577084023325)
XLA Ops:
  12.8 42.1 %all-reduce.9 = (bf16[1024]{0:T(1024)(128)(2,1)S(1)}, bf16[256]{0:T(256)(128)(2,1)S(1)}, bf16[512]{0:T(512)(128)(2,1)S(1)}, bf16[1024]{0:T(1024)(128)(2,1)S(1)}) all-reduce(bf16[1024]{0:T(1024)(128)(2,1)S(1)} %dynamic-update-slice, bf16[256]{0:T(256)(128)(2,1)S(1)} %dynamic-update-slice.2, ...), channel_id=1, replica_groups=mesh['seq'=8,'batch'=4] {'seq','batch'}, use_global_device_ids=true, to_apply=%add | all-reduce | flops 2816 | bytes 11264
  54.9 40.8 %all-gather.2 = bf16[32,32,16]{1,2,0:T(8,128)(2,1)S(1)} all-gather(bf16[1,32,16]{1,2,0:T(8,128)(2,1)} %bitcast.650), channel_id=1, replica_groups=mesh['seq'=8,'batch'=4] {'seq','batch'}, dimensions={0}, use_global_device_ids=true | all-gather | bytes 33792 | tf_op jit(solution)/shard_map/all_gather | solution.py:161
  96.8 37.0 %all_gather.62 = bf16[16,512]{0,1:T(8,128)(2,1)S(1)} all-gather(bf16[16,16]{0,1:T(8,128)(2,1)S(1)} %copy.201), channel_id=1, replica_groups=mesh['seq'=8,'batch'=4] {'seq','batch'}, dimensions={1}, use_global_device_ids=true | all-gather | bytes 16896 | tf_op jit(solution)/shard_map/all_gather | solution.py:162
  144.5 36.7 %all-gather.16.cloned.1.call-done = bf16[1024,1024]{1,0:T(8,128)(2,1)} async-done(((bf16[32,1024]{1,0:T(8,128)(2,1)}), bf16[1024,1024]{1,0:T(8,128)(2,1)}) %all-gather.16.cloned.1.call-update) | async-done | bytes 2097168 | tf_op jit(solution)/shard_map/all_gather | solution.py:159
  194.7 26.7 %all_gather.64 = f32[8,1,4,128]{3,2,1,0:T(4,128)S(1)} all-gather(f32[1,1,4,128]{3,2,1,0:T(4,128)S(1)} %get-tuple-element.790), channel_id=1, replica_groups=mesh['seq'=8,'batch'=4] {'seq'}, dimensions={0}, use_global_device_ids=true | all-gather | bytes 18432 | tf_op jit(solution)/shard_map/all_gather | solution.py:18
  224.3 32.8 %all-gather.30.cloned.1.call-done = f32[32,128,256]{2,1,0:T(8,128)} async-done(((f32[4,128,256]{2,1,0:T(8,128)}), f32[32,128,256]{2,1,0:T(8,128)}) %all-gather.30.cloned.1.call-update) | async-done | bytes 4194320 | tf_op jit(solution)/shard_map/all_gather | solution.py:18
  292.0 22.6 %all-gather.20.cloned.1.call-done = bf16[1024,1024]{1,0:T(8,128)(2,1)} async-done(((bf16[32,1024]{1,0:T(8,128)(2,1)}), bf16[1024,1024]{1,0:T(8,128)(2,1)}) %all-gather.20.cloned.1.call-update) | async-done | bytes 2097168 | tf_op jit(solution)/shard_map/all_gather | solution.py:160
  318.6 53.8 %all-gather.22.cloned.1.call-done = bf16[1024,1024]{1,0:T(8,128)(2,1)} async-done(((bf16[32,1024]{1,0:T(8,128)(2,1)}), bf16[1024,1024]{1,0:T(8,128)(2,1)}) %all-gather.22.cloned.1.call-update) | async-done | bytes 2097168 | tf_op jit(solution)/shard_map/all_gather | solution.py:165
  376.0 65.5 %all-gather.24.cloned.1.call-done = bf16[1024,2816]{1,0:T(8,128)(2,1)} async-done(((bf16[32,2816]{1,0:T(8,128)(2,1)}), bf16[1024,2816]{1,0:T(8,128)(2,1)}) %all-gather.24.cloned.1.call-update) | async-done | bytes 5767184 | tf_op jit(solution)/shard_map/all_gather | solution.py:166
  447.4 63.0 %all-gather.26.cloned.1.call-done = bf16[1024,2816]{1,0:T(8,128)(2,1)} async-done(((bf16[32,2816]{1,0:T(8,128)(2,1)}), bf16[1024,2816]{1,0:T(8,128)(2,1)}) %all-gather.26.cloned.1.call-update) | async-done | bytes 5767184 | tf_op jit(solution)/shard_map/all_gather | solution.py:167
  516.2 63.0 %all-gather.28.cloned.1.call-done = bf16[2816,1024]{1,0:T(8,128)(2,1)} async-done(((bf16[88,1024]{1,0:T(8,128)(2,1)}), bf16[2816,1024]{1,0:T(8,128)(2,1)}) %all-gather.28.cloned.1.call-update) | async-done | bytes 5767184 | tf_op jit(solution)/shard_map/all_gather | solution.py:168
  621.1 67.9 %all-gather.32.cloned.1.call-done = f32[32,128,256]{2,1,0:T(8,128)} async-done(((f32[4,128,256]{2,1,0:T(8,128)}), f32[32,128,256]{2,1,0:T(8,128)}) %all-gather.32.cloned.1.call-update) | async-done | bytes 4194320 | tf_op jit(solution)/shard_map/all_gather | solution.py:18
  701.0 68.4 %while.71 = (s32[]{:T(128)}, f32[1,4,128,256]{3,2,1,0:T(8,128)S(1)}, f32[4,1,64,4,128]{4,2,3,1,0:T(8,128)}, bf16[4,1,64,4,128]{4,2,3,1,0:T(8,128)(2,1)}, bf16[4,...) while((s32[]{:T(128)}, ...), condition=%wide.region_17.18_spmd.clone, body=%wide.region_14.17_spmd.sunk.clone | while | flops 708263424 | bytes 16000373 | solution.py:284
  826.7 39.1 %all-reduce.8 = (f32[1024]{0:T(1024)S(1)}, f32[1024]{0:T(1024)S(1)}, f32[512]{0:T(512)S(1)}, f32[256]{0:T(256)S(1)}) all-reduce(f32[1024]{0:T(1024)S(1)} %get-tuple-element.692, f32[1024]{0:T(1024)S(1)} %copy-done.45, f32[512]{0:T(512)S(1)} %get-tuple-element.766, ...), channel_id=4, replica_groups=mesh['seq'=8,'batch'=4] {'seq','batch'}, use_global_device_ids=true, to_apply=%region_20.21.clone | all-reduce | flops 2816 | bytes 22528
  869.4 38.6 %reduce-scatter.33.cloned.1.call-done = f32[16,16]{1,0:T(8,128)} async-done(((f32[512,16]{1,0:T(8,128)}), f32[16,16]{1,0:T(8,128)}) %reduce-scatter.33.cloned.1.call-update) | async-done | bytes 1040
  909.4 132.4 %reduce-scatter.31.cloned.1.call-done = f32[32,16]{1,0:T(8,128)} async-done(((f32[1024,16]{1,0:T(8,128)}), f32[32,16]{1,0:T(8,128)}) %reduce-scatter.31.cloned.1.call-update) | async-done | bytes 2064
  1043.2 140.0 %reduce-scatter.21.cloned.1.call-done = f32[32,1024]{1,0:T(8,128)} async-done(((f32[1024,1024]{1,0:T(8,128)}), f32[32,1024]{1,0:T(8,128)}) %reduce-scatter.21.cloned.1.call-update) | async-done | bytes 131088 | tf_op jit(solution)/shard_map/reduce_scatter | solution.py:326
  1183.2 140.7 %reduce-scatter.23.cloned.1.call-done = f32[32,1024]{1,0:T(8,128)} async-done(((f32[1024,1024]{1,0:T(8,128)}), f32[32,1024]{1,0:T(8,128)}) %reduce-scatter.23.cloned.1.call-update) | async-done | bytes 131088 | tf_op jit(solution)/shard_map/reduce_scatter | solution.py:331
  1323.9 137.0 %reduce-scatter.15.cloned.1.call-done = f32[32,512]{1,0:T(8,128)} async-done(((f32[1024,512]{1,0:T(8,128)}), f32[32,512]{1,0:T(8,128)}) %reduce-scatter.15.cloned.1.call-update) | async-done | bytes 65552 | tf_op jit(solution)/shard_map/reduce_scatter | solution.py:323
  1460.9 137.0 %reduce-scatter.17.cloned.1.call-done = f32[32,512]{1,0:T(8,128)} async-done(((f32[1024,512]{1,0:T(8,128)}), f32[32,512]{1,0:T(8,128)}) %reduce-scatter.17.cloned.1.call-update) | async-done | bytes 65552 | tf_op jit(solution)/shard_map/reduce_scatter | solution.py:324
  1597.9 141.4 %reduce-scatter.19.cloned.1.call-done = f32[32,1024]{1,0:T(8,128)} async-done(((f32[1024,1024]{1,0:T(8,128)}), f32[32,1024]{1,0:T(8,128)}) %reduce-scatter.19.cloned.1.call-update) | async-done | bytes 131088 | tf_op jit(solution)/shard_map/reduce_scatter | solution.py:325
  1739.2 153.9 %reduce-scatter.25.cloned.1.call-done = f32[32,2816]{1,0:T(8,128)} async-done(((f32[1024,2816]{1,0:T(8,128)}), f32[32,2816]{1,0:T(8,128)}) %reduce-scatter.25.cloned.1.call-update) | async-done | bytes 360464 | tf_op jit(solution)/shard_map/reduce_scatter | solution.py:332
  1893.1 157.4 %reduce-scatter.27.cloned.1.call-done = f32[32,2816]{1,0:T(8,128)} async-done(((f32[1024,2816]{1,0:T(8,128)}), f32[32,2816]{1,0:T(8,128)}) %reduce-scatter.27.cloned.1.call-update) | async-done | bytes 360464 | tf_op jit(solution)/shard_map/reduce_scatter | solution.py:333
  2050.5 157.3 %reduce-scatter.29.cloned.1.call-done = f32[88,1024]{1,0:T(8,128)} async-done(((f32[2816,1024]{1,0:T(8,128)}), f32[88,1024]{1,0:T(8,128)}) %reduce-scatter.29.cloned.1.call-update) | async-done | bytes 360464 | tf_op jit(solution)/shard_map/reduce_scatter | solution.py:334
  (448 shorter events, 311.8 us)
Async XLA Ops:
  7.2 131.9 %all-gather.18.cloned.1.call-start = ((), (), s32[]{:S(2)}) async-start(), calls=%async_computation.12 | async-start | bytes 1081344 | tf_op jit(solution)/shard_map/all_gather | solution.py:157
  7.9 133.1 %all-gather.14.cloned.1.call-start = ((), (), s32[]{:S(2)}) async-start(), calls=%async_computation.10 | async-start | bytes 1081344 | tf_op jit(solution)/shard_map/all_gather | solution.py:158
  8.7 172.6 %all-gather.16.cloned.1.call-start = ((), (), s32[]{:S(2)}) async-start(), calls=%async_computation.11 | async-start | bytes 2162688 | tf_op jit(solution)/shard_map/all_gather | solution.py:159
  9.4 247.7 %all-gather.30.cloned.1.call-start = ((), (), s32[]{:S(2)}) async-start(), calls=%async_computation.26 | async-start | bytes 4718592 | tf_op jit(solution)/shard_map/all_gather | solution.py:18
  135.6 179.0 %copy-start.41 = (f32[256]{0:T(256)}, f32[256]{0:T(256)S(1)}, u32[]{:S(2)}) copy-start(f32[256]{0:T(256)S(1)} %get-tuple-element.794) | copy-start | bytes 3076
  185.0 129.6 %all-gather.20.cloned.1.call-start = ((), (), s32[]{:S(2)}) async-start(), calls=%async_computation.13 | async-start | bytes 2162688 | tf_op jit(solution)/shard_map/all_gather | solution.py:160
  185.6 186.8 %all-gather.22.cloned.1.call-start = ((), (), s32[]{:S(2)}) async-start(), calls=%async_computation.14 | async-start | bytes 2162688 | tf_op jit(solution)/shard_map/all_gather | solution.py:165
  186.2 255.3 %all-gather.24.cloned.1.call-start = ((), (), s32[]{:S(2)}) async-start(), calls=%async_computation.15 | async-start | bytes 5947392 | tf_op jit(solution)/shard_map/all_gather | solution.py:166
  186.9 323.4 %all-gather.26.cloned.1.call-start = ((), (), s32[]{:S(2)}) async-start(), calls=%async_computation.16 | async-start | bytes 5947392 | tf_op jit(solution)/shard_map/all_gather | solution.py:167
  187.7 391.5 %all-gather.28.cloned.1.call-start = ((), (), s32[]{:S(2)}) async-start(), calls=%async_computation.17 | async-start | bytes 5947392 | tf_op jit(solution)/shard_map/all_gather | solution.py:168
  188.4 500.6 %all-gather.32.cloned.1.call-start = ((), (), s32[]{:S(2)}) async-start(), calls=%async_computation.27 | async-start | bytes 4718592 | tf_op jit(solution)/shard_map/all_gather | solution.py:18
  287.1 322.4 %copy-start.4 = (f32[4,1,64,4,256]{4,2,3,1,0:T(8,128)}, f32[4,1,64,4,256]{4,2,3,1,0:T(8,128)S(1)}, u32[]{:S(2)}) copy-start(f32[4,1,64,4,256]{4,2,3,1,0:T(8,128)S(1)} %get-tuple-element.525) | copy-start | bytes 3145732
  318.6 56.3 %copy-start.24 = (bf16[256,1024]{1,0:T(8,128)(2,1)}, bf16[256,1024]{1,0:T(8,128)(2,1)S(1)}, u32[]{:S(2)}) copy-start(bf16[256,1024]{1,0:T(8,128)(2,1)S(1)} %get-tuple-element.799) | copy-start | bytes 1572868
  376.0 134.3 %copy-start.11 = (bf16[256,1024]{1,0:T(8,128)(2,1)}, bf16[256,1024]{1,0:T(8,128)(2,1)S(1)}, u32[]{:S(2)}) copy-start(bf16[256,1024]{1,0:T(8,128)(2,1)S(1)} %multiply_convert_fusion.4) | copy-start | bytes 1572868
  617.4 290.6 %reduce-scatter.33.cloned.1.call-start = ((), (), s32[]{:S(2)}) async-start(), calls=%async_computation.29 | async-start | bytes 270336
  773.7 268.2 %reduce-scatter.31.cloned.1.call-start = ((), (), s32[]{:S(2)}) async-start(), calls=%async_computation.28 | async-start | bytes 540672
  775.6 407.6 %reduce-scatter.21.cloned.1.call-start = ((), (), s32[]{:S(2)}) async-start(), calls=%async_computation.21 | async-start | bytes 4325376 | tf_op jit(solution)/shard_map/reduce_scatter | solution.py:326
  778.5 545.4 %reduce-scatter.23.cloned.1.call-start = ((), (), s32[]{:S(2)}) async-start(), calls=%async_computation.22 | async-start | bytes 4325376 | tf_op jit(solution)/shard_map/reduce_scatter | solution.py:331
  782.6 678.3 %reduce-scatter.15.cloned.1.call-start = ((), (), s32[]{:S(2)}) async-start(), calls=%async_computation.18 | async-start | bytes 2162688 | tf_op jit(solution)/shard_map/reduce_scatter | solution.py:323
  785.9 812.0 %reduce-scatter.17.cloned.1.call-start = ((), (), s32[]{:S(2)}) async-start(), calls=%async_computation.19 | async-start | bytes 2162688 | tf_op jit(solution)/shard_map/reduce_scatter | solution.py:324
  788.1 951.2 %reduce-scatter.19.cloned.1.call-start = ((), (), s32[]{:S(2)}) async-start(), calls=%async_computation.20 | async-start | bytes 4325376 | tf_op jit(solution)/shard_map/reduce_scatter | solution.py:325
  791.4 1101.7 %reduce-scatter.25.cloned.1.call-start = ((), (), s32[]{:S(2)}) async-start(), calls=%async_computation.23 | async-start | bytes 11894784 | tf_op jit(solution)/shard_map/reduce_scatter | solution.py:332
  799.8 1250.7 %reduce-scatter.27.cloned.1.call-start = ((), (), s32[]{:S(2)}) async-start(), calls=%async_computation.24 | async-start | bytes 11894784 | tf_op jit(solution)/shard_map/reduce_scatter | solution.py:333
  807.2 1400.6 %reduce-scatter.29.cloned.1.call-start = ((), (), s32[]{:S(2)}) async-start(), calls=%async_computation.25 | async-start | bytes 11894784 | tf_op jit(solution)/shard_map/reduce_scatter | solution.py:334
  (65 other events, 302.6 us)
Sparse Core Ops, SparseCore 0:
  10.9 56.5 all-gather.17
  70.3 52.7 all-gather.13
  125.9 55.2 all-gather.15
  185.1 71.8 all-gather.29
  259.8 54.8 all-gather.19
  317.3 55.0 all-gather.21
  375.3 66.1 all-gather.23
  444.4 65.9 all-gather.25
  513.3 65.9 all-gather.27
  617.5 71.4 all-gather.31
  773.8 134.1 reduce-scatter.32
  910.1 131.6 reduce-scatter.30
  1044.7 138.4 reduce-scatter.20
  1185.9 137.9 reduce-scatter.22
  1326.6 134.2 reduce-scatter.14
  1463.6 134.2 reduce-scatter.16
  1600.6 138.6 reduce-scatter.18
  1742.0 151.0 reduce-scatter.24
  1896.0 154.4 reduce-scatter.26
  2053.3 154.5 reduce-scatter.28
where the time goes:
time: 2230 us; the launch traced here: 2210 us
  waiting for transfers between devices  1750 us (78%)
  blocking collectives  186 us (8%)
  matrix products  152 us (7%)
  other arithmetic  62.2 us (3%)
  local copies, waits for them, and re-layouts  51.1 us (2%)
    unnamed x22, waiting for transfers between devices  176 us
    reduce_scatter x1, waiting for transfers between devices, local(): lax.psum_scatter(grad_up, ('seq', 'batch'), scatter_dimension=0, tiled=True)  157 us
    reduce_scatter x1, waiting for transfers between devices, local(): lax.psum_scatter(grad_down, ('seq', 'batch'), scatter_dimension=0, tiled=...  157 us
    reduce_scatter x1, waiting for transfers between devices, local(): lax.psum_scatter(grad_gate, ('seq', 'batch'), scatter_dimension=0, tiled=...  154 us
    reduce_scatter x1, waiting for transfers between devices, local(): lax.psum_scatter(grad_value, ('seq', 'batch'), scatter_dimension=0, tiled...  141 us
    reduce_scatter x1, waiting for transfers between devices, local(): lax.psum_scatter(grad_output, ('seq', 'batch'), scatter_dimension=0, tile...  141 us
    reduce_scatter x1, waiting for transfers between devices, local(): lax.psum_scatter(grad_outgate, ('seq', 'batch'), scatter_dimension=0, til...  140 us
    reduce_scatter x1, waiting for transfers between devices, local(): lax.psum_scatter(grad_key, ('seq', 'batch'), scatter_dimension=0, tiled=T...  137 us
  transfers between devices with their start and end apart: 20, of which 18 were waited for; matrix products, arithmetic and copies ran while one was open for 6% of the time, Pallas kernels for 0%

commit v1 on v0

--- a/solution.py
+++ b/solution.py
@@ -1,34 +1,313 @@
+import functools
+
 import jax
 import jax.numpy as jnp
 from jax import lax
+from jax.experimental import pallas as pl
+from jax.experimental.pallas import tpu as pltpu
 from jax.sharding import PartitionSpec as P
 
 HEADS = 4
 KEY_DIM = 128
 VALUE_DIM = 256
 GROUP = 64
-
+LANES = 128
+MESH = pl.DeviceIdType.MESH
 
 epsilon = 1e-06
 highest = lax.Precision.HIGHEST
 
 
-def entering(value, axis, combine, identity, reverse):
-    length, mine = (lax.axis_size(axis), lax.axis_index(axis))
-    everything = jax.tree.map(lambda part: lax.all_gather(part, axis), value)
-    start = jax.tree.map(
-        lambda part, zero: jnp.broadcast_to(jnp.asarray(zero, part.dtype), part.shape),
-        value,
-        identity,
-    )
-
-    def turn(k, before):
-        at = length - 1 - k if reverse else k
-        reached = at > mine if reverse else at < mine
-        new = combine(before, jax.tree.map(lambda part: part[at], everything))
-        return jax.tree.map(lambda a, b: jnp.where(reached, a, b), new, before)
-
-    return lax.fori_loop(0, length, turn, start)
+def grid_of(shape):
+    seq, batch = shape["seq"], shape["batch"]
+    outer = 4 if seq % 4 == 0 else seq
+    core = 2 if batch % 2 == 0 else 1
+    return (outer, seq // outer, batch // core, core)
+
+
+def coords_of(sizes):
+    seq, batch = lax.axis_index("seq"), lax.axis_index("batch")
+    return (seq // sizes[1], seq % sizes[1], batch // sizes[3], batch % sizes[3])
+
+
+def device_of(sizes, at):
+    return {"seq": at[0] * sizes[1] + at[1], "batch": at[2] * sizes[3] + at[3]}
+
+
+def moved(sizes, at, axis, by):
+    new = list(at)
+    new[axis] = lax.rem(at[axis] + (by % sizes[axis]), sizes[axis])
+    return tuple(new)
+
+
+def region(ref, free, at):
+    return ref.at[tuple(slice(None) if k in free else at[k] for k in range(4))]
+
+
+def orders_of(sizes):
+    if sizes[1] == sizes[2] and sizes[3] == 2:
+        return ((0, 1, 2, 3), (0, 2, 1, 3))
+    return ((0, 1, 2, 3),)
+
+
+def greet(sizes, at):
+    barrier = pltpu.get_barrier_semaphore()
+    count = 0
+    for axis in range(4):
+        for by in range(1, sizes[axis]):
+            pl.semaphore_signal(
+                barrier,
+                inc=1,
+                device_id=device_of(sizes, moved(sizes, at, axis, by)),
+                device_id_type=MESH,
+            )
+            count += 1
+    pl.semaphore_wait(barrier, count)
+
+
+def gather_kernel(sizes, count, *refs):
+    shards, wholes = refs[:count], refs[count : 2 * count]
+    send_sem, recv_sem, own_sem = refs[2 * count :]
+    at = coords_of(sizes)
+    greet(sizes, at)
+
+    def copies(item, order, step, arriving):
+        axis, free = order[step], order[:step]
+        made = []
+        for by in range(1, sizes[axis]):
+            source = moved(sizes, at, axis, -by) if arriving else at
+            place = region(wholes[item], free, source)
+            made.append(
+                pltpu.make_async_remote_copy(
+                    src_ref=shards[item] if step == 0 and not arriving else place,
+                    dst_ref=place,
+                    send_sem=send_sem.at[item, step, by - 1],
+                    recv_sem=recv_sem.at[item, step, by - 1],
+                    device_id=device_of(sizes, moved(sizes, at, axis, by)),
+                    device_id_type=MESH,
+                )
+            )
+        return made
+
+    def start(item, order, step):
+        for copy in copies(item, order, step, False):
+            copy.start()
+
+    def arrive(item, order, step):
+        for copy in copies(item, order, step, True):
+            copy.wait_recv()
+
+    def own(item):
+        return pltpu.make_async_copy(
+            shards[item], region(wholes[item], (), at), own_sem.at[item]
+        )
+
+    def run(order):
+        for item in range(count):
+            start(item, order, 0)
+            own(item).start()
+        for tick in range(count + 3):
+            for step in (1, 2, 3):
+                item = tick - step + 1
+                if 0 <= item < count:
+                    arrive(item, order, step - 1)
+                    if step == 1:
+                        own(item).wait()
+                    start(item, order, step)
+            if tick >= 3:
+                arrive(tick - 3, order, 3)
+        for item in range(count):
+            for step in range(4):
+                for copy in copies(item, order, step, False):
+                    copy.wait_send()
+
+    orders = orders_of(sizes)
+    for parity, order in enumerate(orders):
+        pl.when(lax.rem(at[3], len(orders)) == parity)(functools.partial(run, order))
+
+
+def gather_all(sizes, shards, collective_id):
+    count = len(shards)
+    most = max(max(sizes) - 1, 1)
+    wholes = pl.pallas_call(
+        functools.partial(gather_kernel, sizes, count),
+        out_shape=[jax.ShapeDtypeStruct(sizes + s.shape, s.dtype) for s in shards],
+        in_specs=[pl.BlockSpec(memory_space=pltpu.VMEM)] * count,
+        out_specs=[pl.BlockSpec(memory_space=pl.ANY)] * count,
+        scratch_shapes=[
+            pltpu.SemaphoreType.DMA((count, 4, most)),
+            pltpu.SemaphoreType.DMA((count, 4, most)),
+            pltpu.SemaphoreType.DMA((count,)),
+        ],
+        compiler_params=pltpu.CompilerParams(
+            collective_id=collective_id, has_side_effects=True
+        ),
+    )(*shards)
+    return [w.reshape((-1,) + w.shape[4:]) for w in wholes]
+
+
+def scatter_kernel(sizes, count, *refs):
+    grads, outs = refs[:count], refs[count : 2 * count]
+    held, near, half, part, last = (
+        refs[(2 + k) * count : (3 + k) * count] for k in range(5)
+    )
+    send_sem, recv_sem, own_sem = refs[7 * count :]
+    at = coords_of(sizes)
+    greet(sizes, at)
+
+    def landing(item, order, step, by):
+        if step == 3:
+            return near[item]
+        return (last, part, half)[step][item].at[by - 1]
+
+    def copy(item, order, step, by):
+        axis, free = order[step], order[:step]
+        target = moved(sizes, at, axis, by)
+        source = grads[item] if step == 3 else held[item]
+        index = tuple(
+            slice(None) if k in free else target[k] for k in range(4 if step == 3 else 3)
+        )
+        return pltpu.make_async_remote_copy(
+            src_ref=source.at[index],
+            dst_ref=landing(item, order, step, by),
+            send_sem=send_sem.at[item, step, by - 1],
+            recv_sem=recv_sem.at[item, step, by - 1],
+            device_id=device_of(sizes, target),
+            device_id_type=MESH,
+        )
+
+    def start(item, order, step):
+        for by in range(1, sizes[order[step]]):
+            copy(item, order, step, by).start()
+
+    def own(item):
+        return pltpu.make_async_copy(
+            region(grads[item], (0, 1, 2), at), held[item], own_sem.at[item]
+        )
+
+    def gather_in(item, order, step):
+        axis, free = order[step], order[:step]
+        for by in range(1, sizes[axis]):
+            copy(item, order, step, by).wait_recv()
+        if step == 0:
+            total = held[item][at[0], at[1], at[2]].astype(jnp.float32)
+            for by in range(1, sizes[axis]):
+                total = total + last[item][by - 1].astype(jnp.float32)
+            outs[item][...] = total
+            return
+
+        def add(k, carry):
+            for j in range(sizes[free[1]] if len(free) > 1 else 1):
+                for i in range(sizes[free[2]] if len(free) > 2 else 1):
+                    within = (k, j, i)[: len(free)]
+                    place = list(at[:3])
+                    for axis_of, index in zip(free, within):
+                        place[axis_of] = index
+                    place = tuple(place)
+                    total = held[item][place].astype(jnp.float32)
+                    if step == 3:
+                        total = total + near[item][place].astype(jnp.float32)
+                    else:
+                        for by in range(1, sizes[axis]):
+                            total = total + landing(item, order, step, by)[
+                                within
+                            ].astype(jnp.float32)
+                    held[item][place] = total.astype(held[item].dtype)
+            return carry
+
+        lax.fori_loop(0, sizes[0], add, 0)
+
+    def run(order):
+        for item in range(count):
+            start(item, order, 3)
+            own(item).start()
+        for tick in range(count + 3):
+            for step in (3, 2, 1, 0):
+                item = tick - (3 - step)
+                if 0 <= item < count:
+                    if step == 3:
+                        own(item).wait()
+                    gather_in(item, order, step)
+                    if step > 0:
+                        start(item, order, step - 1)
+        for item in range(count):
+            for step in range(4):
+                for by in range(1, sizes[order[step]]):
+                    copy(item, order, step, by).wait_send()
+
+    orders = orders_of(sizes)
+    for parity, order in enumerate(orders):
+        pl.when(lax.rem(at[3], len(orders)) == parity)(functools.partial(run, order))
+
+
+def scatter_all(sizes, grads, collective_id):
+    outer, inner, side, core = sizes
+    count = len(grads)
+    most = max(max(sizes) - 1, 1)
+    shaped = [
+        g.reshape(sizes + (g.shape[0] // (outer * inner * side * core), g.shape[1])) for g in grads
+    ]
+    blocks = [(g.shape[4:], g.dtype) for g in shaped]
+
+    def buffers(lead):
+        return [pltpu.VMEM(lead + block, dtype) for block, dtype in blocks]
+
+    return pl.pallas_call(
+        functools.partial(scatter_kernel, sizes, count),
+        out_shape=[jax.ShapeDtypeStruct(block, jnp.float32) for block, _ in blocks],
+        in_specs=[pl.BlockSpec(memory_space=pl.ANY)] * count,
+        out_specs=[pl.BlockSpec(memory_space=pltpu.VMEM)] * count,
+        scratch_shapes=buffers((outer, inner, side))
+        + buffers((outer, inner, side))
+        + buffers((max(side - 1, 1), outer, inner))
+        + buffers((max(inner - 1, 1), outer))
+        + buffers((max(outer - 1, 1),))
+        + [
+            pltpu.SemaphoreType.DMA((count, 4, most)),
+            pltpu.SemaphoreType.DMA((count, 4, most)),
+            pltpu.SemaphoreType.DMA((count,)),
+        ],
+        compiler_params=pltpu.CompilerParams(
+            collective_id=collective_id, has_side_effects=True, vmem_limit_bytes=60 * 2**20
+        ),
+    )(*shaped)
+
+
+def entering(value, axis, reverse):
+    length = lax.axis_size(axis)
+
+    def shifted(pair, by):
+        pairs = [
+            (k, k - by if reverse else k + by)
+            for k in range(length)
+            if 0 <= (k - by if reverse else k + by) < length
+        ]
+        decay, state = pair
+        moved_state = lax.ppermute(state.astype(jnp.bfloat16), axis, pairs)
+        return (lax.ppermute(decay, axis, pairs), moved_state.astype(jnp.float32))
+
+    def combine(earlier, later):
+        return (earlier[0] * later[0], later[0][..., None] * earlier[1] + later[1])
+
+    whole, before, by = value, None, 1
+    while by < length:
+        come = shifted(whole, by)
+        before = come if before is None else combine(come, before)
+        whole = combine(come, whole)
+        by *= 2
+    return before[1]
+
+
+def small_pack(parts, rows):
+    columns = []
+    for k, part in enumerate(parts):
+        if k not in (0, 3):
+            part = part[..., None]
+        spare = [(0, 0)] * (part.ndim - 2) + [(0, rows - part.shape[-2]), (0, 0)]
+        columns.append(jnp.pad(part, spare))
+    joined = jnp.concatenate(columns, axis=-1)
+    spare = [(0, 0)] * (joined.ndim - 1) + [(0, LANES - joined.shape[-1])]
+    return jnp.pad(joined, spare)
 
 
 def causal_mask():
@@ -109,14 +388,6 @@
     )
 
 
-def chain_combine(earlier, later):
-    return (earlier[0] * later[0], later[0][..., None] * earlier[1] + later[1])
-
-
-def grad_combine(earlier, later):
-    return (earlier[0] * later[0], later[1] + later[0][..., None] * earlier[1])
-
-
 def matmul(left, right):
     return jnp.dot(left, right, preferred_element_type=jnp.float32)
 
@@ -134,6 +405,7 @@
 
 
 def local(
+    sizes,
     inputs,
     cotangent,
     mixer_gain,
@@ -151,38 +423,25 @@
     w_up,
     w_down,
 ):
-    whole = (
-        lax.all_gather(mixer_gain, ("seq", "batch"), axis=0, tiled=True),
-        lax.all_gather(feed_gain, ("seq", "batch"), axis=0, tiled=True),
-        lax.all_gather(w_query, ("seq", "batch"), axis=0, tiled=True),
-        lax.all_gather(w_key, ("seq", "batch"), axis=0, tiled=True),
-        lax.all_gather(w_value, ("seq", "batch"), axis=0, tiled=True),
-        lax.all_gather(w_outgate, ("seq", "batch"), axis=0, tiled=True),
-        lax.all_gather(w_decay_down, ("seq", "batch"), axis=0, tiled=True),
-        lax.all_gather(w_decay_up, ("seq", "batch"), axis=1, tiled=True),
-        lax.all_gather(decay_bias, ("seq", "batch"), axis=0, tiled=True),
-        lax.all_gather(head_gain, ("seq", "batch"), axis=0, tiled=True),
-        lax.all_gather(w_output, ("seq", "batch"), axis=0, tiled=True),
-        lax.all_gather(w_gate, ("seq", "batch"), axis=0, tiled=True),
-        lax.all_gather(w_up, ("seq", "batch"), axis=0, tiled=True),
-        lax.all_gather(w_down, ("seq", "batch"), axis=0, tiled=True),
-    )
-    (
-        gain_one,
-        gain_two,
-        proj_query,
-        proj_key,
-        proj_value,
-        proj_gate,
-        decay_down,
-        decay_up,
-        bias_full,
-        norm_head,
-        proj_output,
-        feed_gate,
-        feed_up,
-        feed_down,
-    ) = whole
+    rows_of, kd_here, vd_here = w_query.shape[0], w_decay_up.shape[1], head_gain.shape[0]
+    small = small_pack(
+        (w_decay_down, mixer_gain, feed_gain, w_decay_up.T, decay_bias, head_gain), rows_of
+    )
+    shards = (
+        small, w_query, w_key, w_value, w_outgate, w_output, w_gate, w_up, w_down
+    )
+    whole = gather_all(sizes, shards, 0)
+    devices = whole[0].shape[0]
+    small_all = whole[0]
+    decay_down = small_all[:, :, 0:16].reshape(-1, 16)
+    gain_one = small_all[:, :, 16].reshape(-1)
+    gain_two = small_all[:, :, 17].reshape(-1)
+    decay_up = small_all[:, :kd_here, 18:34].reshape(-1, 16).T
+    bias_full = small_all[:, :kd_here, 34].reshape(-1)
+    norm_head = small_all[:, :vd_here, 35].reshape(-1)
+    (proj_query, proj_key, proj_value, proj_gate, proj_output, feed_gate, feed_up, feed_down) = (
+        w.reshape(-1, w.shape[-1]) for w in whole[1:]
+    )
     seqs_here, tokens_here, width = inputs.shape
     rows = seqs_here * tokens_here
     key_scale = KEY_DIM ** (-0.5)
@@ -211,13 +470,7 @@
         value_full,
         precision=highest,
     )
-    start_state = entering(
-        (decay_total, local_state),
-        "seq",
-        chain_combine,
-        (jnp.ones_like(decay_total), jnp.zeros_like(local_state)),
-        False,
-    )[1]
+    start_state = entering((decay_total, local_state), "seq", False)
     group_pieces = (
         split_groups(query_scaled),
         split_groups(key_full),
@@ -273,13 +526,7 @@
     local_grad = jnp.einsum(
         "sthc,sthv->shcv", query_scaled * jnp.exp(cumulative_dev), mixed_grad, precision=highest
     )
-    end_grad = entering(
-        (decay_total, local_grad),
-        "seq",
-        grad_combine,
-        (jnp.ones_like(decay_total), jnp.zeros_like(local_grad)),
-        True,
-    )[1]
+    end_grad = entering((decay_total, local_grad), "seq", True)
     back_pieces = group_pieces + (split_groups(mixed_grad), group_starts)
     begin_grad, (query_groups, key_groups, value_groups, log_groups) = lax.scan(
         group_backward, end_grad, back_pieces, reverse=True
@@ -317,21 +564,51 @@
         + mixer_scale * scaled_one
         - hidden_in * mixer_scale**3 * jnp.mean(scaled_one * hidden_in, axis=-1, keepdims=True)
     )
+    small_grad = small_pack(
+        (
+            grad_decay_down.reshape(devices, rows_of, -1),
+            grad_mixer_gain.reshape(devices, rows_of),
+            grad_feed_gain.reshape(devices, rows_of),
+            grad_decay_up.T.reshape(devices, kd_here, -1),
+            grad_decay_bias.reshape(devices, kd_here),
+            grad_head_gain.reshape(devices, vd_here),
+        ),
+        rows_of,
+    ).reshape(devices * rows_of, LANES)
+    bf = jnp.bfloat16
+    summed = scatter_all(
+        sizes,
+        (
+            grad_down.astype(bf),
+            grad_gate.astype(bf),
+            grad_up.astype(bf),
+            grad_output.astype(bf),
+            grad_query.astype(bf),
+            grad_key.astype(bf),
+            grad_value.astype(bf),
+            grad_outgate.astype(bf),
+            small_grad,
+        ),
+        1,
+    )
+    sum_down, sum_gate, sum_up, sum_output, sum_query, sum_key, sum_value, sum_outgate, mine = (
+        summed
+    )
     summed = (
-        lax.psum_scatter(grad_mixer_gain, ("seq", "batch"), scatter_dimension=0, tiled=True),
-        lax.psum_scatter(grad_feed_gain, ("seq", "batch"), scatter_dimension=0, tiled=True),
-        lax.psum_scatter(grad_query, ("seq", "batch"), scatter_dimension=0, tiled=True),
-        lax.psum_scatter(grad_key, ("seq", "batch"), scatter_dimension=0, tiled=True),
-        lax.psum_scatter(grad_value, ("seq", "batch"), scatter_dimension=0, tiled=True),
-        lax.psum_scatter(grad_outgate, ("seq", "batch"), scatter_dimension=0, tiled=True),
-        lax.psum_scatter(grad_decay_down, ("seq", "batch"), scatter_dimension=0, tiled=True),
-        lax.psum_scatter(grad_decay_up, ("seq", "batch"), scatter_dimension=1, tiled=True),
-        lax.psum_scatter(grad_decay_bias, ("seq", "batch"), scatter_dimension=0, tiled=True),
-        lax.psum_scatter(grad_head_gain, ("seq", "batch"), scatter_dimension=0, tiled=True),
-        lax.psum_scatter(grad_output, ("seq", "batch"), scatter_dimension=0, tiled=True),
-        lax.psum_scatter(grad_gate, ("seq", "batch"), scatter_dimension=0, tiled=True),
-        lax.psum_scatter(grad_up, ("seq", "batch"), scatter_dimension=0, tiled=True),
-        lax.psum_scatter(grad_down, ("seq", "batch"), scatter_dimension=0, tiled=True),
+        mine[:, 16],
+        mine[:, 17],
+        sum_query,
+        sum_key,
+        sum_value,
+        sum_outgate,
+        mine[:, 0:16],
+        mine[:kd_here, 18:34].T,
+        mine[:kd_here, 34],
+        mine[:vd_here, 35],
+        sum_output,
+        sum_gate,
+        sum_up,
+        sum_down,
     )
     return (result.reshape(inputs.shape), input_grad.reshape(inputs.shape)) + tuple(summed)
 
@@ -356,7 +633,7 @@
         P(("seq", "batch"), None),
     )
     return jax.shard_map(
-        local,
+        functools.partial(local, grid_of(mesh.shape)),
         mesh=mesh,
         in_specs=placed,
         out_specs=(

time: 2230 us -> 574 us (0.26)
  waiting for transfers between devices: 1750 us -> 30.1 us
  Pallas kernels: 0 us -> 280 us
  blocking collectives: 186 us -> 0 us
  matrix products: 152 us -> 107 us
  starting transfers between devices: 0.97 us -> 33.5 us
  other arithmetic: 62.2 us -> 39.4 us
    reduce_scatter x8 -> x0, waiting for transfers between devices: 1160 us -> none  [the longest x1 157 us: local(): lax.psum_scatter(grad_up, ('seq', 'batch'), scatter_dimension=0, tiled=True)]
    all_gather x10 -> x0, waiting for transfers between devices: 405 us -> none  [the longest x2 101 us: entering(): everything = jax.tree.map(lambda part: lax.all_gather(part, axis), value)]
    pallas_call x0 -> x2, Pallas kernels: none -> 280 us  [the longest x1 142 us: scatter_all(): pl.pallas_call(functools.partial(scatter_kernel, sizes, count), out_shape...]
    unnamed x22 -> x0, waiting for transfers between devices: 176 us -> none
    all_gather x3 -> x0, blocking collectives: 105 us -> none  [the longest x1 40.8 us: local(): lax.all_gather(w_decay_down, ('seq', 'batch'), axis=0, tiled=True)]
    unnamed x2 -> x0, blocking collectives: 81.2 us -> none
    ppermute x0 -> x10, starting transfers between devices: none -> 33.5 us  [the longest x6 21.7 us: shifted(): moved_state = lax.ppermute(state.astype(jnp.bfloat16), axis, pairs)]
    ppermute x0 -> x10, waiting for transfers between devices: none -> 30.1 us  [the longest x6 30.1 us: shifted(): moved_state = lax.ppermute(state.astype(jnp.bfloat16), axis, pairs)]
  transfers between devices with their start and end apart: 20 -> 10, of which waited for: 18 -> 5; matrix products, arithmetic and copies ran while one was open for 6% -> 5% of each run, Pallas kernels for 0% -> 0%
where the time goes in v1:
time: 574 us; the launch traced here: 564 us
  Pallas kernels  280 us (49%)
  matrix products  107 us (19%)
  local copies, waits for them, and re-layouts  70.6 us (12%)
  other arithmetic  39.4 us (7%)
  starting transfers between devices  33.5 us (6%)
  waiting for transfers between devices  30.1 us (5%)
    pallas_call x1, Pallas kernels, scatter_all(): pl.pallas_call(functools.partial(scatter_kernel, sizes, count), out_shape...  142 us
    pallas_call x1, Pallas kernels, gather_all(): pl.pallas_call(functools.partial(gather_kernel, sizes, count), out_shape=...  139 us
    ppermute x6, waiting for transfers between devices, shifted(): moved_state = lax.ppermute(state.astype(jnp.bfloat16), axis, pairs)  30.1 us
    dot_general x10, matrix products, contract_rows(): lax.dot_general(left, right, (((0,), (0,)), ((), ())), preferred_element_...  23.4 us
    ppermute x6, starting transfers between devices, shifted(): moved_state = lax.ppermute(state.astype(jnp.bfloat16), axis, pairs)  21.7 us
    dot_general x10, matrix products, times_transpose(): lax.dot_general(left, right, (((1,), (1,)), ((), ())), preferred_element_...  20.4 us
    unnamed x153, local copies, waits for them, and re-layouts  18.1 us
    dot_general x10, matrix products, matmul(): return jnp.dot(left, right, preferred_element_type=jnp.float32)  15.7 us
  transfers between devices with their start and end apart: 10, of which 5 were waited for; matrix products, arithmetic and copies ran while one was open for 5% of the time, Pallas kernels for 0%

profile of v1, /device:TPU:0, one launch (start us, length us, event | category | flops | bytes accessed | tf_op | source)
XLA Modules:
  0.0 564.3 jit_solution(9896882860169641115)
XLA Ops:
  6.0 138.6 %shard_map.279 = (bf16[4,2,2,2,32,128]{5,4,3,2,1,0:T(8,128)(2,1)}, bf16[4,2,2,2,32,512]{5,4,3,2,1,0:T(8,128)(2,1)}, bf16[4,2,2,2,32,512]{5,4,3,2,1,0:T(8,128)(2,...) custom-call(bf16[32,128]{1,0:T(8,128)(2,1)} %pad.35.refs_0_, ...), custom_call_target="tpu_custom_call" | custom-call | tf_op jit(solution)/shard_map/pallas_call | solution.py:132
  152.7 7.2 %collective-permute-start = (f32[1,4,128]{2,1,0:T(4,128)S(1)}, f32[1,4,128]{2,1,0:T(4,128)S(1)}, u32[]{:S(2)}, u32[]{:S(2)}) collective-permute-start(f32[1,4,128]{2,1,0:T(4,128)S(1)} %bitcast.723), channel_id=1, source_target_pairs={{0,4},{4,8},{8,12},{12,16},{16,20},{20,24},{24,28},{1,5},{5,9},{9,... | collective-permute-start | bytes 6152 | tf_op jit(solution)/shard_map/ppermute | solution.py:287
  165.5 6.4 %collective-permute-start.2 = (bf16[1,4,128,256]{3,2,1,0:T(8,128)(2,1)S(1)}, bf16[1,4,128,256]{3,2,1,0:T(8,128)(2,1)S(1)}, u32[]{:S(2)}, u32[]{:S(2)}) collective-permute-start(bf16[1,4,128,256]{3,2,1,0:T(8,128)(2,1)S(1)} %convert_bitcast_fusion.2), channel_id=1, source_target_pairs={{0,4},{4,8},{8,12},{12,16},{16,20},{20,24},{24,28},{1,5},{5,9},{9,... | collective-permute-start | bytes 786440 | tf_op jit(solution)/shard_map/ppermute | solution.py:286
  173.3 2.5 fusion.100
  178.6 7.1 %collective-permute-start.3 = (bf16[1,4,128,256]{3,2,1,0:T(8,128)(2,1)}, bf16[1,4,128,256]{3,2,1,0:T(8,128)(2,1)}, u32[]{:S(2)}, u32[]{:S(2)}) collective-permute-start(bf16[1,4,128,256]{3,2,1,0:T(8,128)(2,1)} %fusion.159), channel_id=1, source_target_pairs={{0,8},{4,12},{8,16},{12,20},{16,24},{20,28},{1,9},{5,13},{9,17},{1... | collective-permute-start | bytes 786440 | tf_op jit(solution)/shard_map/ppermute | solution.py:286
  200.2 4.2 collective-permute-start.4
  204.5 4.3 collective-permute-done.4
  209.9 19.7 %while.38 = (s32[]{:T(128)}, f32[1,4,128,256]{3,2,1,0:T(8,128)S(1)}, f32[4,1,64,4,256]{4,2,3,1,0:T(8,128)S(1)}, f32[4,1,4,128,256]{4,3,2,1,0:T(8,128)}, f32[4,1,...) while((s32[]{:T(128)}, ...), condition=%wide.region_5.6_spmd.clone, body=%wide.region_3.5_spmd.sunk.clone | while | flops 279470080 | bytes 5886045 | solution.py:480
  243.8 4.5 multiply_convert_fusion
  250.1 2.8 multiply_reduce_fusion.1
  252.9 2.7 reshape.998
  258.8 3.8 multiply_convert_fusion.3
  264.7 4.2 convolution_convert_fusion
  268.9 4.2 convolution_convert_fusion.1
  273.0 4.3 fusion.197
  277.3 2.6 fusion.98
  279.9 2.7 reshape.997
  282.6 3.1 multiply_reduce_fusion
  285.8 3.8 fusion.117
  292.4 3.5 fusion.204
  299.9 11.1 %collective-permute-done.8 = bf16[1,4,128,256]{3,2,1,0:T(8,128)(2,1)S(1)} collective-permute-done((bf16[1,4,128,256]{3,2,1,0:T(8,128)(2,1)S(1)}, bf16[1,4,128,256]{3,2,1,0:T(8,128)(2,1)S(1)}, u32[]{:S(2)}, u32[]{:S(2)}) %collective-permute-start.8) | collective-permute-done | bytes 262176 | tf_op jit(solution)/shard_map/ppermute | solution.py:286
  314.6 10.6 %collective-permute-done.9 = bf16[1,4,128,256]{3,2,1,0:T(8,128)(2,1)S(1)} collective-permute-done((bf16[1,4,128,256]{3,2,1,0:T(8,128)(2,1)S(1)}, bf16[1,4,128,256]{3,2,1,0:T(8,128)(2,1)S(1)}, u32[]{:S(2)}, u32[]{:S(2)}) %collective-permute-start.9) | collective-permute-done | bytes 262176 | tf_op jit(solution)/shard_map/ppermute | solution.py:286
  327.2 63.0 %while.39 = (s32[]{:T(128)}, f32[1,4,128,256]{3,2,1,0:T(8,128)S(1)}, f32[4,1,64,4,128]{4,2,3,1,0:T(8,128)}, bf16[4,1,64,4,128]{4,2,3,1,0:T(8,128)(2,1)}, bf16[4,...) while((s32[]{:T(128)}, ...), condition=%wide.region_13.14_spmd.clone, body=%wide.region_10.13_spmd.sunk.clone | while | flops 708263424 | bytes 18597172 | solution.py:531
  408.3 141.8 %shard_map.280 = (f32[88,1024]{1,0:T(8,128)}, f32[32,2816]{1,0:T(8,128)}, f32[32,2816]{1,0:T(8,128)}, f32[32,1024]{1,0:T(8,128)}, f32[32,512]{1,0:T(8,128)}, /*i...) custom-call(bf16[4,2,2,2,88,1024]{5,4,3,2,1,0:T(8,128)(2,1)} %bitcast.661, ...), custom_call_target="tpu_custom_call" | custom-call | tf_op jit(solution)/shard_map/pallas_call | solution.py:255
  (445 shorter events, 185.6 us)
Async XLA Ops:
  0.6 148.3 %copy-start.2 = (bf16[1,256,1024]{2,1,0:T(8,128)(2,1)S(1)}, bf16[1,256,1024]{2,1,0:T(8,128)(2,1)}, u32[]{:S(2)}) copy-start(bf16[1,256,1024]{2,1,0:T(8,128)(2,1)} %param.20) | copy-start | bytes 1572868
  152.0 9.2 %copy-start.47 = (bf16[4,2,2,2,32,512]{5,4,3,2,1,0:T(8,128)(2,1)S(1)}, bf16[4,2,2,2,32,512]{5,4,3,2,1,0:T(8,128)(2,1)}, u32[]{:S(2)}) copy-start(bf16[4,2,2,2,32,512]{5,4,3,2,1,0:T(8,128)(2,1)} %get-tuple-element.317) | copy-start | bytes 3145732
  152.7 12.1 %copy-start.18 = (f32[1,128,4,256]{1,3,2,0:T(8,128)}, f32[1,128,4,256]{1,3,2,0:T(8,128)S(1)}, u32[]{:S(2)}) copy-start(f32[1,128,4,256]{1,3,2,0:T(8,128)S(1)} %bitcast_add_fusion.1) | copy-start | bytes 1572868
  152.7 42.9 %collective-permute-start = (f32[1,4,128]{2,1,0:T(4,128)S(1)}, f32[1,4,128]{2,1,0:T(4,128)S(1)}, u32[]{:S(2)}, u32[]{:S(2)}) collective-permute-start(f32[1,4,128]{2,1,0:T(4,128)S(1)} %bitcast.723), channel_id=1, source_target_pairs={{0,4},{4,8},{8,12},{12,16},{16,20},{20,24},{24,28},{1,5},{5,9},{9,... | collective-permute-start | bytes 6152 | tf_op jit(solution)/shard_map/ppermute | solution.py:287
  159.8 35.8 %collective-permute-start.5 = (f32[1,4,128]{2,1,0:T(4,128)S(1)}, f32[1,4,128]{2,1,0:T(4,128)S(1)}, u32[]{:S(2)}, u32[]{:S(2)}) collective-permute-start(f32[1,4,128]{2,1,0:T(4,128)S(1)} %bitcast.724), channel_id=1, source_target_pairs={{4,0},{8,4},{12,8},{16,12},{20,16},{24,20},{28,24},{5,1},{9,5},{13... | collective-permute-start | bytes 6152 | tf_op jit(solution)/shard_map/ppermute | solution.py:287
  165.5 12.3 %collective-permute-start.2 = (bf16[1,4,128,256]{3,2,1,0:T(8,128)(2,1)S(1)}, bf16[1,4,128,256]{3,2,1,0:T(8,128)(2,1)S(1)}, u32[]{:S(2)}, u32[]{:S(2)}) collective-permute-start(bf16[1,4,128,256]{3,2,1,0:T(8,128)(2,1)S(1)} %convert_bitcast_fusion.2), channel_id=1, source_target_pairs={{0,4},{4,8},{8,12},{12,16},{16,20},{20,24},{24,28},{1,5},{5,9},{9,... | collective-permute-start | bytes 786440 | tf_op jit(solution)/shard_map/ppermute | solution.py:286
  172.0 14.5 %copy-start.31 = (f32[256,512]{1,0:T(8,128)S(1)}, f32[256,512]{1,0:T(8,128)}, u32[]{:S(2)}) copy-start(f32[256,512]{1,0:T(8,128)} %copy-done.30) | copy-start | bytes 1572868
  175.8 13.2 %copy-start.33 = (f32[256,512]{1,0:T(8,128)S(1)}, f32[256,512]{1,0:T(8,128)}, u32[]{:S(2)}) copy-start(f32[256,512]{1,0:T(8,128)} %copy-done.32) | copy-start | bytes 1572868
  178.6 20.4 %collective-permute-start.3 = (bf16[1,4,128,256]{3,2,1,0:T(8,128)(2,1)}, bf16[1,4,128,256]{3,2,1,0:T(8,128)(2,1)}, u32[]{:S(2)}, u32[]{:S(2)}) collective-permute-start(bf16[1,4,128,256]{3,2,1,0:T(8,128)(2,1)} %fusion.159), channel_id=1, source_target_pairs={{0,8},{4,12},{8,16},{12,20},{16,24},{20,28},{1,9},{5,13},{9,17},{1... | collective-permute-start | bytes 786440 | tf_op jit(solution)/shard_map/ppermute | solution.py:286
  195.6 8.8 %collective-permute-start.1 = (f32[1,4,128]{2,1,0:T(4,128)S(1)}, f32[1,4,128]{2,1,0:T(4,128)S(1)}, u32[]{:S(2)}, u32[]{:S(2)}) collective-permute-start(f32[1,4,128]{2,1,0:T(4,128)S(1)} %get-tuple-element.529), channel_id=1, source_target_pairs={{0,8},{4,12},{8,16},{12,20},{16,24},{20,28},{1,9},{5,13},{9,17},{1... | collective-permute-start | bytes 6152 | tf_op jit(solution)/shard_map/ppermute | solution.py:287
  197.7 6.7 %collective-permute-start.6 = (f32[1,4,128]{2,1,0:T(4,128)S(1)}, f32[1,4,128]{2,1,0:T(4,128)S(1)}, u32[]{:S(2)}, u32[]{:S(2)}) collective-permute-start(f32[1,4,128]{2,1,0:T(4,128)S(1)} %get-tuple-element.528), channel_id=1, source_target_pairs={{8,0},{12,4},{16,8},{20,12},{24,16},{28,20},{9,1},{13,5},{17,9},{2... | collective-permute-start | bytes 6152 | tf_op jit(solution)/shard_map/ppermute | solution.py:287
  200.2 8.5 %collective-permute-start.4 = (bf16[1,4,128,256]{3,2,1,0:T(8,128)(2,1)S(1)}, bf16[1,4,128,256]{3,2,1,0:T(8,128)(2,1)S(1)}, u32[]{:S(2)}, u32[]{:S(2)}) collective-permute-start(bf16[1,4,128,256]{3,2,1,0:T(8,128)(2,1)S(1)} %fusion.132), channel_id=1, source_target_pairs={{0,16},{4,20},{8,24},{12,28},{1,17},{5,21},{9,25},{13,29},{2,18},{... | collective-permute-start | bytes 786440 | tf_op jit(solution)/shard_map/ppermute | solution.py:286
  229.6 53.0 %copy-start = (f32[4,1,64,4,256]{4,2,3,1,0:T(8,128)}, f32[4,1,64,4,256]{4,2,3,1,0:T(8,128)S(1)}, u32[]{:S(2)}) copy-start(f32[4,1,64,4,256]{4,2,3,1,0:T(8,128)S(1)} %get-tuple-element.320) | copy-start | bytes 3145732
  238.6 11.5 %copy-start.6 = (f32[256,1024]{1,0:T(8,128)}, f32[256,1024]{1,0:T(8,128)S(1)}, u32[]{:S(2)}) copy-start(f32[256,1024]{1,0:T(8,128)S(1)} %get-tuple-element.539) | copy-start | bytes 3145732
  268.9 8.4 %slice-start.2 = ((s8[5767168]{0:T(1024)(128)(4,1)}), s8[4194304]{0:T(1024)(128)(4,1)S(1)}, s32[]{:S(2)}) async-start(s8[5767168]{0:T(1024)(128)(4,1)} %bitcast.735), calls=%async_computation.2 | async-start | bytes 8388608
  289.7 8.3 %collective-permute-start.7 = (bf16[1,4,128,256]{3,2,1,0:T(8,128)(2,1)S(1)}, bf16[1,4,128,256]{3,2,1,0:T(8,128)(2,1)S(1)}, u32[]{:S(2)}, u32[]{:S(2)}) collective-permute-start(bf16[1,4,128,256]{3,2,1,0:T(8,128)(2,1)S(1)} %convert_bitcast_fusion.1), channel_id=1, source_target_pairs={{4,0},{8,4},{12,8},{16,12},{20,16},{24,20},{28,24},{5,1},{9,5},{13... | collective-permute-start | bytes 786440 | tf_op jit(solution)/shard_map/ppermute | solution.py:286
  298.1 12.9 %collective-permute-start.8 = (bf16[1,4,128,256]{3,2,1,0:T(8,128)(2,1)S(1)}, bf16[1,4,128,256]{3,2,1,0:T(8,128)(2,1)S(1)}, u32[]{:S(2)}, u32[]{:S(2)}) collective-permute-start(bf16[1,4,128,256]{3,2,1,0:T(8,128)(2,1)S(1)} %fusion.158), channel_id=1, source_target_pairs={{8,0},{12,4},{16,8},{20,12},{24,16},{28,20},{9,1},{13,5},{17,9},{2... | collective-permute-start | bytes 786440 | tf_op jit(solution)/shard_map/ppermute | solution.py:286
  299.4 13.1 %copy-start.29 = (bf16[256,1024]{1,0:T(8,128)(2,1)S(1)}, bf16[256,1024]{1,0:T(8,128)(2,1)}, u32[]{:S(2)}) copy-start(bf16[256,1024]{1,0:T(8,128)(2,1)} %get-tuple-element.541) | copy-start | bytes 1572868
  311.2 14.0 %collective-permute-start.9 = (bf16[1,4,128,256]{3,2,1,0:T(8,128)(2,1)S(1)}, bf16[1,4,128,256]{3,2,1,0:T(8,128)(2,1)S(1)}, u32[]{:S(2)}, u32[]{:S(2)}) collective-permute-start(bf16[1,4,128,256]{3,2,1,0:T(8,128)(2,1)S(1)} %fusion.136), channel_id=1, source_target_pairs={{16,0},{20,4},{24,8},{28,12},{17,1},{21,5},{25,9},{29,13},{18,2},{... | collective-permute-start | bytes 786440 | tf_op jit(solution)/shard_map/ppermute | solution.py:286
  408.3 149.0 %copy-start.5 = (f32[256,1024]{1,0:T(8,128)S(1)}, f32[256,1024]{1,0:T(8,128)}, u32[]{:S(2)}) copy-start(f32[256,1024]{1,0:T(8,128)} %copy-done.4) | copy-start | bytes 3145732
  408.3 149.0 %copy-start.61 = (f32[256]{0:T(256)S(1)}, f32[256]{0:T(256)}, u32[]{:S(2)}) copy-start(f32[256]{0:T(256)} %get-tuple-element.530) | copy-start | bytes 3076
  550.1 8.5 %copy-start.59 = (f32[32,512]{1,0:T(8,128)S(1)}, f32[32,512]{1,0:T(8,128)}, u32[]{:S(2)}) copy-start(f32[32,512]{1,0:T(8,128)} %get-tuple-element.843) | copy-start | bytes 196612
  550.1 9.1 %copy-start.58 = (f32[32,512]{1,0:T(8,128)S(1)}, f32[32,512]{1,0:T(8,128)}, u32[]{:S(2)}) copy-start(f32[32,512]{1,0:T(8,128)} %get-tuple-element.844) | copy-start | bytes 196612
  550.2 9.7 %copy-start.55 = (f32[32,1024]{1,0:T(8,128)S(1)}, f32[32,1024]{1,0:T(8,128)}, u32[]{:S(2)}) copy-start(f32[32,1024]{1,0:T(8,128)} %get-tuple-element.845) | copy-start | bytes 393220
  (71 other events, 224.3 us)

commit v2 on v0

v2 whole, which is shorter than its diff:
```python
import functools

import jax
import jax.numpy as jnp
from jax import lax
from jax.experimental import pallas as pl
from jax.experimental.pallas import tpu as pltpu
from jax.sharding import PartitionSpec as P

HEADS = 4
KEY_DIM = 128
VALUE_DIM = 256
GROUP = 64
LANES = 128
RANK = 16
VECTORS = 32
MESH = pl.DeviceIdType.MESH
VMEM_LIMIT = 63 * 2**20

epsilon = 1e-06
key_scale = KEY_DIM ** (-0.5)
highest = lax.Precision.HIGHEST
high = lax.Precision.HIGH
f32 = jnp.float32
bf16 = jnp.bfloat16


def grid_of(shape):
    seq, batch = shape["seq"], shape["batch"]
    outer = 4 if seq % 4 == 0 else seq
    core = 2 if batch % 2 == 0 else 1
    return (outer, seq // outer, batch // core, core)


def coords_of(sizes):
    seq, batch = lax.axis_index("seq"), lax.axis_index("batch")
    return (seq // sizes[1], seq % sizes[1], batch // sizes[3], batch % sizes[3])


def device_of(sizes, at):
    return {"seq": at[0] * sizes[1] + at[1], "batch": at[2] * sizes[3] + at[3]}


def moved(sizes, at, axis, by):
    new = list(at)
    new[axis] = lax.rem(at[axis] + (by % sizes[axis]), sizes[axis])
    return tuple(new)


def region(ref, free, at):
    return ref.at[tuple(slice(None) if k in free else at[k] for k in range(4))]


def orders_of(sizes):
    if sizes[1] == sizes[2] and sizes[3] == 2:
        return ((0, 1, 2, 3), (0, 2, 1, 3))
    return ((0, 1, 2, 3),)


def hops_of(sizes):
    length, hops = sizes[0] * sizes[1], []
    while 2 ** len(hops) < length:
        hops.append(2 ** len(hops))
    return hops


def greet(sizes, at):
    barrier = pltpu.get_barrier_semaphore()
    length = sizes[0] * sizes[1]
    seq, batch = lax.axis_index("seq"), lax.axis_index("batch")
    targets = [
        device_of(sizes, moved(sizes, at, axis, by))
        for axis in range(4)
        for by in range(1, sizes[axis])
    ]
    for hop in hops_of(sizes):
        for by in (hop, length - hop):
            targets.append({"seq": lax.rem(seq + by, length), "batch": batch})
    for target in targets:
        pl.semaphore_signal(barrier, inc=1, device_id=target, device_id_type=MESH)
    pl.semaphore_wait(barrier, len(targets))


def by_order(sizes, at, act):
    orders = orders_of(sizes)
    if len(orders) == 1:
        act(orders[0])
        return
    for parity, order in enumerate(orders):
        pl.when(at[3] == parity)(functools.partial(act, order))


def loop(count, body):
    def step(k, carry):
        body(k)
        return carry

    lax.fori_loop(0, count, step, 0)


def dot(left, right, dims, precision=None):
    return lax.dot_general(
        left, right, (dims, ((), ())), precision=precision, preferred_element_type=f32
    )


NN = ((1,), (0,))
NT = ((1,), (1,))
TN = ((0,), (0,))


class Gather:
    def __init__(self, sizes, at, shards, wholes, send_sem, recv_sem, own_sem):
        self.sizes, self.at = sizes, at
        self.shards, self.wholes = shards, wholes
        self.send_sem, self.recv_sem, self.own_sem = send_sem, recv_sem, own_sem
        self.count = len(shards)
        self.todo = []
        for tick in range(self.count + 3):
            for step in (1, 2, 3, 4):
                item = tick - step + 1
                if 0 <= item < self.count:
                    self.todo.append((item, step))

    def copies(self, item, order, step, arriving):
        axis, free = order[step], order[:step]
        made = []
        for by in range(1, self.sizes[axis]):
            source = moved(self.sizes, self.at, axis, -by) if arriving else self.at
            place = region(self.wholes[item], free, source)
            made.append(
                pltpu.make_async_remote_copy(
                    src_ref=self.shards[item] if step == 0 and not arriving else place,
                    dst_ref=place,
                    send_sem=self.send_sem.at[item, step, by - 1],
                    recv_sem=self.recv_sem.at[item, step, by - 1],
                    device_id=device_of(self.sizes, moved(self.sizes, self.at, axis, by)),
                    device_id_type=MESH,
                )
            )
        return made

    def own(self, item):
        return pltpu.make_async_copy(
            self.shards[item], region(self.wholes[item], (), self.at), self.own_sem.at[item]
        )

    def begin(self):
        for item in range(self.count):
            for copy in self.copies(item, orders_of(self.sizes)[0], 0, False):
                copy.start()
            self.own(item).start()

    def advance(self, item, step):
        if step == 1:
            self.own(item).wait()

        def act(order):
            for copy in self.copies(item, order, step - 1, True):
                copy.wait_recv()
            if step < 4:
                for copy in self.copies(item, order, step, False):
                    copy.start()

        by_order(self.sizes, self.at, act)

    def pump(self, steps):
        for _ in range(min(steps, len(self.todo))):
            self.advance(*self.todo.pop(0))

    def need(self, item):
        while (item, 4) in self.todo:
            self.pump(1)

    def finish(self):
        self.pump(len(self.todo))

        def act(order):
            for item in range(self.count):
                for step in range(4):
                    for copy in self.copies(item, order, step, False):
                        copy.wait_send()

        by_order(self.sizes, self.at, act)


class Scan:
    def __init__(self, sizes, reverse, total, state, before_total, before_state, buffers, sems):
        self.sizes, self.reverse = sizes, reverse
        self.total, self.state = total, state
        self.before_total, self.before_state = before_total, before_state
        self.total_out, self.total_in, self.state_out, self.state_in = buffers
        self.sems = sems
        self.hops = hops_of(sizes)
        self.length = sizes[0] * sizes[1]
        self.place = self.length - 1 - lax.axis_index("seq") if reverse else lax.axis_index("seq")

    def copies(self, k):
        seq = lax.axis_index("seq")
        hop = self.length - self.hops[k] if self.reverse else self.hops[k]
        target = {"seq": lax.rem(seq + hop, self.length), "batch": lax.axis_index("batch")}
        pairs = ((self.total_out, self.total_in), (self.state_out, self.state_in))
        return [
            pltpu.make_async_remote_copy(
                src_ref=out.at[k],
                dst_ref=come.at[k],
                send_sem=self.sems.at[0, k, n],
                recv_sem=self.sems.at[1, k, n],
                device_id=target,
                device_id_type=MESH,
            )
            for n, (out, come) in enumerate(pairs)
        ]

    def send(self, k):
        if k == 0:
            self.before_total[...] = jnp.ones_like(self.before_total)
            self.before_state[...] = jnp.zeros_like(self.before_state)
        self.total_out[k] = self.total[...]
        for h in range(HEADS):
            self.state_out[k, h] = self.state[h].astype(bf16)

        @pl.when(self.place + self.hops[k] < self.length)
        def _():
            for copy in self.copies(k):
                copy.start()

    def receive(self, k):
        @pl.when(self.place >= self.hops[k])
        def _():
            for copy in self.copies(k):
                copy.wait_recv()
            come = self.total_in[k]
            for h in range(HEADS):
                keys = slice(h * KEY_DIM, (h + 1) * KEY_DIM)
                state = self.state_in[k, h].astype(f32)
                self.before_state[h] = (
                    self.before_state[h] + self.before_total[0:1, keys] * state
                )
                if k + 1 < len(self.hops):
                    self.state[h] = self.state[h] + self.total[0:1, keys] * state
            self.before_total[...] = self.before_total[...] * come
            if k + 1 < len(self.hops):
                self.total[...] = self.total[...] * come

    def finish(self):
        for k in range(len(self.hops)):

            @pl.when(self.place + self.hops[k] < self.length)
            def _(k=k):
                for copy in self.copies(k):
                    copy.wait_send()


def scan_scratch(sizes):
    hops = len(hops_of(sizes))
    keys = HEADS * KEY_DIM
    return [
        pltpu.VMEM((8, keys), f32),
        pltpu.VMEM((HEADS, VALUE_DIM, KEY_DIM), f32),
        pltpu.VMEM((8, keys), f32),
        pltpu.VMEM((HEADS, VALUE_DIM, KEY_DIM), f32),
        pltpu.VMEM((hops, 8, keys), f32),
        pltpu.VMEM((hops, 8, keys), f32),
        pltpu.VMEM((hops, HEADS, VALUE_DIM, KEY_DIM), bf16),
        pltpu.VMEM((hops, HEADS, VALUE_DIM, KEY_DIM), bf16),
        pltpu.SemaphoreType.DMA((2, hops, 2)),
    ]


def lower_mask():
    rows = lax.broadcasted_iota(jnp.int32, (GROUP, GROUP), 0)
    columns = lax.broadcasted_iota(jnp.int32, (GROUP, GROUP), 1)
    return jnp.where(rows >= columns, 1.0, 0.0).astype(f32)


def log_decay_of(decay_pre):
    return jax.nn.log_sigmoid(decay_pre) * (1.0 / 16.0)


def spread(block, offset, per, width):
    devices = width // per
    lane = lax.broadcasted_iota(jnp.int32, (LANES, width), 0)
    column = lax.broadcasted_iota(jnp.int32, (LANES, width), 1)
    pick = jnp.where(lane == offset + column % per, 1.0, 0.0).astype(bf16)
    wide = dot(block.astype(bf16), pick, NN)
    rows = block.shape[0] // devices
    wide = wide.reshape(devices, rows, width)
    device = lax.broadcasted_iota(jnp.int32, wide.shape, 0)
    column = lax.broadcasted_iota(jnp.int32, wide.shape, 2)
    return jnp.sum(jnp.where(device == column // per, wide, 0.0), axis=0)


def forward_kernel(sizes, count, *refs):
    shards, tokens = refs[:count], refs[count]
    refs = refs[count + 1 :]
    far = list(refs[: count - 1])
    refs = refs[count - 1 :]
    (vectors, decay_up, normed, query, key, value, gate_pre, rank_act, decay_pre) = refs[:9]
    (starts, mixed, gated) = refs[9:12]
    refs = refs[12:]
    near = list(refs[:6])
    (query_dev, offsets) = refs[6:8]
    (total, state, before_total, before_state) = refs[8:12]
    scan_buffers, scan_sems = refs[12:16], refs[16]
    send_sem, recv_sem, own_sem, out_sem = refs[17:21]

    at = coords_of(sizes)
    devices = sizes[0] * sizes[1] * sizes[2] * sizes[3]
    width = tokens.shape[1]
    keys, values = HEADS * KEY_DIM, HEADS * VALUE_DIM
    count_rows = tokens.shape[0]
    greet(sizes, at)
    gather = Gather(sizes, at, shards, near + far[5:], send_sem, recv_sem, own_sem)
    gather.begin()

    gather.need(0)
    tiny = near[0][...].reshape(devices, RANK, LANES)
    per_feature, per_key, per_value = width // devices, keys // devices, VALUE_DIM // devices
    vectors[...] = jnp.zeros_like(vectors)
    vectors[0:1, :] = spread(tiny[:, 0], VECTORS, per_feature, width)
    vectors[1:2, :] = spread(tiny[:, 1], VECTORS, per_feature, width)
    vectors[2:3, 0:keys] = spread(tiny[:, 2], VECTORS, per_key, keys)
    vectors[3:4, 0:VALUE_DIM] = spread(tiny[:, 3], VECTORS, per_value, VALUE_DIM)
    decay_up[...] = jnp.zeros_like(decay_up)
    decay_up[0:RANK, :] = spread(tiny.reshape(devices * RANK, LANES), 0, per_key, keys).astype(bf16)

    def norm_rows(k):
        rows = pl.ds(pl.multiple_of(k * 32, 32), 32)
        hidden = tokens[rows, :].astype(f32)
        scale = lax.rsqrt(jnp.mean(hidden * hidden, axis=-1, keepdims=True) + epsilon)
        normed[rows, :] = (hidden * scale * vectors[0:1, :]).astype(bf16)

    loop(count_rows // 32, norm_rows)

    def project(item, into):
        gather.need(item)
        weight = near[item]
        size = min(into.shape[1], 256)

        def columns(k):
            here = pl.ds(pl.multiple_of(k * size, size), size)
            panel = weight[..., here].reshape(width, size)
            into[:, here] = dot(normed[...], panel, NN).astype(into.dtype)

        loop(into.shape[1] // size, columns)

    project(1, rank_act)
    decay_pre[...] = dot(rank_act[...], decay_up[...], NN) + vectors[2:3, 0:keys]
    project(2, query)
    project(3, key)
    project(4, value)

    lower = lower_mask()
    total[...] = jnp.zeros_like(total)
    state[...] = jnp.zeros_like(state)

    def group(k):
        rows = pl.ds(pl.multiple_of(k * GROUP, GROUP), GROUP)
        cumulative = dot(lower, log_decay_of(decay_pre[rows, :]), NN, highest)
        middle = cumulative[GROUP // 2 - 1 : GROUP // 2]
        ending = cumulative[GROUP - 1 :]
        query_scaled = query[rows, :].astype(f32) * key_scale
        key_full = key[rows, :].astype(f32)
        gated_query = query_scaled * jnp.exp(cumulative - middle)
        inverse_key = key_full * jnp.exp(middle - cumulative)
        tail_key = key_full * jnp.exp(ending - cumulative)
        state_query = query_scaled * jnp.exp(cumulative)
        offset = total[0:1, :]
        query_dev[rows, :] = state_query * jnp.exp(offset)
        offsets[k] = total[...]
        for h in range(HEADS):
            across = slice(h * KEY_DIM, (h + 1) * KEY_DIM)
            along = slice(h * VALUE_DIM, (h + 1) * VALUE_DIM)
            value_full = value[rows, along].astype(f32)
            scores = dot(gated_query[:, across], inverse_key[:, across], NT, high) * lower
            start = state[h]
            starts[k, h] = start.astype(bf16)
            mixed[rows, along] = dot(state_query[:, across], start, NT, high) + dot(
                scores, value_full, NN, high
            )
            state[h] = jnp.exp(ending[:, across]) * start + dot(
                value_full, tail_key[:, across], TN, high
            )
        total[...] = total[...] + ending

    loop(count_rows // GROUP, group)
    total[...] = jnp.exp(total[...])
    scan = Scan(
        sizes, False, total, state, before_total, before_state, scan_buffers, scan_sems
    )
    for k in range(len(scan.hops)):
        scan.send(k)
        if k == 0:
            project(5, gate_pre)
        else:
            gather.pump(2)
        scan.receive(k)

    def add_start(k):
        factor = jnp.exp(offsets[k])
        for h in range(HEADS):
            across = slice(h * KEY_DIM, (h + 1) * KEY_DIM)
            whole = starts[k, h].astype(f32) + factor[0:1, across] * before_state[h]
            starts[k, h] = whole.astype(bf16)

    loop(count_rows // GROUP, add_start)

    def finish_rows(k):
        rows = pl.ds(pl.multiple_of(k * GROUP, GROUP), GROUP)
        for h in range(HEADS):
            across = slice(h * KEY_DIM, (h + 1) * KEY_DIM)
            along = slice(h * VALUE_DIM, (h + 1) * VALUE_DIM)
            whole = mixed[rows, along] + dot(
                query_dev[rows, across], before_state[h], NT, high
            )
            mixed[rows, along] = whole
            scale = lax.rsqrt(jnp.mean(whole * whole, axis=-1, keepdims=True) + epsilon)
            gate = gate_pre[rows, along]
            swish = gate * jax.nn.sigmoid(gate)
            gated[rows, along] = (whole * scale * vectors[3:4, 0:VALUE_DIM] * swish).astype(bf16)

    loop(count_rows // GROUP, finish_rows)

    out = [pltpu.make_async_copy(near[k + 1], far[k], out_sem.at[k]) for k in range(5)]
    for copy in out:
        copy.start()
    gather.finish()
    scan.finish()
    for copy in out:
        copy.wait()


def forward(sizes, tokens, shards):
    count = len(shards)
    most = max(max(sizes) - 1, 1)
    rows, width = tokens.shape
    keys, values = HEADS * KEY_DIM, HEADS * VALUE_DIM
    groups = rows // GROUP
    whole = [jax.ShapeDtypeStruct(sizes + s.shape, s.dtype) for s in shards]
    shape = jax.ShapeDtypeStruct
    local_outs = [
        shape((8, width), f32),
        shape((LANES, keys), bf16),
        shape((rows, width), bf16),
        shape((rows, keys), bf16),
        shape((rows, keys), bf16),
        shape((rows, values), bf16),
        shape((rows, values), f32),
        shape((rows, LANES), bf16),
        shape((rows, keys), f32),
        shape((groups, HEADS, VALUE_DIM, KEY_DIM), bf16),
        shape((rows, values), f32),
        shape((rows, values), bf16),
    ]
    results = pl.pallas_call(
        functools.partial(forward_kernel, sizes, count),
        out_shape=whole[1:] + local_outs,
        in_specs=[pl.BlockSpec(memory_space=pltpu.VMEM)] * (count + 1),
        out_specs=[pl.BlockSpec(memory_space=pl.ANY)] * (count - 1)
        + [pl.BlockSpec(memory_space=pltpu.VMEM)] * len(local_outs),
        scratch_shapes=[pltpu.VMEM(w.shape, w.dtype) for w in whole[:6]]
        + [pltpu.VMEM((rows, keys), f32), pltpu.VMEM((groups, 8, keys), f32)]
        + scan_scratch(sizes)
        + [
            pltpu.SemaphoreType.DMA((count, 4, most)),
            pltpu.SemaphoreType.DMA((count, 4, most)),
            pltpu.SemaphoreType.DMA((count,)),
            pltpu.SemaphoreType.DMA((5,)),
        ],
        compiler_params=pltpu.CompilerParams(
            collective_id=0, has_side_effects=True, vmem_limit_bytes=VMEM_LIMIT
        ),
    )(*shards, tokens)
    weights = [w.reshape((-1,) + w.shape[5:]) for w in results[: count - 1]]
    return weights, results[count - 1 :]


class Scatter:
    def __init__(self, sizes, at, sources, stages, near, half, part, last, sums, sems):
        self.sizes, self.at = sizes, at
        self.sources, self.stages, self.near = sources, stages, near
        self.landings = (last, part, half)
        self.sums = sums
        self.send_sem, self.recv_sem, self.own_sem = sems
        self.todo = []
        self.begun = []

    def copy(self, item, order, step, by):
        axis, free = order[step], order[:step]
        target = moved(self.sizes, self.at, axis, by)
        if step == 3:
            source, landing = self.sources[item], self.near[item]
        else:
            source, landing = self.near[item], self.landings[step][item].at[by - 1]
        index = tuple(
            slice(None) if k in free else target[k] for k in range(4 if step == 3 else 3)
        )
        return pltpu.make_async_remote_copy(
            src_ref=source.at[index],
            dst_ref=landing,
            send_sem=self.send_sem.at[item, step, by - 1],
            recv_sem=self.recv_sem.at[item, step, by - 1],
            device_id=device_of(self.sizes, target),
            device_id_type=MESH,
        )

    def own(self, item, k):
        slot = k % 2
        return pltpu.make_async_copy(
            self.sources[item].at[k, :, :, self.at[3]],
            self.stages[item].at[slot],
            self.own_sem.at[item, slot],
        )

    def begin(self, items):
        for item in items:
            self.copy(item, orders_of(self.sizes)[0], 3, 1).start()
            self.begun.append(item)
        for tick in range(len(items) + 3):
            for step in (3, 2, 1, 0):
                k = tick - (3 - step)
                if 0 <= k < len(items):
                    self.todo.append((items[k], step))

    def load(self, item):
        if self.stages[item] is not None:
            for k in range(min(2, self.sizes[0])):
                self.own(item, k).start()

    def advance(self, item, step):
        def act(order):
            self.add(item, order, step)
            if step > 0:
                for by in range(1, self.sizes[order[step - 1]]):
                    self.copy(item, order, step - 1, by).start()

        by_order(self.sizes, self.at, act)

    def add(self, item, order, step):
        sizes, at = self.sizes, self.at
        axis, free = order[step], order[:step]
        near = self.near[item]
        for by in range(1, sizes[axis]):
            self.copy(item, order, step, by).wait_recv()
        if step == 0:
            total = near[at[0], at[1], at[2]].astype(f32)
            for by in range(1, sizes[axis]):
                total = total + self.landings[0][item][by - 1].astype(f32)
            self.sums[item][...] = total
            return

        staged = step == 3 and self.stages[item] is not None

        def at_outer(k):
            if staged:
                self.own(item, k).wait()
            for j in range(sizes[free[1]] if len(free) > 1 else 1):
                for i in range(sizes[free[2]] if len(free) > 2 else 1):
                    within = (k, j, i)[: len(free)]
                    place = list(at[:3])
                    for axis_of, index in zip(free, within):
                        place[axis_of] = index
                    place = tuple(place)
                    total = near[place].astype(f32)
                    if step == 3:
                        if staged:
                            mine = self.stages[item][(k % 2,) + place[1:]]
                        else:
                            mine = self.sources[item][place + (at[3],)]
                        total = total + mine.astype(f32)
                    else:
                        for by in range(1, sizes[axis]):
                            come = self.landings[step][item].at[by - 1]
                            total = total + come[within].astype(f32)
                    near[place] = total.astype(near.dtype)
            if staged:

                @pl.when(k + 2 < sizes[0])
                def _():
                    self.own(item, k + 2).start()

        loop(sizes[0], at_outer)

    def pump(self, steps):
        for _ in range(min(steps, len(self.todo))):
            self.advance(*self.todo.pop(0))

    def finish(self):
        self.pump(len(self.todo))

        def act(order):
            for item in self.begun:
                for step in range(4):
                    for by in range(1, self.sizes[order[step]]):
                        self.copy(item, order, step, by).wait_send()

        by_order(self.sizes, self.at, act)


def fold(rows, offset, per):
    count, width = rows.shape
    devices = width // per
    lane = lax.broadcasted_iota(jnp.int32, (LANES, width), 0)
    column = lax.broadcasted_iota(jnp.int32, (LANES, width), 1)
    pick = jnp.where(lane == offset + column % per, 1.0, 0.0).astype(f32)
    shape = (devices, count, width)
    device = lax.broadcasted_iota(jnp.int32, shape, 0)
    column = lax.broadcasted_iota(jnp.int32, shape, 2)
    wide = jnp.where(device == column // per, jnp.broadcast_to(rows[None], shape), 0.0)
    return dot(wide.reshape(devices * count, width), pick, NT, highest).reshape(
        devices, count, LANES
    )


FAR_ITEMS = 4
NEAR_ITEMS = 6


def backward_kernel(sizes, *refs):
    count = FAR_ITEMS + NEAR_ITEMS
    far_grads, far_weights, far_arrays = refs[:4], refs[4:9], refs[9:13]
    (query, key, value, decay_pre, starts, normed, rank_act, decay_up, vectors, side, tokens) = refs[
        13:24
    ]
    refs = refs[24:]
    sums, input_grad = refs[:count], refs[count]
    refs = refs[count + 1 :]
    local, stages = list(refs[:NEAR_ITEMS]), list(refs[NEAR_ITEMS : NEAR_ITEMS + 3])
    refs = refs[NEAR_ITEMS + 3 :]
    near, half, part, last = (refs[k * count : (k + 1) * count] for k in range(4))
    refs = refs[4 * count :]
    weights = refs[:5]
    (wide_a, wide_b, wide_c, outgate_grad) = refs[5:9]
    (cumulative_all, query_dev, query_grad, key_grad, value_grad, decay_grad) = refs[9:15]
    (rank_grad, rows_sum) = refs[15:17]
    (total, state, before_total, before_state) = refs[17:21]
    scan_buffers, scan_sems = refs[21:25], refs[25]
    send_sem, recv_sem, own_sem, load_sem = refs[26:30]

    at = coords_of(sizes)
    devices = sizes[0] * sizes[1] * sizes[2] * sizes[3]
    count_rows, width = tokens.shape
    keys, values = HEADS * KEY_DIM, HEADS * VALUE_DIM
    groups = count_rows // GROUP

    loads = [
        pltpu.make_async_copy(source, target, load_sem.at[k])
        for k, (source, target) in enumerate(
            zip(far_arrays[:3] + far_weights, (wide_a, wide_b, wide_c) + tuple(weights))
        )
    ]
    for copy in loads:
        copy.start()
    greet(sizes, at)
    scatter = Scatter(
        sizes,
        at,
        list(far_grads) + local,
        [stages[0], stages[1], stages[1], stages[2]] + [None] * NEAR_ITEMS,
        near,
        half,
        part,
        last,
        sums,
        (send_sem, recv_sem, own_sem),
    )
    for item in (0, 1, 3):
        scatter.load(item)
    scatter.begin([0, 1, 2, 3])
    for copy in loads[:3]:
        copy.wait()
    gated_grad, mixed, gate_pre = wide_a, wide_b, wide_c
    mixed_grad = mixed

    rows_sum[...] = jnp.zeros_like(rows_sum)

    def gate_rows(k):
        rows = pl.ds(pl.multiple_of(k * GROUP, GROUP), GROUP)
        for h in range(HEADS):
            along = slice(h * VALUE_DIM, (h + 1) * VALUE_DIM)
            whole, gate, grad = mixed[rows, along], gate_pre[rows, along], gated_grad[rows, along]
            scale = lax.rsqrt(jnp.mean(whole * whole, axis=-1, keepdims=True) + epsilon)
            sig = jax.nn.sigmoid(gate)
            plain = whole * scale
            gain = vectors[3:4, 0:VALUE_DIM]
            through = grad * (gate * sig)
            rows_sum[3:4, 0:VALUE_DIM] = rows_sum[3:4, 0:VALUE_DIM] + jnp.sum(
                through * plain, axis=0, keepdims=True
            )
            back = through * gain
            mixed_grad[rows, along] = scale * (
                back - plain * jnp.mean(back * plain, axis=-1, keepdims=True)
            )
            outgate_grad[rows, along] = (
                grad * plain * gain * sig * (1.0 + gate * (1.0 - sig))
            ).astype(bf16)

    loop(groups, gate_rows)

    lower = lower_mask()
    total[...] = jnp.zeros_like(total)
    state[...] = jnp.zeros_like(state)

    def state_rows(k):
        rows = pl.ds(pl.multiple_of(k * GROUP, GROUP), GROUP)
        cumulative = dot(lower, log_decay_of(decay_pre[rows, :]), NN, highest)
        cumulative_all[rows, :] = cumulative
        query_scaled = query[rows, :].astype(f32) * key_scale
        query_dev[rows, :] = (query_scaled * jnp.exp(cumulative + total[0:1, :])).astype(bf16)
        total[...] = total[...] + cumulative[GROUP - 1 :]

    loop(groups, state_rows)
    for h in range(HEADS):
        across = slice(h * KEY_DIM, (h + 1) * KEY_DIM)
        along = slice(h * VALUE_DIM, (h + 1) * VALUE_DIM)
        state[h] = dot(mixed_grad[:, along].astype(bf16), query_dev[:, across], TN)
    total[...] = jnp.exp(total[...])
    scan = Scan(
        sizes, True, total, state, before_total, before_state, scan_buffers, scan_sems
    )

    def weight_grad(target, right):
        block = width // sizes[0]
        size = min(right.shape[1], 256)

        def features(a):
            left = normed[:, pl.ds(pl.multiple_of(a * block, block), block)]

            def columns(k):
                here = pl.ds(pl.multiple_of(k * size, size), size)
                made = dot(left, right[:, here], TN)
                shaped = made.reshape(target.shape[1:5] + (size,))
                target[a, :, :, :, :, here] = shaped.astype(bf16)

            loop(right.shape[1] // size, columns)

        loop(sizes[0], features)

    for k in range(len(scan.hops)):
        scan.send(k)
        if k == 0:
            scatter.pump(1)
            weight_grad(local[3], outgate_grad)
        else:
            scatter.pump(2)
        if k == 1:
            scatter.load(2)
        scan.receive(k)

    def group(k):
        g = groups - 1 - k
        rows = pl.ds(pl.multiple_of(g * GROUP, GROUP), GROUP)
        cumulative = cumulative_all[rows, :]
        middle = cumulative[GROUP // 2 - 1 : GROUP // 2]
        ending = cumulative[GROUP - 1 :]
        query_scaled = query[rows, :].astype(f32) * key_scale
        key_full = key[rows, :].astype(f32)
        from_middle, to_middle = jnp.exp(cumulative - middle), jnp.exp(middle - cumulative)
        to_end, from_start = jnp.exp(ending - cumulative), jnp.exp(cumulative)
        decay_end = jnp.exp(ending)
        gated_query = (query_scaled * from_middle).astype(bf16)
        inverse_key = (key_full * to_middle).astype(bf16)
        tail_key = (key_full * to_end).astype(bf16)
        state_query = (query_scaled * from_start).astype(bf16)
        grad_cumul, through_end = [], []
        for h in range(HEADS):
            across = slice(h * KEY_DIM, (h + 1) * KEY_DIM)
            along = slice(h * VALUE_DIM, (h + 1) * VALUE_DIM)
            start_b, after = starts[g, h], before_state[h]
            start, after_b = start_b.astype(f32), after.astype(bf16)
            grad_out = mixed_grad[rows, along].astype(bf16)
            value_b = value[rows, along]
            scores = (dot(gated_query[:, across], inverse_key[:, across], NT) * lower).astype(bf16)
            grad_scores = (dot(grad_out, value_b, NT) * lower).astype(bf16)
            to_query = from_start[:, across] * dot(grad_out, start_b, NN)
            to_query = to_query + from_middle[:, across] * dot(
                grad_scores, inverse_key[:, across], NN
            )
            to_key = to_middle[:, across] * dot(grad_scores, gated_query[:, across], TN)
            to_key = to_key + to_end[:, across] * dot(value_b, after_b, NN)
            to_value = dot(scores, grad_out, TN) + dot(tail_key[:, across], after_b, NT)
            end_state = decay_end[:, across] * start + dot(value_b, tail_key[:, across], TN)
            through_end.append(jnp.sum(end_state * after, axis=0, keepdims=True))
            grad_cumul.append(query_scaled[:, across] * to_query - key_full[:, across] * to_key)
            before_state[h] = decay_end[:, across] * after + dot(
                grad_out, state_query[:, across], TN
            )
            query_grad[rows, across] = (to_query * key_scale).astype(bf16)
            key_grad[rows, across] = to_key.astype(bf16)
            value_grad[rows, along] = to_value.astype(bf16)
        log_grad = dot(lower, jnp.concatenate(grad_cumul, axis=1), TN, highest)
        log_grad = log_grad + jnp.concatenate(through_end, axis=1)
        to_decay = log_grad * jax.nn.sigmoid(-decay_pre[rows, :]) * (1.0 / 16.0)
        rows_sum[2:3, 0:keys] = rows_sum[2:3, 0:keys] + jnp.sum(to_decay, axis=0, keepdims=True)
        decay_grad[rows, :] = to_decay.astype(bf16)
        for turn in range(groups):
            pl.when(k == turn)(lambda: scatter.pump(2))

    loop(groups, group)

    weight_grad(local[0], query_grad)
    weight_grad(local[1], key_grad)
    weight_grad(local[2], value_grad)
    rank_grad[...] = dot(decay_grad[...], decay_up[...], NT).astype(bf16)
    weight_grad(local[4], rank_grad)
    scatter.begin([7, 4, 5, 6, 8])
    decay_up_grad = dot(rank_act[...], decay_grad[...], TN)[0:RANK]

    for copy in loads[3:]:
        copy.wait()
    middle_load = pltpu.make_async_copy(far_arrays[3], wide_c, load_sem.at[8])
    middle_load.start()
    gradients = (rank_grad, query_grad, key_grad, value_grad, outgate_grad)

    def features(k):
        here = pl.ds(pl.multiple_of(k * 256, 256), 256)
        made = dot(gradients[0][...], weights[0][here, :], NT)
        for grad, weight in zip(gradients[1:], weights[1:]):
            made = made + dot(grad[...], weight[here, :], NT)
        wide_a[:, here] = made

    loop(width // 256, features)
    middle_load.wait()

    def input_rows(k):
        rows = pl.ds(pl.multiple_of(k * 32, 32), 32)
        hidden = tokens[rows, :].astype(f32)
        scale = lax.rsqrt(jnp.mean(hidden * hidden, axis=-1, keepdims=True) + epsilon)
        plain = hidden * scale
        grad = wide_a[rows, :]
        rows_sum[0:1, :] = rows_sum[0:1, :] + jnp.sum(grad * plain, axis=0, keepdims=True)
        grad = grad * vectors[0:1, :]
        input_grad[rows, :] = wide_c[rows, :] + scale * (
            grad - plain * jnp.mean(grad * plain, axis=-1, keepdims=True)
        )

    loop(count_rows // 32, input_rows)

    per_feature, per_key, per_value = width // devices, keys // devices, VALUE_DIM // devices
    tiny = fold(decay_up_grad, 0, per_key)
    row_of = lax.broadcasted_iota(jnp.int32, tiny.shape, 1)
    for k, vector in enumerate(
        (
            fold(rows_sum[0:1, :], VECTORS, per_feature),
            fold(side[0:1, :], VECTORS, per_feature),
            fold(rows_sum[2:3, 0:keys], VECTORS, per_key),
            fold(rows_sum[3:4, 0:VALUE_DIM], VECTORS, per_value),
        )
    ):
        tiny = tiny + jnp.where(row_of == k, jnp.broadcast_to(vector, tiny.shape), 0.0)
    local[5][...] = tiny.reshape(local[5].shape)
    scatter.begin([9])
    scatter.finish()
    scan.finish()


def backward(sizes, far_grads, weights, arrays, local_arrays):
    outer, inner, side, core = sizes
    devices = outer * inner * side * core
    shape = jax.ShapeDtypeStruct
    most = max(max(sizes) - 1, 1)
    rows, width = local_arrays[-1].shape
    keys, values = HEADS * KEY_DIM, HEADS * VALUE_DIM
    far = [g.reshape(sizes + (g.shape[0] // devices, g.shape[1])) for g in far_grads]
    mine = width // devices
    made = [((mine, n), bf16) for n in (keys, keys, values, values, LANES)] + [((RANK, LANES), f32)]
    blocks = [(g.shape[4:], g.dtype) for g in far] + made

    def buffers(lead, of):
        return [pltpu.VMEM(lead + block, dtype) for block, dtype in of]

    outs = [shape(block, f32) for block, _ in blocks] + [shape((rows, width), f32)]
    vmem = pl.BlockSpec(memory_space=pltpu.VMEM)
    anywhere = pl.BlockSpec(memory_space=pl.ANY)
    results = pl.pallas_call(
        functools.partial(backward_kernel, sizes),
        out_shape=outs,
        in_specs=[anywhere] * (len(far) + len(weights) + len(arrays)) + [vmem] * len(local_arrays),
        out_specs=[vmem] * len(outs),
        scratch_shapes=buffers(sizes, made)
        + buffers((2, inner, side), [blocks[0], blocks[1], blocks[3]])
        + buffers((outer, inner, side), blocks)
        + buffers((max(side - 1, 1), outer, inner), blocks)
        + buffers((max(inner - 1, 1), outer), blocks)
        + buffers((max(outer - 1, 1),), blocks)
        + [pltpu.VMEM(w.shape, w.dtype) for w in weights]
        + [
            pltpu.VMEM((rows, values), f32),
            pltpu.VMEM((rows, values), f32),
            pltpu.VMEM((rows, values), f32),
            pltpu.VMEM((rows, values), bf16),
            pltpu.VMEM((rows, keys), f32),
            pltpu.VMEM((rows, keys), bf16),
            pltpu.VMEM((rows, keys), bf16),
            pltpu.VMEM((rows, keys), bf16),
            pltpu.VMEM((rows, values), bf16),
            pltpu.VMEM((rows, keys), bf16),
            pltpu.VMEM((rows, LANES), bf16),
            pltpu.VMEM((8, width), f32),
        ]
        + scan_scratch(sizes)
        + [
            pltpu.SemaphoreType.DMA((len(blocks), 4, most)),
            pltpu.SemaphoreType.DMA((len(blocks), 4, most)),
            pltpu.SemaphoreType.DMA((len(blocks), 2)),
            pltpu.SemaphoreType.DMA((9,)),
        ],
        compiler_params=pltpu.CompilerParams(
            collective_id=1, has_side_effects=True, vmem_limit_bytes=VMEM_LIMIT
        ),
    )(*far, *weights, *arrays, *local_arrays)
    return results[:-1], results[-1]


def matmul(left, right):
    return jnp.dot(left, right, preferred_element_type=f32)


def contract_rows(left, right):
    return dot(left, right, TN)


def times_transpose(left, right):
    return dot(left, right, NT)


def tiny_pack(decay_up, vectors):
    rows = [jnp.pad(decay_up.astype(f32), ((0, 0), (0, VECTORS - decay_up.shape[1])))]
    stacked = jnp.stack(
        [jnp.pad(v.astype(f32), (0, LANES - VECTORS - v.shape[0])) for v in vectors]
    )
    rows.append(jnp.pad(stacked, ((0, RANK - len(vectors)), (0, 0))))
    return jnp.concatenate(rows, axis=1)


def local(
    sizes,
    inputs,
    cotangent,
    mixer_gain,
    feed_gain,
    w_query,
    w_key,
    w_value,
    w_outgate,
    w_decay_down,
    w_decay_up,
    decay_bias,
    head_gain,
    w_output,
    w_gate,
    w_up,
    w_down,
):
    width = inputs.shape[2]
    rows = inputs.shape[0] * inputs.shape[1]
    per_feature, per_key, per_value = (
        mixer_gain.shape[0],
        decay_bias.shape[0],
        head_gain.shape[0],
    )
    tokens = inputs.reshape(rows, width)
    tiny = tiny_pack(w_decay_up, (mixer_gain, feed_gain, decay_bias, head_gain))
    down_padded = jnp.pad(w_decay_down, ((0, 0), (0, LANES - RANK)))
    shards = (
        tiny, down_padded, w_query, w_key, w_value, w_outgate, w_output, w_gate, w_up, w_down,
    )
    weights, arrays = forward(sizes, tokens, shards)
    weights = [w.reshape(-1, w.shape[-1]) for w in weights]
    proj_output, feed_gate, feed_up, feed_down = weights[5:]
    (vectors, decay_up, normed, query, key, value, gate_pre, rank_act, decay_pre) = arrays[:9]
    (starts, mixed, gated) = arrays[9:]
    gain_two = vectors[1:2]
    hidden_in = tokens.astype(f32)
    middle = hidden_in + matmul(gated, proj_output)
    feed_scale = lax.rsqrt(jnp.mean(middle * middle, axis=-1, keepdims=True) + epsilon)
    normed_two = (middle * feed_scale * gain_two).astype(bf16)
    up_gate = matmul(normed_two, feed_gate)
    up_lin = matmul(normed_two, feed_up)
    up_sig = jax.nn.sigmoid(up_gate)
    activated = (up_gate * up_sig * up_lin).astype(bf16)
    result = middle + matmul(activated, feed_down)
    grad_rows = cotangent.reshape(rows, width)
    grad_b = grad_rows.astype(bf16)
    grad_down = contract_rows(activated, grad_b).astype(bf16)
    act_grad = times_transpose(grad_b, feed_down)
    gate_grad = (act_grad * up_lin * up_sig * (1.0 + up_gate * (1.0 - up_sig))).astype(bf16)
    lin_grad = (act_grad * up_gate * up_sig).astype(bf16)
    grad_gate = contract_rows(normed_two, gate_grad).astype(bf16)
    grad_up = contract_rows(normed_two, lin_grad).astype(bf16)
    normed_two_grad = times_transpose(gate_grad, feed_gate) + times_transpose(lin_grad, feed_up)
    grad_feed_gain = jnp.sum(normed_two_grad * middle * feed_scale, axis=0)
    scaled_two = normed_two_grad * gain_two
    middle_grad = (
        grad_rows
        + feed_scale * scaled_two
        - middle * feed_scale**3 * jnp.mean(scaled_two * middle, axis=-1, keepdims=True)
    )
    middle_b = middle_grad.astype(bf16)
    grad_output = contract_rows(gated, middle_b).astype(bf16)
    gated_grad = times_transpose(middle_b, proj_output)
    side = jnp.broadcast_to(grad_feed_gain[None], (8, width))
    sums, input_grad = backward(
        sizes,
        (grad_down, grad_gate, grad_up, grad_output),
        weights[:5],
        (gated_grad, mixed, gate_pre, middle_grad),
        (query, key, value, decay_pre, starts, normed, rank_act, decay_up, vectors, side, tokens),
    )
    (down, gate, up, output, g_query, g_key, g_value, g_outgate, decay_down, small) = sums
    return (
        result.reshape(inputs.shape),
        input_grad.reshape(inputs.shape),
        small[0, VECTORS : VECTORS + per_feature],
        small[1, VECTORS : VECTORS + per_feature],
        g_query,
        g_key,
        g_value,
        g_outgate,
        decay_down[:, :RANK],
        small[:, :per_key],
        small[2, VECTORS : VECTORS + per_key],
        small[3, VECTORS : VECTORS + per_value],
        output,
        gate,
        up,
        down,
    )


def solution(mesh):
    placed = (
        P("batch", "seq", None),
        P("batch", "seq", None),
        P(("seq", "batch")),
        P(("seq", "batch")),
        P(("seq", "batch"), None),
        P(("seq", "batch"), None),
        P(("seq", "batch"), None),
        P(("seq", "batch"), None),
        P(("seq", "batch"), None),
        P(None, ("seq", "batch")),
        P(("seq", "batch")),
        P(("seq", "batch")),
        P(("seq", "batch"), None),
        P(("seq", "batch"), None),
        P(("seq", "batch"), None),
        P(("seq", "batch"), None),
    )
    return jax.shard_map(
        functools.partial(local, grid_of(mesh.shape)),
        mesh=mesh,
        in_specs=placed,
        out_specs=(
            P("batch", "seq", None),
            P("batch", "seq", None),
            P(("seq", "batch")),
            P(("seq", "batch")),
            P(("seq", "batch"), None),
            P(("seq", "batch"), None),
            P(("seq", "batch"), None),
            P(("seq", "batch"), None),
            P(("seq", "batch"), None),
            P(None, ("seq", "batch")),
            P(("seq", "batch")),
            P(("seq", "batch")),
            P(("seq", "batch"), None),
            P(("seq", "batch"), None),
            P(("seq", "batch"), None),
            P(("seq", "batch"), None),
        ),
        check_vma=False,
    )
```

time: 2230 us -> 385 us (0.17)
  waiting for transfers between devices: 1750 us -> 0 us
  Pallas kernels: 0 us -> 326 us
  blocking collectives: 186 us -> 0 us
  matrix products: 152 us -> 32.4 us
  other arithmetic: 62.2 us -> 1.85 us
  local copies, waits for them, and re-layouts: 51.1 us -> 23.8 us
    reduce_scatter x8 -> x0, waiting for transfers between devices: 1160 us -> none  [the longest x1 157 us: local(): lax.psum_scatter(grad_up, ('seq', 'batch'), scatter_dimension=0, tiled=True)]
    all_gather x10 -> x0, waiting for transfers between devices: 405 us -> none  [the longest x2 101 us: entering(): everything = jax.tree.map(lambda part: lax.all_gather(part, axis), value)]
    pallas_call x0 -> x2, Pallas kernels: none -> 326 us  [the longest x1 183 us: backward(): pl.pallas_call(functools.partial(backward_kernel, sizes), out_shape=outs,...]
    unnamed x22 -> x0, waiting for transfers between devices: 176 us -> none
    dot_general x90 -> x12, matrix products: 148 us -> 32.4 us  [the longest x8 23.5 us: dot(): lax.dot_general(left, right, (dims, ((), ())), precision=precision, prefe...]
    all_gather x3 -> x0, blocking collectives: 105 us -> none  [the longest x1 40.8 us: local(): lax.all_gather(w_decay_down, ('seq', 'batch'), axis=0, tiled=True)]
    unnamed x2 -> x0, blocking collectives: 81.2 us -> none
    select_n x24 -> x0, other arithmetic: 22.4 us -> none  [the longest x16 19.9 us: turn(): return jax.tree.map(lambda a, b: jnp.where(reached, a, b), new, before)]
  transfers between devices with their start and end apart: 20 -> 0, of which waited for: 18 -> 0; matrix products, arithmetic and copies ran while one was open for 6% -> 0% of each run, Pallas kernels for 0% -> 0%
where the time goes in v2:
time: 385 us
  Pallas kernels  326 us (85%)
  matrix products  32.4 us (8%)
  local copies, waits for them, and re-layouts  23.8 us (6%)
    pallas_call x1, Pallas kernels, backward(): pl.pallas_call(functools.partial(backward_kernel, sizes), out_shape=outs,...  183 us
    pallas_call x1, Pallas kernels, forward(): pl.pallas_call(functools.partial(forward_kernel, sizes, count), out_shape...  142 us
    dot_general x8, matrix products, dot(): lax.dot_general(left, right, (dims, ((), ())), precision=precision, prefe...  23.5 us
    unnamed x40, local copies, waits for them, and re-layouts  16.5 us
    dot_general x4, matrix products, matmul(): return jnp.dot(left, right, preferred_element_type=f32)  8.83 us

profile of v2, /device:TPU:0, one launch (start us, length us, event | category | flops | bytes accessed | tf_op | source)
XLA Modules:
  0.0 384.7 jit_solution(13361371438010963102)
XLA Ops:
  2.0 1.4 fusion.13.refs_0_
  4.8 142.4 %shard_map.279 = (bf16[4,2,2,2,32,128]{5,4,3,2,1,0:T(8,128)(2,1)}, bf16[4,2,2,2,32,512]{5,4,3,2,1,0:T(8,128)(2,1)}, bf16[4,2,2,2,32,512]{5,4,3,2,1,0:T(8,128)(2,...) custom-call(f32[16,128]{1,0:T(8,128)} %fusion.13.refs_0_, ...), custom_call_target="tpu_custom_call" | custom-call | tf_op jit(solution)/shard_map/pallas_call | solution.py:456
  147.9 2.8 multiply_reduce_fusion.2
  151.5 1.7 fusion.22
  153.5 1.7 fusion.21
  155.5 3.5 multiply_convert_fusion
  159.1 2.7 fusion
  161.8 1.7 fusion.23
  163.4 1.9 multiply_reduce_fusion
  165.7 1.3 copy-done.1
  167.0 1.7 fusion.4.refs_9_
  169.3 2.1 convolution_convert_fusion.3
  171.4 4.2 %fusion.18 = bf16[2816,1024]{1,0:T(8,128)(2,1)} fusion(bf16[256,2816]{1,0:T(8,128)(2,1)S(1)} %get-tuple-element.100, f32[1,256,1024]{2,1,0:T(8,128)S(1)} %copy-done.2), kind=kOutput, calls=%fused_computation.48 | convolution fusion | flops 1476395008 | bytes 8257536 | tf_op jit(solution)/shard_map/dot_general | solution.py:102
  175.6 4.2 %convolution_convert_fusion = bf16[1024,2816]{1,0:T(8,128)(2,1)} fusion(bf16[256,1024]{1,0:T(8,128)(2,1)S(1)} %multiply_convert_fusion.3, bf16[256,2816]{1,0:T(8,128)(2,1)S(1)} %get-tuple-element.98), kind=kOutput, calls=%fused_computation | convolution fusion | flops 1479278592 | bytes 7733248 | tf_op jit(solution)/shard_map/dot_general | solution.py:102
  179.8 4.3 %convolution_convert_fusion.1 = bf16[1024,2816]{1,0:T(8,128)(2,1)} fusion(bf16[256,1024]{1,0:T(8,128)(2,1)S(1)} %multiply_convert_fusion.3, bf16[256,2816]{1,0:T(8,128)(2,1)S(1)} %get-tuple-element.99), kind=kOutput, calls=%fused_computation.1 | convolution fusion | flops 1479278592 | bytes 7733248 | tf_op jit(solution)/shard_map/dot_general | solution.py:102
  184.0 183.4 %shard_map.280 = (f32[88,1024]{1,0:T(8,128)}, f32[32,2816]{1,0:T(8,128)}, f32[32,2816]{1,0:T(8,128)}, f32[32,1024]{1,0:T(8,128)}, f32[32,512]{1,0:T(8,128)}, /*i...) custom-call(bf16[4,2,2,2,88,1024]{5,4,3,2,1,0:T(8,128)(2,1)} %bitcas, ...), custom_call_target="tpu_custom_call" | custom-call | tf_op jit(solution)/shard_map/pallas_call | solution.py:876
  367.5 1.4 slice_bitcast_fusion.1
  370.1 1.3 slice_bitcast_fusion.2
  371.4 1.4 copy.34
  372.8 2.3 copy.46
  375.1 1.5 copy.47
  376.6 1.5 copy.48
  378.1 1.6 copy.49
  379.7 1.6 copy.50
  (46 shorter events, 10.6 us)
Async XLA Ops:
  147.9 3.6 copy-start.9
  150.7 2.5 slice-start
  151.5 2.0 slice-start.1
  151.5 3.7 slice-start.2
  153.5 1.7 copy-start.2
  153.5 2.1 slice-start.3
  165.4 1.6 copy-start.1
  167.0 4.4 %copy-start = (f32[256,1024]{1,0:T(8,128)}, f32[256,1024]{1,0:T(8,128)S(1)}, u32[]{:S(2)}) copy-start(f32[256,1024]{1,0:T(8,128)S(1)} %fusion.1.refs_12_) | copy-start | bytes 3145732
  167.0 2.3 copy-start.3
  367.4 13.8 %copy-start.8 = (f32[16,128]{1,0:T(8,128)S(1)}, f32[16,128]{1,0:T(8,128)}, u32[]{:S(2)}) copy-start(f32[16,128]{1,0:T(8,128)} %get-tuple-element.70) | copy-start | bytes 24580
  367.5 14.4 %copy-start.7 = (f32[32,1024]{1,0:T(8,128)S(1)}, f32[32,1024]{1,0:T(8,128)}, u32[]{:S(2)}) copy-start(f32[32,1024]{1,0:T(8,128)} %get-tuple-element.140) | copy-start | bytes 393220
  367.5 15.0 %copy-start.6 = (f32[32,2816]{1,0:T(8,128)S(1)}, f32[32,2816]{1,0:T(8,128)}, u32[]{:S(2)}) copy-start(f32[32,2816]{1,0:T(8,128)} %get-tuple-element.141) | copy-start | bytes 1081348
  367.5 15.8 %copy-start.5 = (f32[32,2816]{1,0:T(8,128)S(1)}, f32[32,2816]{1,0:T(8,128)}, u32[]{:S(2)}) copy-start(f32[32,2816]{1,0:T(8,128)} %get-tuple-element.142) | copy-start | bytes 1081348
  367.5 16.5 %copy-start.4 = (f32[88,1024]{1,0:T(8,128)S(1)}, f32[88,1024]{1,0:T(8,128)}, u32[]{:S(2)}) copy-start(f32[88,1024]{1,0:T(8,128)} %get-tuple-element.143) | copy-start | bytes 1081348

commit v3 on v0

v3 whole, which is shorter than its diff:
```python
import functools
from types import SimpleNamespace

import jax
import jax.numpy as jnp
from jax import lax
from jax.experimental import pallas as pl
from jax.experimental.pallas import tpu as pltpu
from jax.sharding import PartitionSpec as P

HEADS = 4
KEY_DIM = 128
VALUE_DIM = 256
GROUP = 64
LANES = 128
RANK = 16
VECTORS = 32
MESH = pl.DeviceIdType.MESH
VMEM_LIMIT = 63 * 2**20


class Names:
    def __getattr__(self, name):
        return name


N = Names()
epsilon = 1e-06
key_scale = KEY_DIM ** (-0.5)
highest = lax.Precision.HIGHEST
high = lax.Precision.HIGH
f32 = jnp.float32
bf16 = jnp.bfloat16


def grid_of(shape):
    seq, batch = shape["seq"], shape["batch"]
    outer = 4 if seq % 4 == 0 else seq
    core = 2 if batch % 2 == 0 else 1
    return (outer, seq // outer, batch // core, core)


def coords_of(sizes):
    seq, batch = lax.axis_index("seq"), lax.axis_index("batch")
    return (seq // sizes[1], seq % sizes[1], batch // sizes[3], batch % sizes[3])


def device_of(sizes, at):
    return {"seq": at[0] * sizes[1] + at[1], "batch": at[2] * sizes[3] + at[3]}


def moved(sizes, at, axis, by):
    new = list(at)
    new[axis] = lax.rem(at[axis] + (by % sizes[axis]), sizes[axis])
    return tuple(new)


def region(ref, free, at):
    return ref.at[tuple(slice(None) if k in free else at[k] for k in range(4))]


def orders_of(sizes, late=False):
    orders = ((1, 2, 0, 3), (2, 1, 0, 3)) if late else ((0, 1, 2, 3), (0, 2, 1, 3))
    return orders if sizes[1] == sizes[2] and sizes[3] == 2 else orders[:1]


def hops_of(sizes):
    length, hops = sizes[0] * sizes[1], []
    while 2 ** len(hops) < length:
        hops.append(2 ** len(hops))
    return hops


def greet(sizes, at):
    barrier = pltpu.get_barrier_semaphore()
    length = sizes[0] * sizes[1]
    seq, batch = lax.axis_index("seq"), lax.axis_index("batch")
    targets = [
        device_of(sizes, moved(sizes, at, axis, by))
        for axis in range(4)
        for by in range(1, sizes[axis])
    ]
    for hop in hops_of(sizes):
        for by in (hop, length - hop):
            targets.append({"seq": lax.rem(seq + by, length), "batch": batch})
    for target in targets:
        pl.semaphore_signal(barrier, inc=1, device_id=target, device_id_type=MESH)
    pl.semaphore_wait(barrier, len(targets))


def by_order(sizes, at, act, late=False):
    orders = orders_of(sizes, late)
    if len(orders) == 1:
        act(orders[0])
        return
    for parity, order in enumerate(orders):
        pl.when(at[3] == parity)(functools.partial(act, order))


def loop(count, body):
    def step(k, carry):
        body(k)
        return carry

    lax.fori_loop(0, count, step, 0)


def dot(left, right, dims, precision=None):
    return lax.dot_general(
        left, right, (dims, ((), ())), precision=precision, preferred_element_type=f32
    )


NN = ((1,), (0,))
NT = ((1,), (1,))
TN = ((0,), (0,))


class Item:
    def __init__(self, ref, start=0, size=None):
        self.ref, self.start = ref, start
        self.size = ref.shape[-1] if size is None else size
        self.part = self.size != ref.shape[-1]

    def tail(self):
        return (slice(None), slice(self.start, self.start + self.size)) if self.part else ()

    def at(self, index):
        return self.ref.at[tuple(index) + self.tail()]


def blocks_of(free, at, axes=4):
    return tuple(slice(None) if k in free else at[k] for k in range(axes))


class Gather:
    def __init__(self, sizes, at, shards, wholes, sems, late):
        self.sizes, self.at, self.late = sizes, at, late
        self.shards, self.wholes = shards, wholes
        self.send_sem, self.recv_sem, self.own_sem = sems
        self.done = {item: 0 for item in range(len(shards))}

    def copies(self, item, order, step, arriving):
        axis, free = order[step], order[:step]
        made = []
        for by in range(1, self.sizes[axis]):
            source = moved(self.sizes, self.at, axis, -by) if arriving else self.at
            place = self.wholes[item].at(blocks_of(free, source))
            made.append(
                pltpu.make_async_remote_copy(
                    src_ref=self.shards[item].at(()) if step == 0 and not arriving else place,
                    dst_ref=place,
                    send_sem=self.send_sem.at[item, step, by - 1],
                    recv_sem=self.recv_sem.at[item, step, by - 1],
                    device_id=device_of(self.sizes, moved(self.sizes, self.at, axis, by)),
                    device_id_type=MESH,
                )
            )
        return made

    def own(self, item):
        return pltpu.make_async_copy(
            self.shards[item].at(()),
            self.wholes[item].at(blocks_of((), self.at)),
            self.own_sem.at[item],
        )

    def begin(self, items):
        for item in items:

            def act(order, item=item):
                for copy in self.copies(item, order, 0, False):
                    copy.start()

            if item in self.late:
                by_order(self.sizes, self.at, act, True)
            else:
                act(orders_of(self.sizes)[0])
            self.own(item).start()

    def advance(self, item, step):
        while self.done[item] < step:
            now = self.done[item] = self.done[item] + 1
            if now == 1:
                self.own(item).wait()

            def act(order, now=now):
                for copy in self.copies(item, order, now - 1, True):
                    copy.wait_recv()
                if now < 4:
                    for copy in self.copies(item, order, now, False):
                        copy.start()

            by_order(self.sizes, self.at, act, item in self.late)

    def finish(self):
        for item in self.done:
            self.advance(item, 4)
        for late in (False, True):

            def act(order, late=late):
                for item in self.done:
                    if (item in self.late) == late:
                        for step in range(4):
                            for copy in self.copies(item, order, step, False):
                                copy.wait_send()

            by_order(self.sizes, self.at, act, late)


class Scatter:
    def __init__(self, sizes, at, sources, stages, near, half, part, last, sums, sems, late):
        self.sizes, self.at, self.late = sizes, at, late
        self.sources, self.stages, self.near = sources, stages, near
        self.landings = (last, part, half)
        self.sums = sums
        self.send_sem, self.recv_sem, self.own_sem = sems
        self.left = {}
        self.released = set()

    def copy(self, item, order, step, by):
        axis, free = order[step], order[:step]
        target = moved(self.sizes, self.at, axis, by)
        if step == 3:
            source = self.sources[item].at(blocks_of(free, target))
            landing = self.near[item]
        else:
            source = self.near[item].at[blocks_of(free, target, 3)]
            landing = self.landings[step][item].at[by - 1]
        return pltpu.make_async_remote_copy(
            src_ref=source,
            dst_ref=landing,
            send_sem=self.send_sem.at[item, step, by - 1],
            recv_sem=self.recv_sem.at[item, step, by - 1],
            device_id=device_of(self.sizes, target),
            device_id_type=MESH,
        )

    def own(self, item, k):
        slot = k % 2
        return pltpu.make_async_copy(
            self.sources[item].at((k, slice(None), slice(None), self.at[3])),
            self.stages[item].at[slot],
            self.own_sem.at[item, slot],
        )

    def begin(self, item):
        self.left[item] = 4
        self.copy(item, orders_of(self.sizes)[0], 3, 1).start()
        if item in self.stages:
            for k in range(min(2, self.sizes[0])):
                self.own(item, k).start()

    def advance(self, item, step):
        while self.left[item] > step:
            now = self.left[item] = self.left[item] - 1

            def act(order, now=now):
                self.add(item, order, now)
                if now > 0:
                    for by in range(1, self.sizes[order[now - 1]]):
                        self.copy(item, order, now - 1, by).start()

            by_order(self.sizes, self.at, act, item in self.late)

    def add(self, item, order, step):
        sizes, at = self.sizes, self.at
        axis, free = order[step], sorted(order[:step])
        near = self.near[item]
        for by in range(1, sizes[axis]):
            self.copy(item, order, step, by).wait_recv()
        if step == 0:
            total = near[at[0], at[1], at[2]].astype(f32)
            for by in range(1, sizes[axis]):
                total = total + self.landings[0][item][by - 1].astype(f32)
            kept = self.sums[item]
            kept.ref[:, kept.start : kept.start + kept.size] = total
            return
        staged = step == 3 and item in self.stages

        def at_outer(k):
            if staged:
                self.own(item, k).wait()
            for j in range(sizes[free[1]] if len(free) > 1 else 1):
                for i in range(sizes[free[2]] if len(free) > 2 else 1):
                    within = (k, j, i)[: len(free)]
                    place = list(at[:3])
                    for axis_of, index in zip(free, within):
                        place[axis_of] = index
                    place = tuple(place)
                    total = near[place].astype(f32)
                    if staged:
                        total = total + self.stages[item][(k % 2,) + place[1:]].astype(f32)
                    elif step == 3:
                        source = self.sources[item]
                        mine = source.ref[place + (at[3],) + source.tail()]
                        total = total + mine.astype(f32)
                    else:
                        for by in range(1, sizes[axis]):
                            come = self.landings[step][item].at[by - 1]
                            total = total + come[within].astype(f32)
                    near[place] = total.astype(near.dtype)
            if staged:

                @pl.when(k + 2 < sizes[0])
                def _():
                    self.own(item, k + 2).start()

        loop(sizes[free[0]], at_outer)

    def release(self, item):
        self.advance(item, 3)
        self.released.add(item)
        self.copy(item, orders_of(self.sizes)[0], 3, 1).wait_send()

    def finish(self):
        for item in self.left:
            self.advance(item, 0)
        for late in (False, True):

            def act(order, late=late):
                for item in self.left:
                    if (item in self.late) == late:
                        for step in range(3 if item in self.released else 4):
                            for by in range(1, self.sizes[order[step]]):
                                self.copy(item, order, step, by).wait_send()

            by_order(self.sizes, self.at, act, late)


class Scan:
    def __init__(self, sizes, reverse, total, state, before_total, before_state, buffers, sems):
        self.sizes, self.reverse = sizes, reverse
        self.total, self.state = total, state
        self.before_total, self.before_state = before_total, before_state
        self.total_out, self.total_in, self.state_out, self.state_in = buffers
        self.sems = sems
        self.hops = hops_of(sizes)
        self.length = sizes[0] * sizes[1]
        self.place = self.length - 1 - lax.axis_index("seq") if reverse else lax.axis_index("seq")

    def copies(self, k):
        seq = lax.axis_index("seq")
        hop = self.length - self.hops[k] if self.reverse else self.hops[k]
        target = {"seq": lax.rem(seq + hop, self.length), "batch": lax.axis_index("batch")}
        pairs = ((self.total_out, self.total_in), (self.state_out, self.state_in))
        return [
            pltpu.make_async_remote_copy(
                src_ref=out.at[k],
                dst_ref=come.at[k],
                send_sem=self.sems.at[0, k, n],
                recv_sem=self.sems.at[1, k, n],
                device_id=target,
                device_id_type=MESH,
            )
            for n, (out, come) in enumerate(pairs)
        ]

    def send(self, k):
        if k == 0:
            self.before_total[...] = jnp.ones_like(self.before_total)
            self.before_state[...] = jnp.zeros_like(self.before_state)
        self.total_out[k] = self.total[...]
        for h in range(HEADS):
            self.state_out[k, h] = self.state[h].astype(bf16)

        @pl.when(self.place + self.hops[k] < self.length)
        def _():
            for copy in self.copies(k):
                copy.start()

    def receive(self, k):
        @pl.when(self.place >= self.hops[k])
        def _():
            for copy in self.copies(k):
                copy.wait_recv()
            come = self.total_in[k]
            for h in range(HEADS):
                keys = slice(h * KEY_DIM, (h + 1) * KEY_DIM)
                state = self.state_in[k, h].astype(f32)
                self.before_state[h] = (
                    self.before_state[h] + self.before_total[0:1, keys] * state
                )
                if k + 1 < len(self.hops):
                    self.state[h] = self.state[h] + self.total[0:1, keys] * state
            self.before_total[...] = self.before_total[...] * come
            if k + 1 < len(self.hops):
                self.total[...] = self.total[...] * come

    def finish(self):
        for k in range(len(self.hops)):

            @pl.when(self.place + self.hops[k] < self.length)
            def _(k=k):
                for copy in self.copies(k):
                    copy.wait_send()


def lower_mask():
    rows = lax.broadcasted_iota(jnp.int32, (GROUP, GROUP), 0)
    columns = lax.broadcasted_iota(jnp.int32, (GROUP, GROUP), 1)
    return jnp.where(rows >= columns, 1.0, 0.0).astype(f32)


def log_decay_of(decay_pre):
    return jax.nn.log_sigmoid(decay_pre) * (1.0 / 16.0)


def spread(block, offset, per, width):
    devices = width // per
    lane = lax.broadcasted_iota(jnp.int32, (LANES, width), 0)
    column = lax.broadcasted_iota(jnp.int32, (LANES, width), 1)
    pick = jnp.where(lane == offset + column % per, 1.0, 0.0).astype(bf16)
    wide = dot(block.astype(bf16), pick, NN)
    rows = block.shape[0] // devices
    wide = wide.reshape(devices, rows, width)
    device = lax.broadcasted_iota(jnp.int32, wide.shape, 0)
    column = lax.broadcasted_iota(jnp.int32, wide.shape, 2)
    return jnp.sum(jnp.where(device == column // per, wide, 0.0), axis=0)


def scan_scratch(sizes):
    hops = len(hops_of(sizes))
    keys = HEADS * KEY_DIM
    return dict(
        total=pltpu.VMEM((8, keys), f32),
        state=pltpu.VMEM((HEADS, VALUE_DIM, KEY_DIM), f32),
        before_total=pltpu.VMEM((8, keys), f32),
        before_state=pltpu.VMEM((HEADS, VALUE_DIM, KEY_DIM), f32),
        total_out=pltpu.VMEM((hops, 8, keys), f32),
        total_in=pltpu.VMEM((hops, 8, keys), f32),
        state_out=pltpu.VMEM((hops, HEADS, VALUE_DIM, KEY_DIM), bf16),
        state_in=pltpu.VMEM((hops, HEADS, VALUE_DIM, KEY_DIM), bf16),
        scan_sem=pltpu.SemaphoreType.DMA((2, hops, 2)),
    )


def scan_of(sizes, reverse, r):
    return Scan(
        sizes,
        reverse,
        r.total,
        r.state,
        r.before_total,
        r.before_state,
        (r.total_out, r.total_in, r.state_out, r.state_in),
        r.scan_sem,
    )


def head_slices(h):
    return slice(h * KEY_DIM, (h + 1) * KEY_DIM), slice(h * VALUE_DIM, (h + 1) * VALUE_DIM)


def tile(k, size):
    return pl.ds(pl.multiple_of(k * size, size), size)


def halves(columns):
    first = -(-columns // 512) * 256
    return ((0, first), (first, columns - first))


WEIGHTS = (N.decay_down, N.query, N.key, N.value, N.outgate, N.output, N.gate, N.up, N.down)
KEPT = WEIGHTS[:5]
LATE_GATHERED = ()
FORWARD_PLAN = (
    1001, 1011, 1002, 1021, 1012, 1003, 1031, 1013, 1022, 1004, 0, 1032, 1014, 1, 1041, 2,
    1023, 1024, 3, 1051, 1033, 1042, 1034, 4, 1061, 1052, 1062, 1071, 1043, 1044, 5, 6,
    1081, 1053, 1072, 100, 1091, 1063, 1054, 7, 1064, 1101, 1082, 200, 101, 1111, 1073, 1092,
    1121, 1074, 201, 102, 1102, 1083, 1112, 202, 300, 8, 9, 1084, 1122, 1093, 10, 1094,
    1103, 1104, 11, 1113, 12, 1114, 13, 1123, 15, 1124, 14, 17, 18, 16,
)


def forward_kernel(sizes, names, *refs):
    r = SimpleNamespace(**dict(zip(names, refs)))
    at = coords_of(sizes)
    devices = sizes[0] * sizes[1] * sizes[2] * sizes[3]
    count_rows, width = r.tokens.shape
    keys, values = HEADS * KEY_DIM, HEADS * VALUE_DIM
    hidden = r.up_gate.shape[1]
    groups = count_rows // GROUP
    vectors = r.vectors
    per_feature, per_key, per_value = width // devices, keys // devices, VALUE_DIM // devices

    tiny = r.tiny_mine
    tiny[...] = jnp.zeros_like(tiny)
    tiny[:, 0:per_key] = r.w_decay_up[...].astype(f32)
    for k, name in enumerate((N.mixer_gain, N.feed_gain, N.decay_bias, N.head_gain)):
        vector = getattr(r, name)
        tiny[k : k + 1, VECTORS : VECTORS + vector.shape[1]] = vector[...].astype(f32)
    down_mine = r.down_mine
    down_mine[...] = jnp.zeros_like(down_mine)
    down_mine[:, 0:RANK] = turned(r.w_decay_down[...]).astype(bf16)
    greet(sizes, at)

    shards, wholes, index = [Item(tiny)], [Item(r.tiny_all)], {N.tiny: 0}
    late = set()

    def item(name, shard, whole, start=0, size=None):
        index[name] = len(shards)
        if name in LATE_GATHERED:
            late.add(len(shards))
        shards.append(Item(shard, start, size))
        wholes.append(Item(whole, start, size))

    item(N.decay_down, down_mine, r.all_decay_down)
    for name in (N.query, N.key, N.value, N.outgate, N.output):
        item(name, getattr(r, N.w_ + name), getattr(r, N.all_ + name))
    for k in range(2):
        for name in (N.gate, N.up):
            item(name + str(k), getattr(r, N.w_ + name), getattr(r, N.all_ + name), *halves(hidden)[k])
    for k in range(2):
        item(N.down + str(k), r.w_down, r.all_down, *halves(width)[k])
    gather = Gather(
        sizes, at, shards, wholes, (r.send_sem, r.recv_sem, r.own_sem), late
    )
    gather.begin([index[name] for name in index])
    scan = scan_of(sizes, False, r)
    saved = []

    def save(*names_of):
        for name in names_of:
            source = getattr(r, N.all_ + name[7:]) if name.startswith(N.weight_) else getattr(r, name)
            copy = pltpu.make_async_copy(source, getattr(r, N.out_ + name), r.save_sem.at[len(saved)])
            copy.start()
            saved.append(copy)

    def need(*names_of):
        for name in names_of:
            gather.advance(index[name], 4)

    lower = lower_mask()

    def unpack():
        need(N.tiny)
        whole = r.tiny_all[...].reshape(devices, RANK, LANES)
        vectors[...] = jnp.zeros_like(vectors)
        vectors[0:1, :] = spread(whole[:, 0], VECTORS, per_feature, width)
        vectors[1:2, :] = spread(whole[:, 1], VECTORS, per_feature, width)
        vectors[2:3, 0:keys] = spread(whole[:, 2], VECTORS, per_key, keys)
        vectors[3:4, 0:VALUE_DIM] = spread(whole[:, 3], VECTORS, per_value, VALUE_DIM)
        decay_up = r.decay_up
        decay_up[...] = jnp.zeros_like(decay_up)
        decay_up[0:RANK, :] = spread(
            whole.reshape(devices * RANK, LANES), 0, per_key, keys
        ).astype(bf16)
        save(N.vectors, N.decay_up)

    def norm():
        def some(k):
            rows = tile(k, 32)
            plain = r.tokens[rows, :].astype(f32)
            scale = lax.rsqrt(jnp.mean(plain * plain, axis=-1, keepdims=True) + epsilon)
            r.normed[rows, :] = (plain * scale * vectors[0:1, :]).astype(bf16)
            r.grad_b[rows, :] = r.cotangent[rows, :].astype(bf16)

        loop(count_rows // 32, some)
        save(N.normed)

    def project(name, into):
        need(name)
        weight = getattr(r, N.all_ + name)
        size = min(into.shape[1], 256)

        def columns(k):
            here = tile(k, size)
            panel = weight[..., here].reshape(width, size)
            into[:, here] = dot(r.normed[...], panel, NN).astype(into.dtype)

        loop(into.shape[1] // size, columns)
        save(N.weight_ + name)

    def decay():
        project(N.decay_down, r.rank_act)
        r.decay_pre[...] = (
            dot(r.rank_act[...], r.decay_up[...], NN) + vectors[2:3, 0:keys]
        )
        save(N.rank_act, N.decay_pre)

    def attention():
        total, state = r.total, r.state
        total[...] = jnp.zeros_like(total)
        state[...] = jnp.zeros_like(state)

        def group(k):
            rows = tile(k, GROUP)
            cumulative = dot(lower, log_decay_of(r.decay_pre[rows, :]), NN, highest)
            middle = cumulative[GROUP // 2 - 1 : GROUP // 2]
            ending = cumulative[GROUP - 1 :]
            query_scaled = r.query[rows, :].astype(f32) * key_scale
            key_full = r.key[rows, :].astype(f32)
            gated_query = query_scaled * jnp.exp(cumulative - middle)
            inverse_key = key_full * jnp.exp(middle - cumulative)
            tail_key = key_full * jnp.exp(ending - cumulative)
            state_query = query_scaled * jnp.exp(cumulative)
            r.query_dev[rows, :] = state_query * jnp.exp(total[0:1, :])
            r.offsets[k] = total[...]
            for h in range(HEADS):
                across, along = head_slices(h)
                value_full = r.value[rows, along].astype(f32)
                scores = dot(gated_query[:, across], inverse_key[:, across], NT, high) * lower
                start = state[h]
                r.starts[k, h] = start.astype(bf16)
                r.mixed[rows, along] = dot(state_query[:, across], start, NT, high) + dot(
                    scores, value_full, NN, high
                )
                state[h] = jnp.exp(ending[:, across]) * start + dot(
                    value_full, tail_key[:, across], TN, high
                )
            total[...] = total[...] + ending

        loop(groups, group)
        total[...] = jnp.exp(total[...])
        save(N.query, N.key, N.value)

    def heads():
        before = r.before_state

        def some(k):
            rows = tile(k, GROUP)
            factor = jnp.exp(r.offsets[k])
            for h in range(HEADS):
                across, along = head_slices(h)
                begin = r.starts[k, h].astype(f32) + factor[0:1, across] * before[h]
                r.starts[k, h] = begin.astype(bf16)
                whole = r.mixed[rows, along] + dot(
                    r.query_dev[rows, across], before[h], NT, high
                )
                r.mixed[rows, along] = whole
                scale = lax.rsqrt(jnp.mean(whole * whole, axis=-1, keepdims=True) + epsilon)
                gate = r.gate_pre[rows, along]
                swish = gate * jax.nn.sigmoid(gate)
                r.gated[rows, along] = (
                    whole * scale * vectors[3:4, 0:VALUE_DIM] * swish
                ).astype(bf16)

        loop(groups, some)
        save(N.starts, N.gated)

    def middle():
        need(N.output)

        def columns(k):
            here = tile(k, 256)
            panel = r.all_output[..., here].reshape(values, 256)
            r.middle[:, here] = r.tokens[:, here].astype(f32) + dot(
                r.gated[...], panel, NN
            )

        loop(width // 256, columns)

        def some(k):
            rows = tile(k, 32)
            plain = r.middle[rows, :]
            scale = lax.rsqrt(jnp.mean(plain * plain, axis=-1, keepdims=True) + epsilon)
            r.normed_two[rows, :] = (plain * scale * vectors[1:2, :]).astype(bf16)

        loop(count_rows // 32, some)
        save(N.normed_two)

    def up(half):
        need(N.gate + str(half), N.up + str(half))
        start, size = halves(hidden)[half]

        def columns(k):
            here = pl.ds(pl.multiple_of(start + k * 256, 256), 256)
            normed_two = r.normed_two[...]
            gate = dot(normed_two, r.all_gate[..., here].reshape(width, 256), NN)
            line = dot(normed_two, r.all_up[..., here].reshape(width, 256), NN)
            r.up_gate[:, here] = gate
            r.up_lin[:, here] = line
            r.activated[:, here] = (gate * jax.nn.sigmoid(gate) * line).astype(bf16)

        loop(size // 256, columns)

    def down_grad():
        def out(k, slot):
            return pltpu.make_async_copy(
                r.panels.at[slot], r.out_down_grad.at[tile(k, 256), :], r.panel_sem.at[slot]
            )

        def some(k):
            slot = lax.rem(k, 2)

            @pl.when(k >= 2)
            def _():
                out(k - 2, slot).wait()

            left = r.activated[:, tile(k, 256)]
            r.panels[slot] = dot(left, r.grad_b[...], TN).astype(bf16)
            out(k, slot).start()

        count = hidden // 256
        loop(count, some)
        for k in range(max(count - 2, 0), count):
            out(k, k % 2).wait()

    down = r.all_down

    def act(half):
        need(N.down + str(half))
        start, size = halves(width)[half]
        along = slice(start, start + size)
        act_grad = r.act_grad
        count = 2 if sizes[0] % 2 == 0 else 1
        some, wide = down.shape[0] // count, hidden // count
        for k in range(count):
            here = slice(k * wide, (k + 1) * wide)
            panel = down[k * some : (k + 1) * some, :, :, :, :, along].reshape(wide, size)
            made = dot(r.grad_b[:, along], panel, NT)
            act_grad[:, here] = made if half == 0 else act_grad[:, here] + made
        if half == 0:
            return

        def finish(k):
            here = tile(k, 256)
            grad, gate, line = act_grad[:, here], r.up_gate[:, here], r.up_lin[:, here]
            sig = jax.nn.sigmoid(gate)
            r.gate_grad[:, here] = (grad * line * sig * (1.0 + gate * (1.0 - sig))).astype(bf16)
            r.lin_grad[:, here] = (grad * gate * sig).astype(bf16)

        loop(hidden // 256, finish)

    def block(half):
        need(N.down + str(half))
        start, size = halves(width)[half]

        def columns(k):
            here = pl.ds(pl.multiple_of(start + k * 256, 256), 256)
            r.block_output[:, here] = r.middle[:, here] + dot(
                r.activated[...], down[..., here].reshape(hidden, 256), NN
            )

        loop(size // 256, columns)

    def feed_back():
        save(N.gate_grad, N.lin_grad)
        part = width // sizes[0]

        def features(a):
            here = tile(a, part)
            r.normed_two_grad[:, here] = dot(
                r.gate_grad[...], r.all_gate[a].reshape(part, hidden), NT
            ) + dot(r.lin_grad[...], r.all_up[a].reshape(part, hidden), NT)

        loop(sizes[0], features)
        side = r.side
        side[...] = jnp.zeros_like(side)

        def some(k):
            rows = tile(k, 32)
            before = r.middle[rows, :]
            scale = lax.rsqrt(jnp.mean(before * before, axis=-1, keepdims=True) + epsilon)
            plain = before * scale
            grad = r.normed_two_grad[rows, :]
            side[1:2, :] = side[1:2, :] + jnp.sum(grad * plain, axis=0, keepdims=True)
            grad = grad * vectors[1:2, :]
            whole = r.cotangent[rows, :] + scale * (
                grad - plain * jnp.mean(grad * plain, axis=-1, keepdims=True)
            )
            r.middle_grad[rows, :] = whole
            r.middle_b[rows, :] = whole.astype(bf16)

        loop(count_rows // 32, some)
        save(N.middle_grad, N.middle_b)

    def heads_back():
        side = r.side
        gain = vectors[3:4, 0:VALUE_DIM]
        part = values // sizes[0]
        for h in range(HEADS):
            across, along = head_slices(h)
            first, count = h * VALUE_DIM // part, max(VALUE_DIM // part, 1)
            weight = r.all_output[first : first + count].reshape(count * part, width)
            r.gated_grad[...] = dot(r.middle_b[...], weight, NT)

            def some(k, along=along):
                rows = tile(k, GROUP)
                whole, gate = r.mixed[rows, along], r.gate_pre[rows, along]
                grad = r.gated_grad[rows, :]
                scale = lax.rsqrt(jnp.mean(whole * whole, axis=-1, keepdims=True) + epsilon)
                sig = jax.nn.sigmoid(gate)
                plain = whole * scale
                through = grad * (gate * sig)
                side[3:4, 0:VALUE_DIM] = side[3:4, 0:VALUE_DIM] + jnp.sum(
                    through * plain, axis=0, keepdims=True
                )
                back = through * gain
                r.mixed_grad[rows, along] = (
                    scale * (back - plain * jnp.mean(back * plain, axis=-1, keepdims=True))
                ).astype(bf16)
                r.outgate_grad[rows, along] = (
                    grad * plain * gain * sig * (1.0 + gate * (1.0 - sig))
                ).astype(bf16)

            loop(groups, some)
        save(N.mixed_grad, N.outgate_grad, N.side)

    pieces = dict(
        unpack=unpack,
        norm=norm,
        decay=decay,
        query=lambda: project(N.query, r.query),
        key=lambda: project(N.key, r.key),
        value=lambda: project(N.value, r.value),
        attention=attention,
        outgate=lambda: project(N.outgate, r.gate_pre),
        heads=heads,
        middle=middle,
        up0=lambda: up(0),
        up1=lambda: up(1),
        down_grad=down_grad,
        act0=lambda: act(0),
        act1=lambda: act(1),
        block0=lambda: block(0),
        block1=lambda: block(1),
        feed_back=feed_back,
        heads_back=heads_back,
    )
    run_plan(
        FORWARD_PLAN,
        pieces,
        scan,
        list(index),
        lambda name, step: gather.advance(index[name], step),
    )
    save(N.block_output)
    gather.finish()
    scan.finish()
    for copy in saved:
        copy.wait()


def run_plan(plan, pieces, scan, names, advance):
    hops = len(scan.hops)
    steps = list(pieces.values())
    for code in plan:
        if code >= 1000:
            advance(names[(code - 1000) // 10], code % 10)
        elif code < 100:
            steps[code]()
        elif code == 300:
            for k in range(3, hops):
                scan.send(k)
                scan.receive(k)
        elif code % 100 < hops:
            (scan.send if code < 200 else scan.receive)(code % 100)


def kernel_call(body, sizes, ins, outs, scratch, collective_id):
    vmem = pl.BlockSpec(memory_space=pltpu.VMEM)
    anywhere = pl.BlockSpec(memory_space=pl.ANY)
    names = list(ins) + list(outs) + list(scratch)
    assert len(set(names)) == len(names)
    results = pl.pallas_call(
        functools.partial(body, sizes, names),
        out_shape=[jax.ShapeDtypeStruct(o[0], o[1]) for o in outs.values()],
        in_specs=[vmem if i[1] else anywhere for i in ins.values()],
        out_specs=[vmem if o[2] else anywhere for o in outs.values()],
        scratch_shapes=list(scratch.values()),
        compiler_params=pltpu.CompilerParams(
            collective_id=collective_id, has_side_effects=True, vmem_limit_bytes=VMEM_LIMIT
        ),
    )(*(i[0] for i in ins.values()))
    return dict(zip(outs, results))


def forward(sizes, tokens, cotangent, small, weights):
    rows, width = tokens.shape
    keys, values = HEADS * KEY_DIM, HEADS * VALUE_DIM
    hidden = weights[N.gate].shape[1]
    groups = rows // GROUP
    most = max(max(sizes) - 1, 1)
    mine = weights[N.query].shape[0]
    ins = {N.tokens: (tokens, True), N.cotangent: (cotangent, True)}
    ins.update({name: (a, True) for name, a in small.items()})
    ins.update({N.w_ + name: (a, True) for name, a in weights.items()})
    shape_of = {name: sizes + a.shape for name, a in weights.items()}
    shape_of[N.decay_down] = sizes + (mine, LANES)
    made = dict(
        vectors=((8, width), f32),
        decay_up=((LANES, keys), bf16),
        normed=((rows, width), bf16),
        rank_act=((rows, LANES), bf16),
        decay_pre=((rows, keys), f32),
        query=((rows, keys), bf16),
        key=((rows, keys), bf16),
        value=((rows, values), bf16),
        starts=((groups, HEADS, VALUE_DIM, KEY_DIM), bf16),
        gated=((rows, values), bf16),
        normed_two=((rows, width), bf16),
        gate_grad=((rows, hidden), bf16),
        lin_grad=((rows, hidden), bf16),
        middle_grad=((rows, width), f32),
        middle_b=((rows, width), bf16),
        mixed_grad=((rows, values), bf16),
        outgate_grad=((rows, values), bf16),
        side=((8, width), f32),
        block_output=((rows, width), f32),
    )
    outs = {N.out_weight_ + name: (shape_of[name], bf16, False) for name in KEPT}
    outs.update({N.out_ + name: o + (False,) for name, o in made.items()})
    outs[N.out_down_grad] = ((hidden, width), bf16, False)
    scratch = {N.all_ + name: pltpu.VMEM(shape_of[name], bf16) for name in WEIGHTS}
    scratch.update({name: pltpu.VMEM(*o) for name, o in made.items()})
    scratch.update(
        tiny_mine=pltpu.VMEM((RANK, LANES), f32),
        tiny_all=pltpu.VMEM(sizes + (RANK, LANES), f32),
        down_mine=pltpu.VMEM((mine, LANES), bf16),
        grad_b=pltpu.VMEM((rows, width), bf16),
        gate_pre=pltpu.VMEM((rows, values), f32),
        query_dev=pltpu.VMEM((rows, keys), f32),
        offsets=pltpu.VMEM((groups, 8, keys), f32),
        mixed=pltpu.VMEM((rows, values), f32),
        middle=pltpu.VMEM((rows, width), f32),
        up_gate=pltpu.VMEM((rows, hidden), f32),
        up_lin=pltpu.VMEM((rows, hidden), f32),
        activated=pltpu.VMEM((rows, hidden), bf16),
        act_grad=pltpu.VMEM((rows, hidden), f32),
        panels=pltpu.VMEM((2, 256, width), bf16),
        normed_two_grad=pltpu.VMEM((rows, width), f32),
        gated_grad=pltpu.VMEM((rows, VALUE_DIM), f32),
        send_sem=pltpu.SemaphoreType.DMA((13, 4, most)),
        recv_sem=pltpu.SemaphoreType.DMA((13, 4, most)),
        own_sem=pltpu.SemaphoreType.DMA((13,)),
        save_sem=pltpu.SemaphoreType.DMA((len(made) + len(KEPT),)),
        panel_sem=pltpu.SemaphoreType.DMA((2,)),
    )
    scratch.update(scan_scratch(sizes))
    results = kernel_call(forward_kernel, sizes, ins, outs, scratch, 0)
    return {name[4:]: a for name, a in results.items()}


LATE_SCATTERED = (N.output,)
BACKWARD_PLAN = (
    0, 100, 2, 3, 1003, 6, 1013, 7, 200, 1023, 101, 4, 1033, 5, 1063, 1002,
    1073, 201, 102, 1043, 1053, 1012, 1001, 1011, 1022, 1062, 1032, 1021, 202, 300, 1, 1031,
    1072, 1000, 10, 8, 9, 1042, 11, 12, 1083, 1093, 1010, 1103, 1071, 1113, 13, 1020,
    1052, 1041, 1123, 1061, 1030, 1051, 1060, 1082, 1070, 1092, 1081, 1040, 1102, 1112, 1091, 1122,
    1050, 1101, 1111, 1121, 1080, 1090, 1100, 1110, 1120,
)
NORMED_BACK = (
    (N.decay_down, N.rank_grad),
    (N.query, N.query_grad),
    (N.key, N.key_grad),
    (N.value, N.value_grad),
    (N.outgate, N.outgate_grad),
)
LOADED = (
    N.query,
    N.decay_pre,
    N.mixed_grad,
    N.vectors,
    N.normed_two,
    N.gate_grad,
    N.lin_grad,
    N.gated,
    N.middle_b,
    N.normed,
    N.outgate_grad,
    N.key,
    N.value,
    N.starts,
    N.decay_up,
    N.rank_act,
    N.side,
    N.tokens,
)


def scatter_items(hidden, width):
    keys, values = HEADS * KEY_DIM, HEADS * VALUE_DIM
    items = {}
    for k, (start, size) in enumerate(halves(width)):
        items[N.down + str(k)] = (size, None, N.down, start)
    for k, (start, size) in enumerate(halves(hidden)):
        items[N.gate + str(k)] = (size, N.panel + str(k), N.gate, start)
    for k, (start, size) in enumerate(halves(hidden)):
        items[N.up + str(k)] = (size, N.panel + str(k), N.up, start)
    items[N.output] = (width, N.square0, N.output, 0)
    items[N.outgate] = (values, N.square1, N.outgate, 0)
    items[N.value] = (values, N.square0, N.value, 0)
    items[N.query] = (keys, N.query, N.query, 0)
    items[N.key] = (keys, N.key, N.key, 0)
    items[N.decay_down] = (LANES, N.decay_down, N.decay_down, 0)
    items[N.tiny] = (LANES, N.tiny, N.tiny, 0)
    return items


def backward_kernel(sizes, names, *refs):
    r = SimpleNamespace(**dict(zip(names, refs)))
    at = coords_of(sizes)
    devices = sizes[0] * sizes[1] * sizes[2] * sizes[3]
    count_rows, width = r.tokens.shape
    keys, values = HEADS * KEY_DIM, HEADS * VALUE_DIM
    hidden = r.gate_grad.shape[1]
    groups = count_rows // GROUP
    part = width // sizes[0]
    vectors, rows_sum = r.vectors, r.rows_sum
    per_feature, per_key, per_value = width // devices, keys // devices, VALUE_DIM // devices

    loads = {}
    for name in LOADED:
        loads[name] = pltpu.make_async_copy(
            getattr(r, N.in_ + name), getattr(r, name), r.load_sem.at[len(loads)]
        )
        loads[name].start()
    middle_load = pltpu.make_async_copy(
        r.in_middle_grad, r.input_grad, r.load_sem.at[len(loads)]
    )
    middle_load.start()

    def ready(*names_of):
        for name in names_of:
            if name in loads:
                loads.pop(name).wait()

    greet(sizes, at)
    items = scatter_items(hidden, width)
    index = {name: k for k, name in enumerate(items)}
    sources, stages, sums = {}, {}, {}
    for name, (size, slot, out, start) in items.items():
        k = index[name]
        if slot is None:
            sources[k] = Item(r.in_down_grad, start, size)
            stages[k] = getattr(r, N.stage_ + name)
        else:
            sources[k] = Item(getattr(r, N.slot_ + slot), 0, size)
        sums[k] = Item(getattr(r, N.sum_ + out), start, size)
    scatter = Scatter(
        sizes,
        at,
        sources,
        stages,
        [getattr(r, N.near_ + name) for name in items],
        [getattr(r, N.half_ + name) for name in items],
        [getattr(r, N.part_ + name) for name in items],
        [getattr(r, N.last_ + name) for name in items],
        sums,
        (r.send_sem, r.recv_sem, r.own_sem),
        {index[name] for name in LATE_SCATTERED},
    )
    scan = scan_of(sizes, True, r)
    in_slot = {}

    def take_slot(name):
        slot = items[name][1]
        if slot in in_slot:
            scatter.release(index[in_slot[slot]])
        in_slot[slot] = name
        return getattr(r, N.slot_ + slot)

    lower = lower_mask()
    scatter.begin(index[N.down0])
    scatter.begin(index[N.down1])

    def weight_grad(name, left, right, start=0):
        ready(left, right)
        target, columns_of = take_slot(name), items[name][0]
        size = min(columns_of, 256)

        def features(a):
            transposed = getattr(r, left)[:, tile(a, part)]

            def columns(k):
                here = pl.ds(pl.multiple_of(start + k * size, size), size)
                made = dot(transposed, getattr(r, right)[:, here], TN)
                shaped = made.reshape(target.shape[1:5] + (size,))
                target[a, :, :, :, :, tile(k, size)] = shaped.astype(bf16)

            loop(columns_of // size, columns)

        loop(sizes[0], features)
        scatter.begin(index[name])

    def begin_state():
        total, state, query_dev = r.total, r.state, r.query_grad
        rows_sum[...] = jnp.zeros_like(rows_sum)
        total[...] = jnp.zeros_like(total)
        ready(N.query, N.decay_pre, N.mixed_grad, N.vectors)

        def some(k):
            rows = tile(k, GROUP)
            cumulative = dot(lower, log_decay_of(r.decay_pre[rows, :]), NN, highest)
            r.cumulative[rows, :] = cumulative
            query_scaled = r.query[rows, :].astype(f32) * key_scale
            query_dev[rows, :] = (query_scaled * jnp.exp(cumulative + total[0:1, :])).astype(bf16)
            total[...] = total[...] + cumulative[GROUP - 1 :]

        loop(groups, some)
        for h in range(HEADS):
            across, along = head_slices(h)
            state[h] = dot(r.mixed_grad[:, along], query_dev[:, across], TN)
        total[...] = jnp.exp(total[...])

    def attention():
        ready(N.key, N.value, N.starts)
        after_state = r.before_state

        def group(k):
            g = groups - 1 - k
            rows = tile(g, GROUP)
            cumulative = r.cumulative[rows, :]
            middle = cumulative[GROUP // 2 - 1 : GROUP // 2]
            ending = cumulative[GROUP - 1 :]
            query_scaled = r.query[rows, :].astype(f32) * key_scale
            key_full = r.key[rows, :].astype(f32)
            from_middle, to_middle = jnp.exp(cumulative - middle), jnp.exp(middle - cumulative)
            to_end, from_start = jnp.exp(ending - cumulative), jnp.exp(cumulative)
            decay_end = jnp.exp(ending)
            gated_query = (query_scaled * from_middle).astype(bf16)
            inverse_key = (key_full * to_middle).astype(bf16)
            tail_key = (key_full * to_end).astype(bf16)
            state_query = (query_scaled * from_start).astype(bf16)
            grad_cumul, through_end = [], []
            for h in range(HEADS):
                across, along = head_slices(h)
                start_b, after = r.starts[g, h], after_state[h]
                start, after_b = start_b.astype(f32), after.astype(bf16)
                grad_out = r.mixed_grad[rows, along]
                value_b = r.value[rows, along]
                query_h, key_h, tail_h = (
                    gated_query[:, across],
                    inverse_key[:, across],
                    tail_key[:, across],
                )
                scores = (dot(query_h, key_h, NT) * lower).astype(bf16)
                grad_scores = (dot(grad_out, value_b, NT) * lower).astype(bf16)
                to_query = from_start[:, across] * dot(grad_out, start_b, NN)
                to_query = to_query + from_middle[:, across] * dot(grad_scores, key_h, NN)
                to_key = to_middle[:, across] * dot(grad_scores, query_h, TN)
                to_key = to_key + to_end[:, across] * dot(value_b, after_b, NN)
                to_value = dot(scores, grad_out, TN) + dot(tail_h, after_b, NT)
                end_state = decay_end[:, across] * start + dot(value_b, tail_h, TN)
                through_end.append(jnp.sum(end_state * after, axis=0, keepdims=True))
                grad_cumul.append(
                    query_scaled[:, across] * to_query - key_full[:, across] * to_key
                )
                after_state[h] = decay_end[:, across] * after + dot(
                    grad_out, state_query[:, across], TN
                )
                r.query_grad[rows, across] = (to_query * key_scale).astype(bf16)
                r.key_grad[rows, across] = to_key.astype(bf16)
                r.value_grad[rows, along] = to_value.astype(bf16)
            log_grad = dot(lower, jnp.concatenate(grad_cumul, axis=1), TN, highest)
            log_grad = log_grad + jnp.concatenate(through_end, axis=1)
            to_decay = log_grad * jax.nn.sigmoid(-r.decay_pre[rows, :]) * (1.0 / 16.0)
            rows_sum[2:3, 0:keys] = rows_sum[2:3, 0:keys] + jnp.sum(
                to_decay, axis=0, keepdims=True
            )
            r.decay_grad[rows, :] = to_decay.astype(bf16)

        loop(groups, group)

    def decay_down():
        ready(N.decay_up)
        r.rank_grad[...] = dot(r.decay_grad[...], r.decay_up[...], NT).astype(bf16)
        weight_grad(N.decay_down, N.normed, N.rank_grad)

    def input_grad():
        def panel(a, slot):
            return [
                pltpu.make_async_copy(
                    getattr(r, N.in_weight_ + name).at[a],
                    getattr(r, N.panel_ + name).at[slot],
                    r.panel_sem.at[k, slot],
                )
                for k, (name, _) in enumerate(NORMED_BACK)
            ]

        for a in range(min(2, sizes[0])):
            for copy in panel(a, a):
                copy.start()

        def features(a):
            slot = lax.rem(a, 2)
            for copy in panel(a, slot):
                copy.wait()
            made = None
            for name, grad in NORMED_BACK:
                weight = getattr(r, N.panel_ + name).at[slot]
                term = dot(getattr(r, grad)[...], weight[...].reshape(part, weight.shape[-1]), NT)
                made = term if made is None else made + term
            r.normed_grad[:, tile(a, part)] = made

            @pl.when(a + 2 < sizes[0])
            def _():
                for copy in panel(a + 2, slot):
                    copy.start()

        loop(sizes[0], features)
        middle_load.wait()
        ready(N.tokens)

        def some(k):
            rows = tile(k, 32)
            before = r.tokens[rows, :].astype(f32)
            scale = lax.rsqrt(jnp.mean(before * before, axis=-1, keepdims=True) + epsilon)
            plain = before * scale
            grad = r.normed_grad[rows, :]
            rows_sum[0:1, :] = rows_sum[0:1, :] + jnp.sum(grad * plain, axis=0, keepdims=True)
            grad = grad * vectors[0:1, :]
            r.input_grad[rows, :] = r.input_grad[rows, :] + scale * (
                grad - plain * jnp.mean(grad * plain, axis=-1, keepdims=True)
            )

        loop(count_rows // 32, some)

    def tiny():
        ready(N.rank_act, N.side)
        side = r.side
        decay_up_grad = dot(r.rank_act[...], r.decay_grad[...], TN)[0:RANK]
        row = lax.broadcasted_iota(jnp.int32, (RANK, LANES), 0)
        lane = lax.broadcasted_iota(jnp.int32, (RANK, LANES), 1)
        vectors_of = (
            (rows_sum[0:1, :], per_feature),
            (side[1:2, :], per_feature),
            (rows_sum[2:3, 0:keys], per_key),
            (side[3:4, 0:VALUE_DIM], per_value),
        )

        def cut(values_of, device, per, offset):
            group, first = divmod(device * per, LANES)
            piece = values_of[:, group * LANES : (group + 1) * LANES]
            return pltpu.roll(piece, (offset - first) % LANES, 1)

        target = take_slot(N.tiny)
        for device in range(devices):
            whole = jnp.where(lane < per_key, cut(decay_up_grad, device, per_key, 0), 0.0)
            for k, (vector, per) in enumerate(vectors_of):
                wide = jnp.broadcast_to(vector, (RANK, vector.shape[1]))
                here = (row == k) & (lane >= VECTORS) & (lane < VECTORS + per)
                whole = jnp.where(here, cut(wide, device, per, VECTORS), whole)
            place, rest = [], device
            for size in reversed(sizes):
                rest, last = divmod(rest, size)
                place.insert(0, last)
            target[tuple(place)] = whole
        scatter.begin(index[N.tiny])

    first = halves(hidden)[1][0]
    pieces = dict(
        state=begin_state,
        attention=attention,
        gate0=lambda: weight_grad(N.gate0, N.normed_two, N.gate_grad),
        gate1=lambda: weight_grad(N.gate1, N.normed_two, N.gate_grad, first),
        up0=lambda: weight_grad(N.up0, N.normed_two, N.lin_grad),
        up1=lambda: weight_grad(N.up1, N.normed_two, N.lin_grad, first),
        output=lambda: weight_grad(N.output, N.gated, N.middle_b),
        outgate=lambda: weight_grad(N.outgate, N.normed, N.outgate_grad),
        query=lambda: weight_grad(N.query, N.normed, N.query_grad),
        key=lambda: weight_grad(N.key, N.normed, N.key_grad),
        value=lambda: weight_grad(N.value, N.normed, N.value_grad),
        decay_down=decay_down,
        input_grad=input_grad,
        tiny=tiny,
    )
    run_plan(
        BACKWARD_PLAN,
        pieces,
        scan,
        list(items),
        lambda name, step: scatter.advance(index[name], step),
    )
    scatter.finish()
    scan.finish()
    ready(*list(loads))


def backward(sizes, tokens, saved):
    outer, inner, side, core = sizes
    devices = outer * inner * side * core
    most = max(max(sizes) - 1, 1)
    rows, width = tokens.shape
    hidden = saved[N.gate_grad].shape[1]
    keys, values = HEADS * KEY_DIM, HEADS * VALUE_DIM
    mine, mine_down = width // devices, hidden // devices
    down_grad = saved[N.down_grad].reshape(sizes + (mine_down, width))
    saved = dict(saved, tokens=tokens)
    ins = {N.in_ + name: (saved[name], False) for name in LOADED}
    ins[N.in_middle_grad] = (saved[N.middle_grad], False)
    ins[N.in_down_grad] = (down_grad, False)
    ins.update({N.in_weight_ + name: (saved[N.weight_ + name], False) for name in KEPT})
    items = scatter_items(hidden, width)
    block, scratch, sums = {}, {}, {}
    for name, (size, slot, out, start) in items.items():
        rows_of = {N.down: mine_down, N.tiny: RANK}.get(out, mine)
        dtype = f32 if out == N.tiny else bf16
        block = (rows_of, size)
        sums[N.sum_ + out] = ((rows_of, start + size), f32, True)
        if slot is None:
            scratch[N.stage_ + name] = pltpu.VMEM((2, inner, side) + block, dtype)
        elif N.slot_ + slot not in scratch:
            scratch[N.slot_ + slot] = pltpu.VMEM(sizes + block, dtype)
        scratch[N.near_ + name] = pltpu.VMEM((outer, inner, side) + block, dtype)
        order = orders_of(sizes, name in LATE_SCATTERED)[0]
        for step, landing in ((2, N.half_), (1, N.part_), (0, N.last_)):
            lead = (max(sizes[order[step]] - 1, 1),) + tuple(sizes[k] for k in order[:step])
            scratch[landing + name] = pltpu.VMEM(lead + block, dtype)
    scratch.update({n: pltpu.VMEM(saved[n].shape, saved[n].dtype) for n in LOADED})
    scratch.update(
        {
            N.panel_ + n: pltpu.VMEM((2,) + saved[N.weight_ + n].shape[1:], bf16)
            for n, _ in NORMED_BACK
        }
    )
    scratch.update(
        rows_sum=pltpu.VMEM((8, width), f32),
        cumulative=pltpu.VMEM((rows, keys), f32),
        query_grad=pltpu.VMEM((rows, keys), bf16),
        key_grad=pltpu.VMEM((rows, keys), bf16),
        value_grad=pltpu.VMEM((rows, values), bf16),
        decay_grad=pltpu.VMEM((rows, keys), bf16),
        rank_grad=pltpu.VMEM((rows, LANES), bf16),
        normed_grad=pltpu.VMEM((rows, width), f32),
        send_sem=pltpu.SemaphoreType.DMA((len(items), 4, most)),
        recv_sem=pltpu.SemaphoreType.DMA((len(items), 4, most)),
        own_sem=pltpu.SemaphoreType.DMA((len(items), 2)),
        load_sem=pltpu.SemaphoreType.DMA((len(LOADED) + 1,)),
        panel_sem=pltpu.SemaphoreType.DMA((len(NORMED_BACK), 2)),
    )
    scratch.update(scan_scratch(sizes))
    outs = dict(sums, input_grad=((rows, width), f32, True))
    return kernel_call(backward_kernel, sizes, ins, outs, scratch, 1)


def turned(array, precision=None):
    size = array.shape[0]
    rows = lax.broadcasted_iota(jnp.int32, (size, size), 0)
    columns = lax.broadcasted_iota(jnp.int32, (size, size), 1)
    return dot(array, jnp.where(rows == columns, 1.0, 0.0).astype(array.dtype), TN, precision)


def hand_out_kernel(count, cuts, *refs):
    whole, down, tiny = refs[:count], refs[count], refs[count + 1]
    outs, small, sems = refs[count + 2 : 2 * count + 2], refs[2 * count + 2 : -1], refs[-1]
    copies = []
    for k, (source, target) in enumerate(zip(whole, outs)):
        copies.append(pltpu.make_async_copy(source, target, sems.at[k]))
        copies[-1].start()
    small[0][...] = turned(down[...], highest)[0 : small[0].shape[0]]
    for target, (row, column) in zip(small[1:], cuts):
        target[...] = tiny[row : row + target.shape[0], column : column + target.shape[1]]
    for copy in copies:
        copy.wait()


def hand_out(arrays, decay_down, tiny, cuts):
    vmem = pl.BlockSpec(memory_space=pltpu.VMEM)
    shapes = [a.shape for a in arrays] + [(RANK, decay_down.shape[0])] + [c[0] for c in cuts]
    return pl.pallas_call(
        functools.partial(hand_out_kernel, len(arrays), [c[1] for c in cuts]),
        out_shape=[jax.ShapeDtypeStruct(s, f32) for s in shapes],
        in_specs=[vmem] * (len(arrays) + 2),
        out_specs=[pl.BlockSpec(memory_space=pl.ANY)] * len(arrays) + [vmem] * (len(cuts) + 1),
        scratch_shapes=[pltpu.SemaphoreType.DMA((len(arrays),))],
        compiler_params=pltpu.CompilerParams(vmem_limit_bytes=VMEM_LIMIT),
    )(*arrays, decay_down, tiny)


def local(
    sizes,
    inputs,
    cotangent,
    mixer_gain,
    feed_gain,
    w_query,
    w_key,
    w_value,
    w_outgate,
    w_decay_down,
    w_decay_up,
    decay_bias,
    head_gain,
    w_output,
    w_gate,
    w_up,
    w_down,
):
    width = inputs.shape[2]
    rows = inputs.shape[0] * inputs.shape[1]
    per_feature, per_key, per_value = (
        mixer_gain.shape[0],
        decay_bias.shape[0],
        head_gain.shape[0],
    )
    tokens = inputs.reshape(rows, width)
    small = dict(
        w_decay_up=w_decay_up,
        mixer_gain=mixer_gain.reshape(1, -1),
        feed_gain=feed_gain.reshape(1, -1),
        decay_bias=decay_bias.reshape(1, -1),
        head_gain=head_gain.reshape(1, -1),
    )
    weights = dict(
        decay_down=w_decay_down.T,
        query=w_query,
        key=w_key,
        value=w_value,
        outgate=w_outgate,
        output=w_output,
        gate=w_gate,
        up=w_up,
        down=w_down,
    )
    saved = forward(sizes, tokens, cotangent.reshape(rows, width), small, weights)
    got = backward(sizes, tokens, saved)
    names = (N.query, N.key, N.value, N.outgate, N.output, N.gate, N.up, N.down)
    handed = hand_out(
        [saved[N.block_output], got[N.input_grad]] + [got[N.sum_ + name] for name in names],
        got[N.sum_decay_down],
        got[N.sum_tiny],
        (
            ((RANK, per_key), (0, 0)),
            ((1, per_feature), (0, VECTORS)),
            ((1, per_feature), (1, VECTORS)),
            ((1, per_key), (2, VECTORS)),
            ((1, per_value), (3, VECTORS)),
        ),
    )
    result, input_grad = (a.reshape(inputs.shape) for a in handed[:2])
    g_query, g_key, g_value, g_outgate, g_output, g_gate, g_up, g_down = handed[2:10]
    decay_down, decay_up = handed[10:12]
    g_mixer, g_feed, g_bias, g_head = (a.reshape(-1) for a in handed[12:])
    return (
        result,
        input_grad,
        g_mixer,
        g_feed,
        g_query,
        g_key,
        g_value,
        g_outgate,
        decay_down.T,
        decay_up,
        g_bias,
        g_head,
        g_output,
        g_gate,
        g_up,
        g_down,
    )


def solution(mesh):
    placed = (
        P("batch", "seq", None),
        P("batch", "seq", None),
        P(("seq", "batch")),
        P(("seq", "batch")),
        P(("seq", "batch"), None),
        P(("seq", "batch"), None),
        P(("seq", "batch"), None),
        P(("seq", "batch"), None),
        P(("seq", "batch"), None),
        P(None, ("seq", "batch")),
        P(("seq", "batch")),
        P(("seq", "batch")),
        P(("seq", "batch"), None),
        P(("seq", "batch"), None),
        P(("seq", "batch"), None),
        P(("seq", "batch"), None),
    )
    return jax.shard_map(
        functools.partial(local, grid_of(mesh.shape)),
        mesh=mesh,
        in_specs=placed,
        out_specs=(
            P("batch", "seq", None),
            P("batch", "seq", None),
            P(("seq", "batch")),
            P(("seq", "batch")),
            P(("seq", "batch"), None),
            P(("seq", "batch"), None),
            P(("seq", "batch"), None),
            P(("seq", "batch"), None),
            P(("seq", "batch"), None),
            P(None, ("seq", "batch")),
            P(("seq", "batch")),
            P(("seq", "batch")),
            P(("seq", "batch"), None),
            P(("seq", "batch"), None),
            P(("seq", "batch"), None),
            P(("seq", "batch"), None),
        ),
        check_vma=False,
    )
```

time: 2230 us -> 308 us (0.14)
  waiting for transfers between devices: 1750 us -> 0 us
  Pallas kernels: 0 us -> 304 us
  blocking collectives: 186 us -> 0 us
  matrix products: 152 us -> 0 us
  other arithmetic: 62.2 us -> 0 us
  local copies, waits for them, and re-layouts: 51.1 us -> 0 us
    reduce_scatter x8 -> x0, waiting for transfers between devices: 1160 us -> none  [the longest x1 157 us: local(): lax.psum_scatter(grad_up, ('seq', 'batch'), scatter_dimension=0, tiled=True)]
    all_gather x10 -> x0, waiting for transfers between devices: 405 us -> none  [the longest x2 101 us: entering(): everything = jax.tree.map(lambda part: lax.all_gather(part, axis), value)]
    pallas_call x0 -> x3, Pallas kernels: none -> 304 us  [the longest x2 300 us: kernel_call(): pl.pallas_call(functools.partial(body, sizes, names), out_shape=[jax.Shap...]
    unnamed x22 -> x0, waiting for transfers between devices: 176 us -> none
    dot_general x90 -> x0, matrix products: 148 us -> none  [the longest x8 34 us: contract_rows(): lax.dot_general(left, right, (((0,), (0,)), ((), ())), preferred_element_...]
    all_gather x3 -> x0, blocking collectives: 105 us -> none  [the longest x1 40.8 us: local(): lax.all_gather(w_decay_down, ('seq', 'batch'), axis=0, tiled=True)]
    unnamed x2 -> x0, blocking collectives: 81.2 us -> none
    select_n x24 -> x0, other arithmetic: 22.4 us -> none  [the longest x16 19.9 us: turn(): return jax.tree.map(lambda a, b: jnp.where(reached, a, b), new, before)]
  transfers between devices with their start and end apart: 20 -> 0, of which waited for: 18 -> 0; matrix products, arithmetic and copies ran while one was open for 6% -> 0% of each run, Pallas kernels for 0% -> 0%
where the time goes in v3:
time: 308 us; the launch traced here: 305 us
  Pallas kernels  304 us (99%)
    pallas_call x2, Pallas kernels, kernel_call(): pl.pallas_call(functools.partial(body, sizes, names), out_shape=[jax.Shap...  300 us

profile of v3, /device:TPU:0, one launch (start us, length us, event | category | flops | bytes accessed | tf_op | source)
XLA Modules:
  0.0 305.3 jit_solution(8104253998223759375)
XLA Ops:
  0.7 150.7 %shard_map.279 = (bf16[4,2,2,2,32,128]{5,4,3,2,1,0:T(8,128)(2,1)}, bf16[4,2,2,2,32,512]{5,4,3,2,1,0:T(8,128)(2,1)}, bf16[4,2,2,2,32,512]{5,4,3,2,1,0:T(8,128)(2,...) custom-call(bf16[256,1024]{1,0:T(8,128)(2,1)} %bitcast.16, ...), custom_call_target="tpu_custom_call" | custom-call | tf_op jit(solution)/shard_map/pallas_call | solution.py:857
  151.4 149.1 %shard_map.280 = (f32[88,1024]{1,0:T(8,128)}, f32[32,2816]{1,0:T(8,128)}, f32[32,2816]{1,0:T(8,128)}, f32[32,1024]{1,0:T(8,128)}, f32[32,1024]{1,0:T(8,128)}, /*...) custom-call(bf16[256,512]{1,0:T(8,128)(2,1)} %get-tuple-element.69.r, ...), custom_call_target="tpu_custom_call" | custom-call | tf_op jit(solution)/shard_map/pallas_call | solution.py:857
  300.5 4.6 %shard_map.281 = (f32[256,1024]{1,0:T(8,128)}, f32[256,1024]{1,0:T(8,128)}, f32[32,512]{1,0:T(8,128)}, f32[32,512]{1,0:T(8,128)}, f32[32,1024]{1,0:T(8,128)}, /*...) custom-call(f32[256,1024]{1,0:T(8,128)} %get-tuple-element.68.refs_0, ...), custom_call_target="tpu_custom_call" | custom-call | tf_op jit(solution)/shard_map/pallas_call | solution.py:1353

commit v4 on v3

--- a/solution.py
+++ b/solution.py
@@ -16,7 +16,7 @@
 RANK = 16
 VECTORS = 32
 MESH = pl.DeviceIdType.MESH
-VMEM_LIMIT = 63 * 2**20
+VMEM_LIMIT = 67_000_000
 
 
 class Names:
@@ -47,6 +47,14 @@
 
 def device_of(sizes, at):
     return {"seq": at[0] * sizes[1] + at[1], "batch": at[2] * sizes[3] + at[3]}
+
+
+def place_of(sizes, device):
+    place = []
+    for size in reversed(sizes):
+        device, last = divmod(device, size)
+        place.insert(0, last)
+    return tuple(place)
 
 
 def moved(sizes, at, axis, by):
@@ -209,14 +217,13 @@
 
 
 class Scatter:
-    def __init__(self, sizes, at, sources, stages, near, half, part, last, sums, sems, late):
-        self.sizes, self.at, self.late = sizes, at, late
-        self.sources, self.stages, self.near = sources, stages, near
-        self.landings = (last, part, half)
-        self.sums = sums
-        self.send_sem, self.recv_sem, self.own_sem = sems
-        self.left = {}
-        self.released = set()
+    def __init__(self, sizes, at, sources, lands, sums, outs, sems, late, stop=0):
+        self.sizes, self.at, self.late, self.stop = sizes, at, late, stop
+        self.outs = outs
+        self.sources, self.sums = sources, sums
+        self.near, self.lands = lands[3], lands
+        self.send_sem, self.recv_sem, self.load_sem, self.out_sem = sems
+        self.left, self.sent, self.resumed = {}, {}, {}
 
     def copy(self, item, order, step, by):
         axis, free = order[step], order[:step]
@@ -225,8 +232,9 @@
             source = self.sources[item].at(blocks_of(free, target))
             landing = self.near[item]
         else:
-            source = self.near[item].at[blocks_of(free, target, 3)]
-            landing = self.landings[step][item].at[by - 1]
+            whole = self.resumed[item] if step == 1 and item in self.resumed else self.near[item]
+            source = whole.at[blocks_of(free, target, 3)]
+            landing = self.lands[step][item].at[by - 1]
         return pltpu.make_async_remote_copy(
             src_ref=source,
             dst_ref=landing,
@@ -236,32 +244,49 @@
             device_id_type=MESH,
         )
 
-    def own(self, item, k):
-        slot = k % 2
-        return pltpu.make_async_copy(
-            self.sources[item].at((k, slice(None), slice(None), self.at[3])),
-            self.stages[item].at[slot],
-            self.own_sem.at[item, slot],
-        )
-
     def begin(self, item):
         self.left[item] = 4
+        self.sent[item] = {3}
         self.copy(item, orders_of(self.sizes)[0], 3, 1).start()
-        if item in self.stages:
-            for k in range(min(2, self.sizes[0])):
-                self.own(item, k).start()
+
+    def load(self, item):
+        return pltpu.make_async_copy(self.resumed[item], self.near[item], self.load_sem.at[item])
+
+    def resume(self, item, far):
+        self.left[item] = 2
+        self.sent[item] = {1}
+        self.resumed[item] = far
+        self.load(item).start()
+
+        def act(order):
+            for by in range(1, self.sizes[order[1]]):
+                self.copy(item, order, 1, by).start()
+
+        by_order(self.sizes, self.at, act, item in self.late)
 
     def advance(self, item, step):
-        while self.left[item] > step:
+        while self.left[item] > max(step, self.stop):
             now = self.left[item] = self.left[item] - 1
-
-            def act(order, now=now):
+            more = now > self.stop
+            if more:
+                self.sent[item].add(now - 1)
+            if now == 1 and item in self.resumed:
+                self.load(item).wait()
+
+            def act(order, now=now, more=more):
                 self.add(item, order, now)
-                if now > 0:
+                if more:
                     for by in range(1, self.sizes[order[now - 1]]):
                         self.copy(item, order, now - 1, by).start()
 
             by_order(self.sizes, self.at, act, item in self.late)
+            if now == 0:
+                self.out(item).start()
+
+    def out(self, item):
+        return pltpu.make_async_copy(
+            self.sums[item].at(()), self.outs[item].at(()), self.out_sem.at[item]
+        )
 
     def add(self, item, order, step):
         sizes, at = self.sizes, self.at
@@ -272,15 +297,12 @@
         if step == 0:
             total = near[at[0], at[1], at[2]].astype(f32)
             for by in range(1, sizes[axis]):
-                total = total + self.landings[0][item][by - 1].astype(f32)
+                total = total + self.lands[0][item][by - 1].astype(f32)
             kept = self.sums[item]
             kept.ref[:, kept.start : kept.start + kept.size] = total
             return
-        staged = step == 3 and item in self.stages
-
-        def at_outer(k):
-            if staged:
-                self.own(item, k).wait()
+
+        def at_first(k):
             for j in range(sizes[free[1]] if len(free) > 1 else 1):
                 for i in range(sizes[free[2]] if len(free) > 2 else 1):
                     within = (k, j, i)[: len(free)]
@@ -289,39 +311,34 @@
                         place[axis_of] = index
                     place = tuple(place)
                     total = near[place].astype(f32)
-                    if staged:
-                        total = total + self.stages[item][(k % 2,) + place[1:]].astype(f32)
-                    elif step == 3:
+                    if step == 3:
                         source = self.sources[item]
                         mine = source.ref[place + (at[3],) + source.tail()]
                         total = total + mine.astype(f32)
                     else:
                         for by in range(1, sizes[axis]):
-                            come = self.landings[step][item].at[by - 1]
+                            come = self.lands[step][item].at[by - 1]
                             total = total + come[within].astype(f32)
                     near[place] = total.astype(near.dtype)
-            if staged:
-
-                @pl.when(k + 2 < sizes[0])
-                def _():
-                    self.own(item, k + 2).start()
-
-        loop(sizes[free[0]], at_outer)
+
+        loop(sizes[free[0]], at_first)
 
     def release(self, item):
         self.advance(item, 3)
-        self.released.add(item)
+        self.sent[item].remove(3)
         self.copy(item, orders_of(self.sizes)[0], 3, 1).wait_send()
 
     def finish(self):
         for item in self.left:
             self.advance(item, 0)
+            if self.stop == 0:
+                self.out(item).wait()
         for late in (False, True):
 
             def act(order, late=late):
                 for item in self.left:
                     if (item in self.late) == late:
-                        for step in range(3 if item in self.released else 4):
+                        for step in sorted(self.sent[item]):
                             for by in range(1, self.sizes[order[step]]):
                                 self.copy(item, order, step, by).wait_send()
 
@@ -419,6 +436,13 @@
     return jnp.sum(jnp.where(device == column // per, wide, 0.0), axis=0)
 
 
+def turned(array, precision=None):
+    size = array.shape[0]
+    rows = lax.broadcasted_iota(jnp.int32, (size, size), 0)
+    columns = lax.broadcasted_iota(jnp.int32, (size, size), 1)
+    return dot(array, jnp.where(rows == columns, 1.0, 0.0).astype(array.dtype), TN, precision)
+
+
 def scan_scratch(sizes):
     hops = len(hops_of(sizes))
     keys = HEADS * KEY_DIM
@@ -463,18 +487,21 @@
 
 WEIGHTS = (N.decay_down, N.query, N.key, N.value, N.outgate, N.output, N.gate, N.up, N.down)
 KEPT = WEIGHTS[:5]
-LATE_GATHERED = ()
+LATE_GATHERED = (N.down1,)
+GATHER_ORDER = (0, 3, 2, 1, 4, 5, 10, 6, 7, 12, 9, 11, 8)
 FORWARD_PLAN = (
-    1001, 1011, 1002, 1021, 1012, 1003, 1031, 1013, 1022, 1004, 0, 1032, 1014, 1, 1041, 2,
-    1023, 1024, 3, 1051, 1033, 1042, 1034, 4, 1061, 1052, 1062, 1071, 1043, 1044, 5, 6,
-    1081, 1053, 1072, 100, 1091, 1063, 1054, 7, 1064, 1101, 1082, 200, 101, 1111, 1073, 1092,
-    1121, 1074, 201, 102, 1102, 1083, 1112, 202, 300, 8, 9, 1084, 1122, 1093, 10, 1094,
-    1103, 1104, 11, 1113, 12, 1114, 13, 1123, 15, 1124, 14, 17, 18, 16,
+    1001, 1121, 1031, 1002, 1021, 1011, 1003, 1032, 1022, 1004, 0, 1012, 1, 1041, 1033, 1023,
+    1034, 4, 1013, 1051, 1042, 1024, 3, 1014, 2, 1052, 1101, 1043, 1061, 1102, 1044, 5,
+    6, 1071, 1062, 1053, 100, 1054, 7, 1103, 1072, 1104, 1063, 200, 101, 1081, 1064, 201,
+    102, 1091, 1111, 1073, 1082, 1074, 202, 1122, 300, 8, 1092, 9, 1112, 1083, 1084, 10,
+    1093, 1094, 1113, 11, 1123, 12, 1114, 1124, 14, 2003, 13, 16, 2013, 2002, 17, 15,
+    2012,
 )
 
 
 def forward_kernel(sizes, names, *refs):
     r = SimpleNamespace(**dict(zip(names, refs)))
+    r.mixed_grad, r.outgate_grad, r.middle_b = r.gated, r.normed, r.tokens
     at = coords_of(sizes)
     devices = sizes[0] * sizes[1] * sizes[2] * sizes[3]
     count_rows, width = r.tokens.shape
@@ -484,6 +511,12 @@
     vectors = r.vectors
     per_feature, per_key, per_value = width // devices, keys // devices, VALUE_DIM // devices
 
+    loads = [
+        pltpu.make_async_copy(r.in_tokens, r.tokens, r.input_sem.at[0]),
+        pltpu.make_async_copy(r.in_cotangent, r.cotangent, r.input_sem.at[1]),
+    ]
+    for copy in loads:
+        copy.start()
     tiny = r.tiny_mine
     tiny[...] = jnp.zeros_like(tiny)
     tiny[:, 0:per_key] = r.w_decay_up[...].astype(f32)
@@ -516,9 +549,20 @@
     gather = Gather(
         sizes, at, shards, wholes, (r.send_sem, r.recv_sem, r.own_sem), late
     )
-    gather.begin([index[name] for name in index])
+    gather.begin(GATHER_ORDER)
     scan = scan_of(sizes, False, r)
     saved = []
+    scatter = Scatter(
+        sizes,
+        at,
+        [Item(r.down_grad, 0, size) for _, size in halves(width)],
+        {3: (r.near_down0, r.near_down1), 2: (r.half_down0, r.half_down1)},
+        None,
+        None,
+        (r.back_send_sem, r.back_recv_sem, None, None),
+        (),
+        2,
+    )
 
     def save(*names_of):
         for name in names_of:
@@ -532,6 +576,12 @@
             gather.advance(index[name], 4)
 
     lower = lower_mask()
+
+    def turn(source, target):
+        def columns(k):
+            target[tile(k, 256), :] = turned(source[:, tile(k, 256)]).astype(bf16)
+
+        loop(source.shape[1] // 256, columns)
 
     def unpack():
         need(N.tiny)
@@ -543,12 +593,21 @@
         vectors[3:4, 0:VALUE_DIM] = spread(whole[:, 3], VECTORS, per_value, VALUE_DIM)
         decay_up = r.decay_up
         decay_up[...] = jnp.zeros_like(decay_up)
-        decay_up[0:RANK, :] = spread(
-            whole.reshape(devices * RANK, LANES), 0, per_key, keys
-        ).astype(bf16)
+        lane = lax.broadcasted_iota(jnp.int32, (RANK, LANES), 1)
+        together = LANES // per_key
+        for group in range(keys // LANES):
+            joined = jnp.zeros((RANK, LANES), f32)
+            for k in range(together):
+                block = r.tiny_all[place_of(sizes, group * together + k)]
+                here = (lane >= k * per_key) & (lane < (k + 1) * per_key)
+                joined = jnp.where(here, pltpu.roll(block, k * per_key, 1), joined)
+            decay_up[0:RANK, group * LANES : (group + 1) * LANES] = joined.astype(bf16)
         save(N.vectors, N.decay_up)
 
     def norm():
+        for copy in loads:
+            copy.wait()
+
         def some(k):
             rows = tile(k, 32)
             plain = r.tokens[rows, :].astype(f32)
@@ -557,7 +616,8 @@
             r.grad_b[rows, :] = r.cotangent[rows, :].astype(bf16)
 
         loop(count_rows // 32, some)
-        save(N.normed)
+        turn(r.normed, r.normed_t)
+        save(N.normed_t)
 
     def project(name, into):
         need(name)
@@ -637,7 +697,8 @@
                 ).astype(bf16)
 
         loop(groups, some)
-        save(N.starts, N.gated)
+        turn(r.gated, r.gated_t)
+        save(N.starts, N.gated_t)
 
     def middle():
         need(N.output)
@@ -658,7 +719,8 @@
             r.normed_two[rows, :] = (plain * scale * vectors[1:2, :]).astype(bf16)
 
         loop(count_rows // 32, some)
-        save(N.normed_two)
+        turn(r.normed_two, r.normed_two_t)
+        save(N.normed_two_t)
 
     def up(half):
         need(N.gate + str(half), N.up + str(half))
@@ -675,65 +737,55 @@
 
         loop(size // 256, columns)
 
-    def down_grad():
-        def out(k, slot):
-            return pltpu.make_async_copy(
-                r.panels.at[slot], r.out_down_grad.at[tile(k, 256), :], r.panel_sem.at[slot]
-            )
-
-        def some(k):
-            slot = lax.rem(k, 2)
-
-            @pl.when(k >= 2)
-            def _():
-                out(k - 2, slot).wait()
-
-            left = r.activated[:, tile(k, 256)]
-            r.panels[slot] = dot(left, r.grad_b[...], TN).astype(bf16)
-            out(k, slot).start()
-
-        count = hidden // 256
-        loop(count, some)
-        for k in range(max(count - 2, 0), count):
-            out(k, k % 2).wait()
+    def down_grad(half):
+        if half > 0:
+            scatter.release(half - 1)
+        start, size = halves(width)[half]
+        target = r.down_grad
+        count = 2 if sizes[0] % 2 == 0 else 1
+        some, wide = sizes[0] // count, hidden // count
+        for k in range(count):
+            left = r.activated[:, k * wide : (k + 1) * wide]
+
+            def columns(m, left=left, k=k):
+                made = dot(left, r.grad_b[:, pl.ds(pl.multiple_of(start + m * 256, 256), 256)], TN)
+                shaped = made.reshape((some,) + target.shape[1:5] + (256,))
+                target[k * some : (k + 1) * some, :, :, :, :, tile(m, 256)] = shaped.astype(bf16)
+
+            loop(size // 256, columns)
+        scatter.begin(half)
 
     down = r.all_down
 
-    def act(half):
-        need(N.down + str(half))
-        start, size = halves(width)[half]
-        along = slice(start, start + size)
-        act_grad = r.act_grad
+    def act():
+        need(N.down0, N.down1)
         count = 2 if sizes[0] % 2 == 0 else 1
         some, wide = down.shape[0] // count, hidden // count
         for k in range(count):
-            here = slice(k * wide, (k + 1) * wide)
-            panel = down[k * some : (k + 1) * some, :, :, :, :, along].reshape(wide, size)
-            made = dot(r.grad_b[:, along], panel, NT)
-            act_grad[:, here] = made if half == 0 else act_grad[:, here] + made
-        if half == 0:
-            return
-
-        def finish(k):
+            for start, size in halves(width):
+                along = slice(start, start + size)
+                panel = down[k * some : (k + 1) * some, :, :, :, :, along].reshape(wide, size)
+                made = dot(r.grad_b[:, along], panel, NT)
+                r.act_grad[...] = made if start == 0 else r.act_grad[...] + made
+
+            def finish(m, k=k):
+                here = pl.ds(pl.multiple_of(k * wide + m * 128, 128), 128)
+                grad, gate, line = r.act_grad[:, tile(m, 128)], r.up_gate[:, here], r.up_lin[:, here]
+                sig = jax.nn.sigmoid(gate)
+                r.gate_grad[:, here] = (grad * line * sig * (1.0 + gate * (1.0 - sig))).astype(bf16)
+                r.lin_grad[:, here] = (grad * gate * sig).astype(bf16)
+
+            loop(wide // 128, finish)
+
+    def block():
+        def columns(k):
             here = tile(k, 256)
-            grad, gate, line = act_grad[:, here], r.up_gate[:, here], r.up_lin[:, here]
-            sig = jax.nn.sigmoid(gate)
-            r.gate_grad[:, here] = (grad * line * sig * (1.0 + gate * (1.0 - sig))).astype(bf16)
-            r.lin_grad[:, here] = (grad * gate * sig).astype(bf16)
-
-        loop(hidden // 256, finish)
-
-    def block(half):
-        need(N.down + str(half))
-        start, size = halves(width)[half]
-
-        def columns(k):
-            here = pl.ds(pl.multiple_of(start + k * 256, 256), 256)
-            r.block_output[:, here] = r.middle[:, here] + dot(
+            r.middle[:, here] = r.middle[:, here] + dot(
                 r.activated[...], down[..., here].reshape(hidden, 256), NN
             )
 
-        loop(size // 256, columns)
+        loop(width // 256, columns)
+        save(N.middle)
 
     def feed_back():
         save(N.gate_grad, N.lin_grad)
@@ -760,11 +812,11 @@
             whole = r.cotangent[rows, :] + scale * (
                 grad - plain * jnp.mean(grad * plain, axis=-1, keepdims=True)
             )
-            r.middle_grad[rows, :] = whole
+            r.normed_two_grad[rows, :] = whole
             r.middle_b[rows, :] = whole.astype(bf16)
 
         loop(count_rows // 32, some)
-        save(N.middle_grad, N.middle_b)
+        save(N.normed_two_grad, N.middle_b)
 
     def heads_back():
         side = r.side
@@ -774,12 +826,12 @@
             across, along = head_slices(h)
             first, count = h * VALUE_DIM // part, max(VALUE_DIM // part, 1)
             weight = r.all_output[first : first + count].reshape(count * part, width)
-            r.gated_grad[...] = dot(r.middle_b[...], weight, NT)
+            r.act_grad[:, 0:VALUE_DIM] = dot(r.middle_b[...], weight, NT)
 
             def some(k, along=along):
                 rows = tile(k, GROUP)
                 whole, gate = r.mixed[rows, along], r.gate_pre[rows, along]
-                grad = r.gated_grad[rows, :]
+                grad = r.act_grad[rows, 0:VALUE_DIM]
                 scale = lax.rsqrt(jnp.mean(whole * whole, axis=-1, keepdims=True) + epsilon)
                 sig = jax.nn.sigmoid(gate)
                 plain = whole * scale
@@ -811,11 +863,10 @@
         middle=middle,
         up0=lambda: up(0),
         up1=lambda: up(1),
-        down_grad=down_grad,
-        act0=lambda: act(0),
-        act1=lambda: act(1),
-        block0=lambda: block(0),
-        block1=lambda: block(1),
+        down_grad0=lambda: down_grad(0),
+        down_grad1=lambda: down_grad(1),
+        act=act,
+        block=block,
         feed_back=feed_back,
         heads_back=heads_back,
     )
@@ -823,22 +874,23 @@
         FORWARD_PLAN,
         pieces,
         scan,
-        list(index),
-        lambda name, step: gather.advance(index[name], step),
-    )
-    save(N.block_output)
+        lambda item, step: gather.advance(item, step),
+        lambda item, step: scatter.advance(item, step),
+    )
+    scatter.finish()
+    save(N.near_down0, N.near_down1)
     gather.finish()
     scan.finish()
     for copy in saved:
         copy.wait()
 
 
-def run_plan(plan, pieces, scan, names, advance):
+def run_plan(plan, pieces, scan, gather, scatter):
     hops = len(scan.hops)
     steps = list(pieces.values())
     for code in plan:
         if code >= 1000:
-            advance(names[(code - 1000) // 10], code % 10)
+            (gather if code < 2000 else scatter)(code % 1000 // 10, code % 10)
         elif code < 100:
             steps[code]()
         elif code == 300:
@@ -867,6 +919,19 @@
     return dict(zip(outs, results))
 
 
+LANDINGS = {3: N.near_, 2: N.half_, 1: N.part_, 0: N.last_}
+
+
+def landings(sizes, block, dtype, name, late, steps):
+    order = orders_of(sizes, late)[0]
+    made = {}
+    for step in steps:
+        lead = tuple(sizes[k] for k in order[:step])
+        lead = sizes[:3] if step == 3 else (max(sizes[order[step]] - 1, 1),) + lead
+        made[LANDINGS[step] + name] = pltpu.VMEM(lead + block, dtype)
+    return made
+
+
 def forward(sizes, tokens, cotangent, small, weights):
     rows, width = tokens.shape
     keys, values = HEADS * KEY_DIM, HEADS * VALUE_DIM
@@ -874,72 +939,81 @@
     groups = rows // GROUP
     most = max(max(sizes) - 1, 1)
     mine = weights[N.query].shape[0]
-    ins = {N.tokens: (tokens, True), N.cotangent: (cotangent, True)}
+    ins = {N.in_tokens: (tokens, False), N.in_cotangent: (cotangent, False)}
     ins.update({name: (a, True) for name, a in small.items()})
-    ins.update({N.w_ + name: (a, True) for name, a in weights.items()})
+    ins.update({N.w_ + name: (a, name == N.decay_down) for name, a in weights.items()})
     shape_of = {name: sizes + a.shape for name, a in weights.items()}
     shape_of[N.decay_down] = sizes + (mine, LANES)
     made = dict(
         vectors=((8, width), f32),
         decay_up=((LANES, keys), bf16),
-        normed=((rows, width), bf16),
+        normed_t=((width, rows), bf16),
         rank_act=((rows, LANES), bf16),
         decay_pre=((rows, keys), f32),
         query=((rows, keys), bf16),
         key=((rows, keys), bf16),
         value=((rows, values), bf16),
         starts=((groups, HEADS, VALUE_DIM, KEY_DIM), bf16),
-        gated=((rows, values), bf16),
-        normed_two=((rows, width), bf16),
+        gated_t=((values, rows), bf16),
+        normed_two_t=((width, rows), bf16),
         gate_grad=((rows, hidden), bf16),
         lin_grad=((rows, hidden), bf16),
-        middle_grad=((rows, width), f32),
+        normed_two_grad=((rows, width), f32),
         middle_b=((rows, width), bf16),
         mixed_grad=((rows, values), bf16),
         outgate_grad=((rows, values), bf16),
         side=((8, width), f32),
-        block_output=((rows, width), f32),
-    )
+        middle=((rows, width), f32),
+    )
+    for k, (_, size) in enumerate(halves(width)):
+        made[N.near_down + str(k)] = (sizes[:3] + (weights[N.down].shape[0], size), bf16)
     outs = {N.out_weight_ + name: (shape_of[name], bf16, False) for name in KEPT}
     outs.update({N.out_ + name: o + (False,) for name, o in made.items()})
-    outs[N.out_down_grad] = ((hidden, width), bf16, False)
     scratch = {N.all_ + name: pltpu.VMEM(shape_of[name], bf16) for name in WEIGHTS}
-    scratch.update({name: pltpu.VMEM(*o) for name, o in made.items()})
+    shared = (N.mixed_grad, N.outgate_grad, N.middle_b)
+    scratch.update({name: pltpu.VMEM(*o) for name, o in made.items() if name not in shared})
     scratch.update(
+        tokens=pltpu.VMEM((rows, width), tokens.dtype),
+        cotangent=pltpu.VMEM((rows, width), f32),
+        input_sem=pltpu.SemaphoreType.DMA((2,)),
         tiny_mine=pltpu.VMEM((RANK, LANES), f32),
         tiny_all=pltpu.VMEM(sizes + (RANK, LANES), f32),
         down_mine=pltpu.VMEM((mine, LANES), bf16),
         grad_b=pltpu.VMEM((rows, width), bf16),
+        normed=pltpu.VMEM((rows, width), bf16),
+        gated=pltpu.VMEM((rows, values), bf16),
+        normed_two=pltpu.VMEM((rows, width), bf16),
         gate_pre=pltpu.VMEM((rows, values), f32),
         query_dev=pltpu.VMEM((rows, keys), f32),
         offsets=pltpu.VMEM((groups, 8, keys), f32),
         mixed=pltpu.VMEM((rows, values), f32),
-        middle=pltpu.VMEM((rows, width), f32),
         up_gate=pltpu.VMEM((rows, hidden), f32),
         up_lin=pltpu.VMEM((rows, hidden), f32),
         activated=pltpu.VMEM((rows, hidden), bf16),
-        act_grad=pltpu.VMEM((rows, hidden), f32),
-        panels=pltpu.VMEM((2, 256, width), bf16),
-        normed_two_grad=pltpu.VMEM((rows, width), f32),
-        gated_grad=pltpu.VMEM((rows, VALUE_DIM), f32),
+        act_grad=pltpu.VMEM((rows, hidden // (2 if sizes[0] % 2 == 0 else 1)), f32),
+        down_grad=pltpu.VMEM(sizes + (weights[N.down].shape[0], halves(width)[0][1]), bf16),
         send_sem=pltpu.SemaphoreType.DMA((13, 4, most)),
         recv_sem=pltpu.SemaphoreType.DMA((13, 4, most)),
         own_sem=pltpu.SemaphoreType.DMA((13,)),
         save_sem=pltpu.SemaphoreType.DMA((len(made) + len(KEPT),)),
-        panel_sem=pltpu.SemaphoreType.DMA((2,)),
-    )
+        back_send_sem=pltpu.SemaphoreType.DMA((2, 4, most)),
+        back_recv_sem=pltpu.SemaphoreType.DMA((2, 4, most)),
+    )
+    for k, (_, size) in enumerate(halves(width)):
+        block = (weights[N.down].shape[0], size)
+        scratch.update(landings(sizes, block, bf16, N.down + str(k), False, (2,)))
     scratch.update(scan_scratch(sizes))
     results = kernel_call(forward_kernel, sizes, ins, outs, scratch, 0)
     return {name[4:]: a for name, a in results.items()}
 
 
-LATE_SCATTERED = (N.output,)
+LATE_SCATTERED = (N.decay_down,)
 BACKWARD_PLAN = (
-    0, 100, 2, 3, 1003, 6, 1013, 7, 200, 1023, 101, 4, 1033, 5, 1063, 1002,
-    1073, 201, 102, 1043, 1053, 1012, 1001, 1011, 1022, 1062, 1032, 1021, 202, 300, 1, 1031,
-    1072, 1000, 10, 8, 9, 1042, 11, 12, 1083, 1093, 1010, 1103, 1071, 1113, 13, 1020,
-    1052, 1041, 1123, 1061, 1030, 1051, 1060, 1082, 1070, 1092, 1081, 1040, 1102, 1112, 1091, 1122,
-    1050, 1101, 1111, 1121, 1080, 1090, 1100, 1110, 1120,
+    0, 100, 2, 3, 6, 2001, 7, 2023, 4, 2033, 5, 2011, 2063, 2073, 2000, 200,
+    2043, 2022, 101, 2053, 2010, 2032, 201, 102, 2021, 2062, 2031, 202, 2072, 300, 1, 2061,
+    2020, 2071, 10, 8, 9, 11, 12, 2030, 2042, 2083, 2093, 2103, 2113, 2060, 2070, 2052,
+    13, 2123, 2112, 2041, 2082, 2092, 2051, 2040, 2102, 2081, 2122, 2111, 2050, 2091, 2101, 2121,
+    2110, 2080, 2090, 2100, 2120,
 )
 NORMED_BACK = (
     (N.decay_down, N.rank_grad),
@@ -953,12 +1027,12 @@
     N.decay_pre,
     N.mixed_grad,
     N.vectors,
-    N.normed_two,
+    N.normed_two_t,
     N.gate_grad,
     N.lin_grad,
-    N.gated,
+    N.gated_t,
     N.middle_b,
-    N.normed,
+    N.normed_t,
     N.outgate_grad,
     N.key,
     N.value,
@@ -1008,9 +1082,12 @@
         )
         loads[name].start()
     middle_load = pltpu.make_async_copy(
-        r.in_middle_grad, r.input_grad, r.load_sem.at[len(loads)]
+        r.in_normed_two_grad, r.input_grad, r.load_sem.at[len(loads)]
     )
     middle_load.start()
+    result = pltpu.make_async_copy(
+        r.input_grad, r.out_input_grad, r.out_sem.at[r.out_sem.shape[0] - 1]
+    )
 
     def ready(*names_of):
         for name in names_of:
@@ -1020,28 +1097,28 @@
     greet(sizes, at)
     items = scatter_items(hidden, width)
     index = {name: k for k, name in enumerate(items)}
-    sources, stages, sums = {}, {}, {}
+    sources, sums, outs = {}, {}, {}
     for name, (size, slot, out, start) in items.items():
         k = index[name]
-        if slot is None:
-            sources[k] = Item(r.in_down_grad, start, size)
-            stages[k] = getattr(r, N.stage_ + name)
-        else:
+        if slot is not None:
             sources[k] = Item(getattr(r, N.slot_ + slot), 0, size)
         sums[k] = Item(getattr(r, N.sum_ + out), start, size)
+        outs[k] = Item(getattr(r, N.out_ + out), start, size)
     scatter = Scatter(
         sizes,
         at,
         sources,
-        stages,
-        [getattr(r, N.near_ + name) for name in items],
-        [getattr(r, N.half_ + name) for name in items],
-        [getattr(r, N.part_ + name) for name in items],
-        [getattr(r, N.last_ + name) for name in items],
+        {
+            step: [getattr(r, kind + name, None) for name in items]
+            for step, kind in LANDINGS.items()
+        },
         sums,
-        (r.send_sem, r.recv_sem, r.own_sem),
+        outs,
+        (r.send_sem, r.recv_sem, r.own_sem, r.out_sem),
         {index[name] for name in LATE_SCATTERED},
     )
+    for k in range(2):
+        scatter.resume(index[N.down + str(k)], getattr(r, N.in_near_down + str(k)))
     scan = scan_of(sizes, True, r)
     in_slot = {}
 
@@ -1053,26 +1130,18 @@
         return getattr(r, N.slot_ + slot)
 
     lower = lower_mask()
-    scatter.begin(index[N.down0])
-    scatter.begin(index[N.down1])
 
     def weight_grad(name, left, right, start=0):
         ready(left, right)
         target, columns_of = take_slot(name), items[name][0]
         size = min(columns_of, 256)
 
-        def features(a):
-            transposed = getattr(r, left)[:, tile(a, part)]
-
-            def columns(k):
-                here = pl.ds(pl.multiple_of(start + k * size, size), size)
-                made = dot(transposed, getattr(r, right)[:, here], TN)
-                shaped = made.reshape(target.shape[1:5] + (size,))
-                target[a, :, :, :, :, tile(k, size)] = shaped.astype(bf16)
-
-            loop(columns_of // size, columns)
-
-        loop(sizes[0], features)
+        def columns(k):
+            here = pl.ds(pl.multiple_of(start + k * size, size), size)
+            made = dot(getattr(r, left)[...], getattr(r, right)[:, here], NN)
+            target[..., tile(k, size)] = made.reshape(target.shape[:5] + (size,)).astype(bf16)
+
+        loop(columns_of // size, columns)
         scatter.begin(index[name])
 
     def begin_state():
@@ -1157,7 +1226,7 @@
     def decay_down():
         ready(N.decay_up)
         r.rank_grad[...] = dot(r.decay_grad[...], r.decay_up[...], NT).astype(bf16)
-        weight_grad(N.decay_down, N.normed, N.rank_grad)
+        weight_grad(N.decay_down, N.normed_t, N.rank_grad)
 
     def input_grad():
         def panel(a, slot):
@@ -1207,6 +1276,7 @@
             )
 
         loop(count_rows // 32, some)
+        result.start()
 
     def tiny():
         ready(N.rank_act, N.side)
@@ -1233,26 +1303,22 @@
                 wide = jnp.broadcast_to(vector, (RANK, vector.shape[1]))
                 here = (row == k) & (lane >= VECTORS) & (lane < VECTORS + per)
                 whole = jnp.where(here, cut(wide, device, per, VECTORS), whole)
-            place, rest = [], device
-            for size in reversed(sizes):
-                rest, last = divmod(rest, size)
-                place.insert(0, last)
-            target[tuple(place)] = whole
+            target[place_of(sizes, device)] = whole
         scatter.begin(index[N.tiny])
 
     first = halves(hidden)[1][0]
     pieces = dict(
         state=begin_state,
         attention=attention,
-        gate0=lambda: weight_grad(N.gate0, N.normed_two, N.gate_grad),
-        gate1=lambda: weight_grad(N.gate1, N.normed_two, N.gate_grad, first),
-        up0=lambda: weight_grad(N.up0, N.normed_two, N.lin_grad),
-        up1=lambda: weight_grad(N.up1, N.normed_two, N.lin_grad, first),
-        output=lambda: weight_grad(N.output, N.gated, N.middle_b),
-        outgate=lambda: weight_grad(N.outgate, N.normed, N.outgate_grad),
-        query=lambda: weight_grad(N.query, N.normed, N.query_grad),
-        key=lambda: weight_grad(N.key, N.normed, N.key_grad),
-        value=lambda: weight_grad(N.value, N.normed, N.value_grad),
+        gate0=lambda: weight_grad(N.gate0, N.normed_two_t, N.gate_grad),
+        gate1=lambda: weight_grad(N.gate1, N.normed_two_t, N.gate_grad, first),
+        up0=lambda: weight_grad(N.up0, N.normed_two_t, N.lin_grad),
+        up1=lambda: weight_grad(N.up1, N.normed_two_t, N.lin_grad, first),
+        output=lambda: weight_grad(N.output, N.gated_t, N.middle_b),
+        outgate=lambda: weight_grad(N.outgate, N.normed_t, N.outgate_grad),
+        query=lambda: weight_grad(N.query, N.normed_t, N.query_grad),
+        key=lambda: weight_grad(N.key, N.normed_t, N.key_grad),
+        value=lambda: weight_grad(N.value, N.normed_t, N.value_grad),
         decay_down=decay_down,
         input_grad=input_grad,
         tiny=tiny,
@@ -1261,12 +1327,13 @@
         BACKWARD_PLAN,
         pieces,
         scan,
-        list(items),
-        lambda name, step: scatter.advance(index[name], step),
+        None,
+        lambda item, step: scatter.advance(item, step),
     )
     scatter.finish()
     scan.finish()
     ready(*list(loads))
+    result.wait()
 
 
 def backward(sizes, tokens, saved):
@@ -1276,29 +1343,27 @@
     rows, width = tokens.shape
     hidden = saved[N.gate_grad].shape[1]
     keys, values = HEADS * KEY_DIM, HEADS * VALUE_DIM
-    mine, mine_down = width // devices, hidden // devices
-    down_grad = saved[N.down_grad].reshape(sizes + (mine_down, width))
+    mine = width // devices
     saved = dict(saved, tokens=tokens)
     ins = {N.in_ + name: (saved[name], False) for name in LOADED}
-    ins[N.in_middle_grad] = (saved[N.middle_grad], False)
-    ins[N.in_down_grad] = (down_grad, False)
+    ins[N.in_normed_two_grad] = (saved[N.normed_two_grad], False)
+    for k in range(2):
+        ins[N.in_near_down + str(k)] = (saved[N.near_down + str(k)], False)
     ins.update({N.in_weight_ + name: (saved[N.weight_ + name], False) for name in KEPT})
     items = scatter_items(hidden, width)
     block, scratch, sums = {}, {}, {}
     for name, (size, slot, out, start) in items.items():
-        rows_of = {N.down: mine_down, N.tiny: RANK}.get(out, mine)
+        rows_of = RANK if out == N.tiny else mine
+        if slot is None:
+            rows_of = saved[N.near_down0].shape[3]
         dtype = f32 if out == N.tiny else bf16
         block = (rows_of, size)
-        sums[N.sum_ + out] = ((rows_of, start + size), f32, True)
-        if slot is None:
-            scratch[N.stage_ + name] = pltpu.VMEM((2, inner, side) + block, dtype)
-        elif N.slot_ + slot not in scratch:
+        sums[N.out_ + out] = ((rows_of, start + size), f32, False)
+        scratch[N.sum_ + out] = pltpu.VMEM((rows_of, start + size), f32)
+        if slot is not None and N.slot_ + slot not in scratch:
             scratch[N.slot_ + slot] = pltpu.VMEM(sizes + block, dtype)
-        scratch[N.near_ + name] = pltpu.VMEM((outer, inner, side) + block, dtype)
-        order = orders_of(sizes, name in LATE_SCATTERED)[0]
-        for step, landing in ((2, N.half_), (1, N.part_), (0, N.last_)):
-            lead = (max(sizes[order[step]] - 1, 1),) + tuple(sizes[k] for k in order[:step])
-            scratch[landing + name] = pltpu.VMEM(lead + block, dtype)
+        steps = (3, 1, 0) if slot is None else (3, 2, 1, 0)
+        scratch.update(landings(sizes, block, dtype, name, name in LATE_SCATTERED, steps))
     scratch.update({n: pltpu.VMEM(saved[n].shape, saved[n].dtype) for n in LOADED})
     scratch.update(
         {
@@ -1317,45 +1382,47 @@
         normed_grad=pltpu.VMEM((rows, width), f32),
         send_sem=pltpu.SemaphoreType.DMA((len(items), 4, most)),
         recv_sem=pltpu.SemaphoreType.DMA((len(items), 4, most)),
-        own_sem=pltpu.SemaphoreType.DMA((len(items), 2)),
+        input_grad=pltpu.VMEM((rows, width), f32),
+        own_sem=pltpu.SemaphoreType.DMA((2,)),
+        out_sem=pltpu.SemaphoreType.DMA((len(items) + 1,)),
         load_sem=pltpu.SemaphoreType.DMA((len(LOADED) + 1,)),
         panel_sem=pltpu.SemaphoreType.DMA((len(NORMED_BACK), 2)),
     )
     scratch.update(scan_scratch(sizes))
-    outs = dict(sums, input_grad=((rows, width), f32, True))
+    outs = dict(sums, out_input_grad=((rows, width), f32, False))
     return kernel_call(backward_kernel, sizes, ins, outs, scratch, 1)
-
-
-def turned(array, precision=None):
-    size = array.shape[0]
-    rows = lax.broadcasted_iota(jnp.int32, (size, size), 0)
-    columns = lax.broadcasted_iota(jnp.int32, (size, size), 1)
-    return dot(array, jnp.where(rows == columns, 1.0, 0.0).astype(array.dtype), TN, precision)
 
 
 def hand_out_kernel(count, cuts, *refs):
     whole, down, tiny = refs[:count], refs[count], refs[count + 1]
-    outs, small, sems = refs[count + 2 : 2 * count + 2], refs[2 * count + 2 : -1], refs[-1]
-    copies = []
-    for k, (source, target) in enumerate(zip(whole, outs)):
-        copies.append(pltpu.make_async_copy(source, target, sems.at[k]))
-        copies[-1].start()
+    refs = refs[count + 2 :]
+    outs, small, held, sems = refs[:count], refs[count : -count - 1], refs[-count - 1 : -1], refs[-1]
+    loads, copies = [], []
+    for k in range(count):
+        loads.append(pltpu.make_async_copy(whole[k], held[k], sems.at[0, k]))
+        loads[-1].start()
+        copies.append(pltpu.make_async_copy(held[k], outs[k], sems.at[1, k]))
     small[0][...] = turned(down[...], highest)[0 : small[0].shape[0]]
     for target, (row, column) in zip(small[1:], cuts):
         target[...] = tiny[row : row + target.shape[0], column : column + target.shape[1]]
+    for load, copy in zip(loads, copies):
+        load.wait()
+        copy.start()
     for copy in copies:
         copy.wait()
 
 
 def hand_out(arrays, decay_down, tiny, cuts):
     vmem = pl.BlockSpec(memory_space=pltpu.VMEM)
+    anywhere = pl.BlockSpec(memory_space=pl.ANY)
     shapes = [a.shape for a in arrays] + [(RANK, decay_down.shape[0])] + [c[0] for c in cuts]
     return pl.pallas_call(
         functools.partial(hand_out_kernel, len(arrays), [c[1] for c in cuts]),
         out_shape=[jax.ShapeDtypeStruct(s, f32) for s in shapes],
-        in_specs=[vmem] * (len(arrays) + 2),
-        out_specs=[pl.BlockSpec(memory_space=pl.ANY)] * len(arrays) + [vmem] * (len(cuts) + 1),
-        scratch_shapes=[pltpu.SemaphoreType.DMA((len(arrays),))],
+        in_specs=[anywhere] * len(arrays) + [vmem] * 2,
+        out_specs=[anywhere] * len(arrays) + [vmem] * (len(cuts) + 1),
+        scratch_shapes=[pltpu.VMEM(a.shape, f32) for a in arrays]
+        + [pltpu.SemaphoreType.DMA((2, len(arrays)))],
         compiler_params=pltpu.CompilerParams(vmem_limit_bytes=VMEM_LIMIT),
     )(*arrays, decay_down, tiny)
 
@@ -1409,9 +1476,10 @@
     got = backward(sizes, tokens, saved)
     names = (N.query, N.key, N.value, N.outgate, N.output, N.gate, N.up, N.down)
     handed = hand_out(
-        [saved[N.block_output], got[N.input_grad]] + [got[N.sum_ + name] for name in names],
-        got[N.sum_decay_down],
-        got[N.sum_tiny],
+        [saved[N.middle], got[N.out_input_grad]]
+        + [got[N.out_ + name] for name in names],
+        got[N.out_decay_down],
+        got[N.out_tiny],
         (
             ((RANK, per_key), (0, 0)),
             ((1, per_feature), (0, VECTORS)),

time: 308 us -> 283 us (0.919)
  Pallas kernels: 304 us -> 282 us
    pallas_call x2, Pallas kernels: 300 us -> 277 us  [kernel_call(): pl.pallas_call(functools.partial(body, sizes, names), out_shape=[jax.Shap...]
where the time goes in v4:
time: 283 us
  Pallas kernels  282 us (100%)
    pallas_call x2, Pallas kernels, kernel_call(): pl.pallas_call(functools.partial(body, sizes, names), out_shape=[jax.Shap...  277 us

profile of v4, /device:TPU:0, one launch (start us, length us, event | category | flops | bytes accessed | tf_op | source)
XLA Modules:
  0.0 282.5 jit_solution(2045022331024955142)
XLA Ops:
  0.7 150.1 %shard_map.279 = (bf16[4,2,2,2,32,128]{5,4,3,2,1,0:T(8,128)(2,1)}, bf16[4,2,2,2,32,512]{5,4,3,2,1,0:T(8,128)(2,1)}, bf16[4,2,2,2,32,512]{5,4,3,2,1,0:T(8,128)(2,...) custom-call(bf16[256,1024]{1,0:T(8,128)(2,1)} %bitcast.14, ...), custom_call_target="tpu_custom_call" | custom-call | tf_op jit(solution)/shard_map/pallas_call | solution.py:909
  150.7 127.0 %shard_map.280 = (f32[88,1024]{1,0:T(8,128)}, f32[32,2816]{1,0:T(8,128)}, f32[32,2816]{1,0:T(8,128)}, f32[32,1024]{1,0:T(8,128)}, f32[32,1024]{1,0:T(8,128)}, /*...) custom-call(bf16[256,512]{1,0:T(8,128)(2,1)} %get-tuple-element.70.r, ...), custom_call_target="tpu_custom_call" | custom-call | tf_op jit(solution)/shard_map/pallas_call | solution.py:909
  277.8 4.6 %shard_map.281 = (f32[256,1024]{1,0:T(8,128)}, f32[256,1024]{1,0:T(8,128)}, f32[32,512]{1,0:T(8,128)}, f32[32,512]{1,0:T(8,128)}, f32[32,1024]{1,0:T(8,128)}, /*...) custom-call(f32[256,1024]{1,0:T(8,128)} %get-tuple-element.69.refs_0, ...), custom_call_target="tpu_custom_call" | custom-call | tf_op jit(solution)/shard_map/pallas_call | solution.py:1419

commit v5 on v4

--- a/solution.py
+++ b/solution.py
@@ -105,12 +105,17 @@
         pl.when(at[3] == parity)(functools.partial(act, order))
 
 
-def loop(count, body):
+def loop(count, body, together=1):
+    together = min(together, count)
+    while count % together:
+        together -= 1
+
     def step(k, carry):
-        body(k)
+        for j in range(together):
+            body(k * together + j)
         return carry
 
-    lax.fori_loop(0, count, step, 0)
+    lax.fori_loop(0, count // together, step, 0)
 
 
 def dot(left, right, dims, precision=None):
@@ -437,10 +442,10 @@
 
 
 def turned(array, precision=None):
-    size = array.shape[0]
+    size = array.shape[1]
     rows = lax.broadcasted_iota(jnp.int32, (size, size), 0)
     columns = lax.broadcasted_iota(jnp.int32, (size, size), 1)
-    return dot(array, jnp.where(rows == columns, 1.0, 0.0).astype(array.dtype), TN, precision)
+    return dot(jnp.where(rows == columns, 1.0, 0.0).astype(array.dtype), array, NT, precision)
 
 
 def scan_scratch(sizes):
@@ -494,7 +499,7 @@
     1034, 4, 1013, 1051, 1042, 1024, 3, 1014, 2, 1052, 1101, 1043, 1061, 1102, 1044, 5,
     6, 1071, 1062, 1053, 100, 1054, 7, 1103, 1072, 1104, 1063, 200, 101, 1081, 1064, 201,
     102, 1091, 1111, 1073, 1082, 1074, 202, 1122, 300, 8, 1092, 9, 1112, 1083, 1084, 10,
-    1093, 1094, 1113, 11, 1123, 12, 1114, 1124, 14, 2003, 13, 16, 2013, 2002, 17, 15,
+    1093, 1094, 1113, 11, 12, 1123, 2003, 13, 1114, 2013, 1124, 14, 16, 2002, 17, 15,
     2012,
 )
 
@@ -615,7 +620,7 @@
             r.normed[rows, :] = (plain * scale * vectors[0:1, :]).astype(bf16)
             r.grad_b[rows, :] = r.cotangent[rows, :].astype(bf16)
 
-        loop(count_rows // 32, some)
+        loop(count_rows // 32, some, 4)
         turn(r.normed, r.normed_t)
         save(N.normed_t)
 
@@ -671,7 +676,7 @@
                 )
             total[...] = total[...] + ending
 
-        loop(groups, group)
+        loop(groups, group, 2)
         total[...] = jnp.exp(total[...])
         save(N.query, N.key, N.value)
 
@@ -696,7 +701,7 @@
                     whole * scale * vectors[3:4, 0:VALUE_DIM] * swish
                 ).astype(bf16)
 
-        loop(groups, some)
+        loop(groups, some, 2)
         turn(r.gated, r.gated_t)
         save(N.starts, N.gated_t)
 
@@ -718,7 +723,7 @@
             scale = lax.rsqrt(jnp.mean(plain * plain, axis=-1, keepdims=True) + epsilon)
             r.normed_two[rows, :] = (plain * scale * vectors[1:2, :]).astype(bf16)
 
-        loop(count_rows // 32, some)
+        loop(count_rows // 32, some, 4)
         turn(r.normed_two, r.normed_two_t)
         save(N.normed_two_t)
 
@@ -733,7 +738,8 @@
             line = dot(normed_two, r.all_up[..., here].reshape(width, 256), NN)
             r.up_gate[:, here] = gate
             r.up_lin[:, here] = line
-            r.activated[:, here] = (gate * jax.nn.sigmoid(gate) * line).astype(bf16)
+            activated = (gate * jax.nn.sigmoid(gate) * line).astype(bf16)
+            r.activated_t[here, :] = turned(activated).astype(bf16)
 
         loop(size // 256, columns)
 
@@ -745,10 +751,10 @@
         count = 2 if sizes[0] % 2 == 0 else 1
         some, wide = sizes[0] // count, hidden // count
         for k in range(count):
-            left = r.activated[:, k * wide : (k + 1) * wide]
+            left = r.activated_t[k * wide : (k + 1) * wide, :]
 
             def columns(m, left=left, k=k):
-                made = dot(left, r.grad_b[:, pl.ds(pl.multiple_of(start + m * 256, 256), 256)], TN)
+                made = dot(left, r.grad_b[:, pl.ds(pl.multiple_of(start + m * 256, 256), 256)], NN)
                 shaped = made.reshape((some,) + target.shape[1:5] + (256,))
                 target[k * some : (k + 1) * some, :, :, :, :, tile(m, 256)] = shaped.astype(bf16)
 
@@ -775,13 +781,13 @@
                 r.gate_grad[:, here] = (grad * line * sig * (1.0 + gate * (1.0 - sig))).astype(bf16)
                 r.lin_grad[:, here] = (grad * gate * sig).astype(bf16)
 
-            loop(wide // 128, finish)
+            loop(wide // 128, finish, 2)
 
     def block():
         def columns(k):
             here = tile(k, 256)
             r.middle[:, here] = r.middle[:, here] + dot(
-                r.activated[...], down[..., here].reshape(hidden, 256), NN
+                r.activated_t[...], down[..., here].reshape(hidden, 256), TN
             )
 
         loop(width // 256, columns)
@@ -815,7 +821,7 @@
             r.normed_two_grad[rows, :] = whole
             r.middle_b[rows, :] = whole.astype(bf16)
 
-        loop(count_rows // 32, some)
+        loop(count_rows // 32, some, 4)
         save(N.normed_two_grad, N.middle_b)
 
     def heads_back():
@@ -847,7 +853,7 @@
                     grad * plain * gain * sig * (1.0 + gate * (1.0 - sig))
                 ).astype(bf16)
 
-            loop(groups, some)
+            loop(groups, some, 4)
         save(N.mixed_grad, N.outgate_grad, N.side)
 
     pieces = dict(
@@ -989,7 +995,7 @@
         mixed=pltpu.VMEM((rows, values), f32),
         up_gate=pltpu.VMEM((rows, hidden), f32),
         up_lin=pltpu.VMEM((rows, hidden), f32),
-        activated=pltpu.VMEM((rows, hidden), bf16),
+        activated_t=pltpu.VMEM((hidden, rows), bf16),
         act_grad=pltpu.VMEM((rows, hidden // (2 if sizes[0] % 2 == 0 else 1)), f32),
         down_grad=pltpu.VMEM(sizes + (weights[N.down].shape[0], halves(width)[0][1]), bf16),
         send_sem=pltpu.SemaphoreType.DMA((13, 4, most)),
@@ -1009,11 +1015,11 @@
 
 LATE_SCATTERED = (N.decay_down,)
 BACKWARD_PLAN = (
-    0, 100, 2, 3, 6, 2001, 7, 2023, 4, 2033, 5, 2011, 2063, 2073, 2000, 200,
-    2043, 2022, 101, 2053, 2010, 2032, 201, 102, 2021, 2062, 2031, 202, 2072, 300, 1, 2061,
-    2020, 2071, 10, 8, 9, 11, 12, 2030, 2042, 2083, 2093, 2103, 2113, 2060, 2070, 2052,
-    13, 2123, 2112, 2041, 2082, 2092, 2051, 2040, 2102, 2081, 2122, 2111, 2050, 2091, 2101, 2121,
-    2110, 2080, 2090, 2100, 2120,
+    0, 100, 3, 6, 7, 2, 2001, 2033, 5, 2011, 2023, 4, 2000, 2053, 2032, 200,
+    101, 2063, 2043, 2010, 2031, 201, 102, 2022, 2030, 2052, 2021, 2062, 202, 2051, 300, 1,
+    2073, 2061, 2042, 2020, 10, 8, 11, 9, 12, 2050, 2083, 2072, 2060, 2093, 2113, 2103,
+    2041, 13, 2112, 2123, 2071, 2082, 2040, 2092, 2081, 2070, 2091, 2102, 2111, 2122, 2101, 2110,
+    2121, 2080, 2090, 2100, 2120,
 )
 NORMED_BACK = (
     (N.decay_down, N.rank_grad),
@@ -1158,7 +1164,7 @@
             query_dev[rows, :] = (query_scaled * jnp.exp(cumulative + total[0:1, :])).astype(bf16)
             total[...] = total[...] + cumulative[GROUP - 1 :]
 
-        loop(groups, some)
+        loop(groups, some, 4)
         for h in range(HEADS):
             across, along = head_slices(h)
             state[h] = dot(r.mixed_grad[:, along], query_dev[:, across], TN)
@@ -1221,7 +1227,7 @@
             )
             r.decay_grad[rows, :] = to_decay.astype(bf16)
 
-        loop(groups, group)
+        loop(groups, group, 2)
 
     def decay_down():
         ready(N.decay_up)
@@ -1275,7 +1281,7 @@
                 grad - plain * jnp.mean(grad * plain, axis=-1, keepdims=True)
             )
 
-        loop(count_rows // 32, some)
+        loop(count_rows // 32, some, 4)
         result.start()
 
     def tiny():

time: 283 us -> 276 us (0.975)
  Pallas kernels: 282 us -> 275 us
    pallas_call x2, Pallas kernels: 277 us -> 271 us  [kernel_call(): pl.pallas_call(functools.partial(body, sizes, names), out_shape=[jax.Shap...]
where the time goes in v5:
time: 276 us
  Pallas kernels  275 us (100%)
    pallas_call x2, Pallas kernels, kernel_call(): pl.pallas_call(functools.partial(body, sizes, names), out_shape=[jax.Shap...  271 us

profile of v5, /device:TPU:0, one launch (start us, length us, event | category | flops | bytes accessed | tf_op | source)
XLA Modules:
  0.0 276.1 jit_solution(3343013572489957961)
XLA Ops:
  0.7 148.3 %shard_map.279 = (bf16[4,2,2,2,32,128]{5,4,3,2,1,0:T(8,128)(2,1)}, bf16[4,2,2,2,32,512]{5,4,3,2,1,0:T(8,128)(2,1)}, bf16[4,2,2,2,32,512]{5,4,3,2,1,0:T(8,128)(2,...) custom-call(bf16[256,1024]{1,0:T(8,128)(2,1)} %bitcast.14, ...), custom_call_target="tpu_custom_call" | custom-call | tf_op jit(solution)/shard_map/pallas_call | solution.py:915
  149.0 122.4 %shard_map.280 = (f32[88,1024]{1,0:T(8,128)}, f32[32,2816]{1,0:T(8,128)}, f32[32,2816]{1,0:T(8,128)}, f32[32,1024]{1,0:T(8,128)}, f32[32,1024]{1,0:T(8,128)}, /*...) custom-call(bf16[256,512]{1,0:T(8,128)(2,1)} %get-tuple-element.70.r, ...), custom_call_target="tpu_custom_call" | custom-call | tf_op jit(solution)/shard_map/pallas_call | solution.py:915
  271.4 4.6 %shard_map.281 = (f32[256,1024]{1,0:T(8,128)}, f32[256,1024]{1,0:T(8,128)}, f32[32,512]{1,0:T(8,128)}, f32[32,512]{1,0:T(8,128)}, f32[32,1024]{1,0:T(8,128)}, /*...) custom-call(f32[256,1024]{1,0:T(8,128)} %get-tuple-element.69.refs_0, ...), custom_call_target="tpu_custom_call" | custom-call | tf_op jit(solution)/shard_map/pallas_call | solution.py:1425

commit v6 on v5

--- a/solution.py
+++ b/solution.py
@@ -55,6 +55,10 @@
         device, last = divmod(device, size)
         place.insert(0, last)
     return tuple(place)
+
+
+def others(size):
+    return sorted(range(1, size), key=lambda by: min(by, size - by))
 
 
 def moved(sizes, at, axis, by):
@@ -156,7 +160,7 @@
     def copies(self, item, order, step, arriving):
         axis, free = order[step], order[:step]
         made = []
-        for by in range(1, self.sizes[axis]):
+        for by in others(self.sizes[axis]):
             source = moved(self.sizes, self.at, axis, -by) if arriving else self.at
             place = self.wholes[item].at(blocks_of(free, source))
             made.append(
@@ -281,7 +285,7 @@
             def act(order, now=now, more=more):
                 self.add(item, order, now)
                 if more:
-                    for by in range(1, self.sizes[order[now - 1]]):
+                    for by in others(self.sizes[order[now - 1]]):
                         self.copy(item, order, now - 1, by).start()
 
             by_order(self.sizes, self.at, act, item in self.late)

time: 276 us -> 272 us (0.986)
  Pallas kernels: 275 us -> 271 us
    pallas_call x2, Pallas kernels: 271 us -> 266 us  [kernel_call(): pl.pallas_call(functools.partial(body, sizes, names), out_shape=[jax.Shap...]
where the time goes in v6:
time: 272 us
  Pallas kernels  271 us (100%)
    pallas_call x2, Pallas kernels, kernel_call(): pl.pallas_call(functools.partial(body, sizes, names), out_shape=[jax.Shap...  266 us

profile of v6, /device:TPU:0, one launch (start us, length us, event | category | flops | bytes accessed | tf_op | source)
XLA Modules:
  0.0 271.9 jit_solution(8563487022652236170)
XLA Ops:
  0.7 152.9 %shard_map.279 = (bf16[4,2,2,2,32,128]{5,4,3,2,1,0:T(8,128)(2,1)}, bf16[4,2,2,2,32,512]{5,4,3,2,1,0:T(8,128)(2,1)}, bf16[4,2,2,2,32,512]{5,4,3,2,1,0:T(8,128)(2,...) custom-call(bf16[256,1024]{1,0:T(8,128)(2,1)} %bitcast.14, ...), custom_call_target="tpu_custom_call" | custom-call | tf_op jit(solution)/shard_map/pallas_call | solution.py:919
  153.5 113.6 %shard_map.280 = (f32[88,1024]{1,0:T(8,128)}, f32[32,2816]{1,0:T(8,128)}, f32[32,2816]{1,0:T(8,128)}, f32[32,1024]{1,0:T(8,128)}, f32[32,1024]{1,0:T(8,128)}, /*...) custom-call(bf16[256,512]{1,0:T(8,128)(2,1)} %get-tuple-element.70.r, ...), custom_call_target="tpu_custom_call" | custom-call | tf_op jit(solution)/shard_map/pallas_call | solution.py:919
  267.1 4.6 %shard_map.281 = (f32[256,1024]{1,0:T(8,128)}, f32[256,1024]{1,0:T(8,128)}, f32[32,512]{1,0:T(8,128)}, f32[32,512]{1,0:T(8,128)}, f32[32,1024]{1,0:T(8,128)}, /*...) custom-call(f32[256,1024]{1,0:T(8,128)} %get-tuple-element.69.refs_0, ...), custom_call_target="tpu_custom_call" | custom-call | tf_op jit(solution)/shard_map/pallas_call | solution.py:1429
